TPU v7x, 8 devices: a whole 2x2x1 slice. The times are simulated.
8 devices in a mesh: data: 4 (over z, y, x), model: 2 (over core).
Axes of the slice: x: 2, y: 2, z: 1, core: 2. Of those that a mesh axis runs over, the one named last changes fastest.
Arguments:
- teacher_in: bfloat16 [8, 1024, 4096], P('data', 'model')
- student_in: bfloat16 [8, 1024, 2048], P(('data', 'model'))
- teacher_gain: float32 [3, 4096], replicated
- teacher_up: bfloat16 [3, 4096, 16384], P(None, None, 'model')
- teacher_down: bfloat16 [3, 16384, 4096], P(None, 'model')
- student_gain: float32 [1, 2048], replicated
- student_up: bfloat16 [1, 2048, 8192], replicated
- student_down: bfloat16 [1, 8192, 2048], replicated
- student_proj: bfloat16 [1, 4096, 2048], replicated
Outputs:
- output 1: float32 [], replicated
- output 2: float32 [1, 2048, 8192], replicated
- output 3: float32 [1, 8192, 2048], replicated
- output 4: float32 [1, 2048], replicated
- output 5: float32 [1, 4096, 2048], replicated
All inputs are finite; a program needn't handle non-finite values.
Results may differ from a plain program's by a relative error of at most 0.0137251.
Values are sent between devices in bfloat16 or wider.
A program may use at most 2.5 GiB of HBM per device.

v0:
```python
import jax
import jax.numpy as jnp
from jax import lax
from jax.sharding import PartitionSpec as P

EPS = 1e-6


def rms_unit(values):
    return values * lax.rsqrt(jnp.mean(values * values, axis=-1, keepdims=True) + EPS)


def rms_back(values, grad_out):
    inv_rms = lax.rsqrt(jnp.mean(values * values, axis=-1, keepdims=True) + EPS)
    unit = values * inv_rms
    return inv_rms * (grad_out - unit * jnp.mean(grad_out * unit, axis=-1, keepdims=True))


def gelu_back(pre_act, grad_out):
    return jax.vjp(jax.nn.gelu, pre_act)[1](grad_out)[0]


def student_pass(student_in, targets, student_gain, student_up, student_down, grad_scale):
    n_feats = len(targets)
    state = student_in
    saved = []
    errors = []
    for feat_idx in range(n_feats):
        normed = rms_unit(state.astype(jnp.float32))
        act_in = (normed * student_gain[feat_idx]).astype(jnp.bfloat16)
        pre_act = jnp.einsum("bsd,df->bsf", act_in, student_up[feat_idx], preferred_element_type=jnp.float32)
        up_act = jax.nn.gelu(pre_act).astype(jnp.bfloat16)
        down_out = jnp.einsum("bsf,fd->bsd", up_act, student_down[feat_idx], preferred_element_type=jnp.float32)
        new_state = (state.astype(jnp.float32) + down_out).astype(jnp.bfloat16)
        errors.append(targets[feat_idx].astype(jnp.float32) - rms_unit(new_state.astype(jnp.float32)))
        saved.append((state, normed, act_in, pre_act, up_act, new_state))
        state = new_state
    loss_sum = sum(jnp.sum(error * error) for error in errors)
    d_res = jnp.zeros(student_in.shape, jnp.float32)
    grads_up = []
    grads_down = []
    grads_gain = []
    for feat_idx in reversed(range(n_feats)):
        state, normed, act_in, pre_act, up_act, new_state = saved[feat_idx]
        d_res = d_res + rms_back(new_state.astype(jnp.float32), -grad_scale * errors[feat_idx])
        d_out = d_res.astype(jnp.bfloat16)
        grads_down.append(jnp.einsum("bsf,bsd->fd", up_act, d_out, preferred_element_type=jnp.float32))
        d_up = jnp.einsum("bsd,fd->bsf", d_out, student_down[feat_idx], preferred_element_type=jnp.float32)
        d_pre = gelu_back(pre_act, d_up).astype(jnp.bfloat16)
        grads_up.append(jnp.einsum("bsd,bsf->df", act_in, d_pre, preferred_element_type=jnp.float32))
        d_act = jnp.einsum("bsf,df->bsd", d_pre, student_up[feat_idx], preferred_element_type=jnp.float32)
        grads_gain.append(jnp.sum(d_act * normed, axis=(0, 1)))
        if feat_idx > 0:
            d_res = d_res + rms_back(state.astype(jnp.float32), d_act * student_gain[feat_idx])
    return loss_sum, errors, jnp.stack(grads_up[::-1]), jnp.stack(grads_down[::-1]), jnp.stack(grads_gain[::-1])


def solution(mesh):
    dev_count = mesh.shape["data"] * mesh.shape["model"]
    all_axes = ("data", "model")

    def body(teacher_in, student_in, teacher_gain, teacher_up, teacher_down, student_gain, student_up, student_down, student_proj):
        n_feats = student_proj.shape[0]
        n_layers = teacher_up.shape[0]
        t_step = n_layers // n_feats
        seq_rows, seq_len, s_width = student_in.shape
        total = n_feats * seq_rows * dev_count * seq_len * s_width
        grad_scale = 2.0 / total
        hidden = teacher_in
        features = []
        targets = []
        for layer in range(n_layers):
            act_in = (rms_unit(hidden.astype(jnp.float32)) * teacher_gain[layer]).astype(jnp.bfloat16)
            act_full = lax.all_gather(act_in, "model", axis=1, tiled=True)
            pre_act = jnp.einsum("bsd,df->bsf", act_full, teacher_up[layer], preferred_element_type=jnp.float32)
            up_act = jax.nn.gelu(pre_act).astype(jnp.bfloat16)
            part_out = jnp.einsum("bsf,fd->bsd", up_act, teacher_down[layer], preferred_element_type=jnp.float32).astype(jnp.bfloat16)
            delta = lax.psum_scatter(part_out, "model", scatter_dimension=1, tiled=True)
            hidden = (hidden.astype(jnp.float32) + delta.astype(jnp.float32)).astype(jnp.bfloat16)
            if (layer + 1) % t_step == 0:
                local_target = jnp.einsum("bsd,de->bse", hidden, student_proj[layer // t_step], preferred_element_type=jnp.float32).astype(jnp.bfloat16)
                targets.append(lax.all_to_all(local_target, "model", 0, 1, tiled=True))
                features.append(hidden)
        loss_sum, errors, grad_up, grad_down, grad_gain = student_pass(student_in, targets, student_gain, student_up, student_down, grad_scale)
        proj_list = []
        for feat_idx in range(n_feats):
            error_back = lax.all_to_all(errors[feat_idx].astype(jnp.bfloat16), "model", 1, 0, tiled=True)
            proj_list.append(grad_scale * jnp.einsum("bsd,bse->de", features[feat_idx], error_back, preferred_element_type=jnp.float32))
        totals = lax.psum((loss_sum, grad_up, grad_down, grad_gain, jnp.stack(proj_list)), all_axes)
        return (totals[0] / total, totals[1], totals[2], totals[3], totals[4])

    return jax.shard_map(
        body,
        mesh=mesh,
        in_specs=(
            P("data", "model", None),
            P(("data", "model"), None, None),
            P(),
            P(None, None, "model"),
            P(None, "model", None),
            P(),
            P(),
            P(),
            P(),
        ),
        out_specs=(P(), P(), P(), P(), P()),
        check_vma=False,
    )
```

profile of v0, /device:TPU:1, one launch (start us, length us, event | category | flops | bytes accessed | tf_op | source)
XLA Modules:
  0.0 3379.5 jit_solution(17596311033367210513)
XLA Ops:
  24.7 29.9 all-gather.4.cloned.1.call-done
  54.6 149.0 %fusion.34 = f32[2,1024,8192]{2,1,0:T(8,128)} fusion(bf16[2,1024,4096]{2,1,0:T(8,128)(2,1)} %all-gather.4.cloned.1.call-done, bf16[3,4096,8192]{2,1,0:T(8,128)(2,1)} %param.12), kind=kOutput, calls=%fused_computation.37 | convolution fusion | flops 137438953472 | bytes 150994944 | tf_op jit(solution)/shard_map/bsd,df->bsf/dot_general | solution.py:75
  203.6 33.5 fusion.181
  237.1 153.1 %fusion.89 = bf16[2,1024,4096]{2,1,0:T(8,128)(2,1)} fusion(bf16[3,8192,4096]{2,1,0:T(8,128)(2,1)} %param.13, bf16[2,1024,8192]{2,1,0:T(8,128)(2,1)} %fusion.181), kind=kOutput, calls=%fused_computation.105 | convolution fusion | flops 137447342080 | bytes 117440512 | tf_op jit(solution)/shard_map/bsf,fd->bsd/dot_general | solution.py:77
  432.7 29.1 all-gather.6.cloned.1.call-done
  461.8 149.0 %fusion.30 = f32[2,1024,8192]{2,1,0:T(8,128)} fusion(bf16[2,1024,4096]{2,1,0:T(8,128)(2,1)} %all-gather.6.cloned.1.call-done, bf16[3,4096,8192]{2,1,0:T(8,128)(2,1)} %param.12), kind=kOutput, calls=%fused_computation.33 | convolution fusion | flops 137438953472 | bytes 150994944 | tf_op jit(solution)/shard_map/bsd,df->bsf/dot_general | solution.py:75
  610.7 33.5 fusion.183
  644.2 153.2 %fusion.94 = bf16[2,1024,4096]{2,1,0:T(8,128)(2,1)} fusion(bf16[3,8192,4096]{2,1,0:T(8,128)(2,1)} %param.13, bf16[2,1024,8192]{2,1,0:T(8,128)(2,1)} %fusion.183), kind=kOutput, calls=%fused_computation.106 | convolution fusion | flops 137447342080 | bytes 117440512 | tf_op jit(solution)/shard_map/bsf,fd->bsd/dot_general | solution.py:77
  844.1 29.1 all-gather.8.cloned.1.call-done
  873.1 149.0 %fusion.26 = f32[2,1024,8192]{2,1,0:T(8,128)} fusion(bf16[2,1024,4096]{2,1,0:T(8,128)(2,1)} %all-gather.8.cloned.1.call-done, bf16[3,4096,8192]{2,1,0:T(8,128)(2,1)} %param.12), kind=kOutput, calls=%fused_computation.29 | convolution fusion | flops 137438953472 | bytes 150994944 | tf_op jit(solution)/shard_map/bsd,df->bsf/dot_general | solution.py:75
  1022.1 33.5 fusion.185
  1055.6 153.2 %fusion.99 = bf16[2,1024,4096]{2,1,0:T(8,128)(2,1)} fusion(bf16[3,8192,4096]{2,1,0:T(8,128)(2,1)} %param.13, bf16[2,1024,8192]{2,1,0:T(8,128)(2,1)} %fusion.185), kind=kOutput, calls=%fused_computation.107 | convolution fusion | flops 137447342080 | bytes 117440512 | tf_op jit(solution)/shard_map/bsf,fd->bsd/dot_general | solution.py:77
  1213.0 42.1 %fusion.59 = f32[1024,8192]{1,0:T(8,128)} fusion(bf16[1,2048,8192]{2,1,0:T(8,128)(2,1)} %param.15, bf16[1,1024,2048]{2,1,0:T(8,128)(2,1)} %param.10, f32[2048]{0:T(1024)S(1)} %bitcast.131, f32[1024]{0:T(1024)S(1)} %add_rsqrt_fusion.1), kind=kOutput, calls=%fused_computation.64 | convolution fusion | flops 34368126976 | bytes 71315456 | tf_op jit(solution)/shard_map/bsd,df->bsf/dot_general | solution.py:31
  1255.0 45.9 %fusion.115 = (f32[1024]{0:T(1024)S(1)}, bf16[1,1024,2048]{2,1,0:T(8,128)(2,1)}) fusion(bf16[1,8192,2048]{2,1,0:T(8,128)(2,1)} %param.16, f32[1024,8192]{1,0:T(8,128)} %fusion.59, bf16[1,1024,2048]{2,1,0:T(8,128)(2,1)S(1)} %copy-done.1), kind=kOutput, calls=%fused_computation.121 | convolution fusion | flops 34447818752 | bytes 75501568 | tf_op jit(solution)/shard_map/bsf,fd->bsd/dot_general | solution.py:33
  1343.2 51.8 %convolution_bitcast_fusion = f32[1,8192,2048]{2,1,0:T(8,128)} fusion(bf16[1024,2048]{1,0:T(8,128)(2,1)} %fusion.123, f32[1024,8192]{1,0:T(8,128)} %fusion.59), kind=kOutput, calls=%fused_computation.47 | convolution fusion | flops 34435235840 | bytes 104857600 | tf_op jit(solution)/shard_map/bsf,bsd->fd/dot_general | solution.py:47
  1404.5 26.7 reduce.3
  1464.3 29.2 fusion.52
  1493.5 62.7 %fusion.48 = bf16[1024,8192]{1,0:T(8,128)(2,1)} fusion(f32[1024,8192]{1,0:T(8,128)} %fusion.59, bf16[1024,2048]{1,0:T(8,128)(2,1)} %fusion.123, bf16[1,8192,2048]{2,1,0:T(8,128)(2,1)} %param.16), kind=kOutput, calls=%fused_computation.55 | convolution fusion | flops 34527510528 | bytes 88080384 | tf_op jit(solution)/shard_map/bsd,fd->bsf/dot_general | solution.py:48
  1556.2 46.5 %convolution_bitcast_fusion.1 = f32[1,2048,8192]{2,1,0:T(8,128)} fusion(bf16[1024,8192]{1,0:T(8,128)(2,1)} %fusion.48, bf16[1,1024,2048]{2,1,0:T(8,128)(2,1)} %param.10, f32[2048]{0:T(1024)S(1)} %bitcast.132, f32[1024]{0:T(1024)S(1)} %copy-done.5), kind=kOutput, calls=%fused_computation.48 | convolution fusion | flops 34368126976 | bytes 88092672 | tf_op jit(solution)/shard_map/bsd,bsf->df/dot_general | solution.py:50
  1602.7 44.2 %fusion.110 = f32[2048]{0:T(1024)S(1)} fusion(bf16[1,1024,2048]{2,1,0:T(8,128)(2,1)} %param.10, bf16[1024,8192]{1,0:T(8,128)(2,1)} %fusion.48, bf16[1,2048,8192]{2,1,0:T(8,128)(2,1)} %param.15, f32[1024]{0:T(1024)S(1)} %copy-done.5), kind=kOutput, calls=%fused_computation.116 | convolution fusion | flops 34368126976 | bytes 54538240 | tf_op jit(solution)/shard_map/bsf,df->bsd/dot_general | solution.py:51
  1672.1 472.1 %all-reduce.5.cloned.1.call-done = f32[1,8192,2048]{2,1,0:T(8,128)} async-done(((f32[1,8192,2048]{2,1,0:T(8,128)}), f32[1,8192,2048]{2,1,0:T(8,128)}) %all-reduce.5.cloned.1.call-update) | async-done | bytes 67108880 | tf_op jit(solution)/shard_map/psum | solution.py:89
  2144.2 1116.4 %all-reduce.7.cloned.1.call-done = (f32[1,2048,8192]{2,1,0:T(8,128)}, f32[1,4096,2048]{2,1,0:T(8,128)}) async-done(((f32[1,2048,8192]{2,1,0:T(8,128)}, f32[1,4096,2048]{2,1,0:T(8,128)}), (f32[1,2048,8192]{2,1,0:T(8,128)}, f32[1,4096,2048]{2,1,0:T(8,128)})) %all-reduce.7.cloned.1.call-update) | async-done | bytes 100663312 | tf_op jit(solution)/shard_map/psum | solution.py:89
  3260.6 43.9 %copy.26 = f32[1,2048,8192]{2,1,0:T(8,128)} copy(f32[1,2048,8192]{2,1,0:T(8,128)} %get-tuple-element.20) | data formatting | bytes 134217728
  3304.5 43.6 %copy.27 = f32[1,8192,2048]{2,1,0:T(8,128)} copy(f32[1,8192,2048]{2,1,0:T(8,128)} %all-reduce.5.cloned.1.call-done) | data formatting | bytes 134217728
  (61 shorter events, 243.0 us)
Async XLA Ops:
  7.2 47.4 %all-gather.4.cloned.1.call-start = ((), (), s32[]{:S(2)}) async-start(), calls=%async_computation.5 | async-start | bytes 25165824 | tf_op jit(solution)/shard_map/all_gather | solution.py:74
  24.4 388.9 %reduce-scatter.4.cloned.1.call-start = ((), (), s32[]{:S(2)}) async-start(), calls=%async_computation.6 | async-start | bytes 25165824 | tf_op jit(solution)/shard_map/reduce_scatter | solution.py:78
  390.2 31.7 copy-start.2
  390.2 71.5 %all-gather.6.cloned.1.call-start = ((), (), s32[]{:S(2)}) async-start(), calls=%async_computation.7 | async-start | bytes 25165824 | tf_op jit(solution)/shard_map/all_gather | solution.py:74
  432.6 387.9 %reduce-scatter.6.cloned.1.call-start = ((), (), s32[]{:S(2)}) async-start(), calls=%async_computation.8 | async-start | bytes 25165824 | tf_op jit(solution)/shard_map/reduce_scatter | solution.py:78
  797.5 36.0 %copy-start.3 = (f32[1,4096]{1,0:T(1,128)S(1)}, f32[1,4096]{1,0:T(1,128)}, u32[]{:S(2)}) copy-start(f32[1,4096]{1,0:T(1,128)} %get-tuple-element.14) | copy-start | bytes 49156
  797.5 75.7 %all-gather.8.cloned.1.call-start = ((), (), s32[]{:S(2)}) async-start(), calls=%async_computation.9 | async-start | bytes 25165824 | tf_op jit(solution)/shard_map/all_gather | solution.py:74
  844.0 457.0 %reduce-scatter.8.cloned.1.call-start = ((), (), s32[]{:S(2)}) async-start(), calls=%async_computation.10 | async-start | bytes 25165824 | tf_op jit(solution)/shard_map/reduce_scatter | solution.py:78
  1208.8 4.2 copy-start.6
  1208.8 935.4 %all-reduce.5.cloned.1.call-start = ((), (), s32[]{:S(2)}) async-start(), calls=%async_computation.11 | async-start | bytes 134217728 | tf_op jit(solution)/shard_map/psum | solution.py:89
  1212.4 0.6 copy-start.4
  1213.0 42.1 %copy-start.1 = (bf16[1,1024,2048]{2,1,0:T(8,128)(2,1)S(1)}, bf16[1,1024,2048]{2,1,0:T(8,128)(2,1)}, u32[]{:S(2)}) copy-start(bf16[1,1024,2048]{2,1,0:T(8,128)(2,1)} %param.10) | copy-start | bytes 12582916
  1301.0 32.5 copy-start
  1395.1 1865.5 %all-reduce.7.cloned.1.call-start = ((), (), s32[]{:S(2)}) async-start(), calls=%async_computation.12 | async-start | bytes 201326592 | tf_op jit(solution)/shard_map/psum | solution.py:89
  1493.5 62.7 %copy-start.5 = (f32[1024]{0:T(1024)S(1)}, f32[1024]{0:T(1024)}, u32[]{:S(2)}) copy-start(f32[1024]{0:T(1024)} %copy-done.4) | copy-start | bytes 12292
  1493.5 62.7 %copy-start.7 = (f32[1,2048]{1,0:T(1,128)S(1)}, f32[1,2048]{1,0:T(1,128)}, u32[]{:S(2)}) copy-start(f32[1,2048]{1,0:T(1,128)} %param.14) | copy-start | bytes 24580
Sparse Core Ops, SparseCore 0:
  24.6 29.9 all-gather.3
  390.4 22.9 reduce-scatter.3
  432.7 28.9 all-gather.5
  797.6 22.9 reduce-scatter.5
  844.1 28.9 all-gather.7
  1209.0 22.9 reduce-scatter.7
  1395.2 748.9 all-reduce.4
  2148.9 1111.6 all-reduce.6
where the time goes:
time: 3380 us
  waiting for transfers between devices  1720 us (51%)
  matrix products  1250 us (37%)
  other arithmetic  198 us (6%)
  local copies, waits for them, and re-layouts  143 us (4%)
  blocking collectives  43.8 us (1%)
    psum x2, waiting for transfers between devices, body(): lax.psum((loss_sum, grad_up, grad_down, grad_gain, jnp.stack(proj_list)),...  1590 us
    dot_general x3, matrix products, body(): jnp.einsum('bsf,fd->bsd', up_act, teacher_down[layer], preferred_element_...  459 us
    dot_general x3, matrix products, body(): jnp.einsum('bsd,df->bsf', act_full, teacher_up[layer], preferred_element_...  447 us
    unnamed x23, local copies, waits for them, and re-layouts  133 us
    dot_general x3, other arithmetic, body(): jnp.einsum('bsf,fd->bsd', up_act, teacher_down[layer], preferred_element_...  101 us
    all_gather x3, waiting for transfers between devices, body(): act_full = lax.all_gather(act_in, 'model', axis=1, tiled=True)  88.1 us
  transfers between devices with their start and end apart: 8, of which 7 were waited for; matrix products, arithmetic and copies ran while one was open for 10% of the time, Pallas kernels for 0%

commit v1 on v0

v1 whole, which is shorter than its diff:
```python
import functools

import jax
import jax.numpy as jnp
from jax import lax
from jax.experimental import pallas as pl
from jax.experimental.pallas import tpu as pltpu
from jax.sharding import PartitionSpec as P


EPS = 1e-6
VMEM_CAP = 64 * 1024 * 1024 - 65536
AXES = ("data", "model")


def after(values, dep):
    return lax.optimization_barrier((values, dep))[0]


def rms_unit(values):
    return values * lax.rsqrt(jnp.mean(values * values, axis=-1, keepdims=True) + EPS)


def up_kernel(sub, a_ref, w_ref, u_ref):
    for j in range(u_ref.shape[1] // sub):
        cols = slice(j * sub, (j + 1) * sub)
        acc = jnp.dot(a_ref[...], w_ref[:, cols], preferred_element_type=jnp.float32)
        u_ref[:, cols] = jax.nn.gelu(acc).astype(jnp.bfloat16)


def teacher_up(act, weights, layer, tn=1024, sub=256):
    rows, depth = act.shape
    cols = weights.shape[2]
    return pl.pallas_call(
        functools.partial(up_kernel, sub),
        grid=(cols // tn,),
        in_specs=[
            pl.BlockSpec((rows, depth), lambda j: (0, 0)),
            pl.BlockSpec((None, depth, tn), lambda j: (layer, 0, j)),
        ],
        out_specs=pl.BlockSpec((rows, tn), lambda j: (0, j)),
        out_shape=jax.ShapeDtypeStruct((rows, cols), jnp.bfloat16),
        compiler_params=pltpu.CompilerParams(vmem_limit_bytes=VMEM_CAP),
        cost_estimate=pl.CostEstimate(
            flops=2 * rows * depth * cols,
            bytes_accessed=2 * (rows * depth + depth * cols + rows * cols),
            transcendentals=rows * cols,
        ),
        name="teacher_up",
    )(act, weights)


def norm_kernel(h_ref, g_ref, a_ref):
    state = h_ref[...].astype(jnp.float32)
    inv = lax.rsqrt(jnp.mean(state * state, axis=-1, keepdims=True) + EPS)
    a_ref[...] = (state * inv * g_ref[...]).astype(jnp.bfloat16)


def step_kernel(h_ref, y_ref, g_ref, o_ref, a_ref):
    state = (h_ref[...].astype(jnp.float32) + y_ref[...].astype(jnp.float32)).astype(jnp.bfloat16)
    o_ref[...] = state
    state = state.astype(jnp.float32)
    inv = lax.rsqrt(jnp.mean(state * state, axis=-1, keepdims=True) + EPS)
    a_ref[...] = (state * inv * g_ref[...]).astype(jnp.bfloat16)


def teacher_norm(hidden, delta, gains, layer, block=128):
    rows, width = hidden.shape
    spec = pl.BlockSpec((block, width), lambda i: (i, 0))
    gain_spec = pl.BlockSpec((1, width), lambda i: (0, 0))
    shape = jax.ShapeDtypeStruct((rows, width), jnp.bfloat16)
    count = rows * width
    common = dict(
        grid=(rows // block,),
        compiler_params=pltpu.CompilerParams(vmem_limit_bytes=48 * 1024 * 1024),
    )
    gain = gains[layer : layer + 1]
    if delta is None:
        cost = pl.CostEstimate(flops=8 * count, bytes_accessed=4 * count, transcendentals=0)
        return hidden, pl.pallas_call(norm_kernel, in_specs=[spec, gain_spec], out_specs=spec, out_shape=shape, cost_estimate=cost, name="norm", **common)(hidden, gain)
    cost = pl.CostEstimate(flops=10 * count, bytes_accessed=8 * count, transcendentals=0)
    return pl.pallas_call(step_kernel, in_specs=[spec, spec, gain_spec], out_specs=[spec, spec], out_shape=[shape, shape], cost_estimate=cost, name="step", **common)(hidden, delta, gain)


def error_kernel(grad_scale, z_ref, s_ref, e_ref, d_ref, sq_ref):
    @pl.when((pl.program_id(0) == 0) & (pl.program_id(1) == 0))
    def _():
        sq_ref[...] = jnp.zeros_like(sq_ref)

    state = s_ref[...].astype(jnp.float32)
    inv = lax.rsqrt(jnp.mean(state * state, axis=-1, keepdims=True) + EPS)
    unit = state * inv
    error = z_ref[...].astype(jnp.float32) - unit
    lean = jnp.mean(error * unit, axis=-1, keepdims=True)
    e_ref[...] = error.astype(jnp.bfloat16)
    d_ref[...] = ((error - unit * lean) * (-grad_scale * inv)).astype(jnp.bfloat16)
    rows, width = error.shape
    sq_ref[...] += jnp.sum((error * error).reshape(rows // 8, 8, width), axis=0)


def errors_of(targets, states, parity, grad_scale, block=256):
    n_seq, seq_len, width = states.shape
    half = n_seq // 2
    spec = pl.BlockSpec((None, block, width), lambda i, j: (i, j, 0))
    shape = jax.ShapeDtypeStruct((half, seq_len, width), jnp.bfloat16)
    count = half * seq_len * width
    return pl.pallas_call(
        functools.partial(error_kernel, grad_scale),
        grid=(half, seq_len // block),
        in_specs=[spec, pl.BlockSpec((None, block, width), lambda i, j: (2 * i + parity, j, 0))],
        out_specs=[spec, spec, pl.BlockSpec((8, width), lambda i, j: (0, 0))],
        out_shape=[shape, shape, jax.ShapeDtypeStruct((8, width), jnp.float32)],
        compiler_params=pltpu.CompilerParams(vmem_limit_bytes=48 * 1024 * 1024),
        cost_estimate=pl.CostEstimate(flops=16 * count, bytes_accessed=8 * count, transcendentals=0),
        name="errors",
    )(targets.reshape(half, seq_len, width), states)


def act_kernel(s_ref, g_ref, a_ref):
    state = s_ref[...].astype(jnp.float32)
    inv = lax.rsqrt(jnp.mean(state * state, axis=-1, keepdims=True) + EPS)
    a_ref[...] = (state * inv * g_ref[...]).astype(jnp.bfloat16)


def acts_of(states, gain, parity, block=256):
    n_seq, seq_len, width = states.shape
    half = n_seq // 2
    count = half * seq_len * width
    return pl.pallas_call(
        act_kernel,
        grid=(half, seq_len // block),
        in_specs=[
            pl.BlockSpec((None, block, width), lambda i, j: (2 * i + parity, j, 0)),
            pl.BlockSpec((1, width), lambda i, j: (0, 0)),
        ],
        out_specs=pl.BlockSpec((None, block, width), lambda i, j: (i, j, 0)),
        out_shape=jax.ShapeDtypeStruct((half, seq_len, width), jnp.bfloat16),
        compiler_params=pltpu.CompilerParams(vmem_limit_bytes=48 * 1024 * 1024),
        cost_estimate=pl.CostEstimate(flops=8 * count, bytes_accessed=4 * count, transcendentals=0),
        name="acts",
    )(states, gain).reshape(half * seq_len, width)


def place_kernel(where_ref, piece_ref, *rest):
    rest[-1][...] = piece_ref[...].astype(jnp.float32)


def place(out, piece, where, shape, block):
    rows, cols = piece.shape
    steps = rows // block
    specs = [pl.BlockSpec((block, cols), lambda i, w: (i, 0))]
    args = [where, piece]
    alias = {}
    if out is not None:
        specs.append(pl.BlockSpec(memory_space=pl.ANY))
        args.append(out)
        alias = {2: 0}
    return pl.pallas_call(
        place_kernel,
        grid_spec=pltpu.PrefetchScalarGridSpec(
            num_scalar_prefetch=1,
            grid=(steps,),
            in_specs=specs,
            out_specs=pl.BlockSpec((block, cols), lambda i, w: (w[0] * steps + i, w[1])),
        ),
        out_shape=jax.ShapeDtypeStruct(shape, jnp.float32),
        input_output_aliases=alias,
        compiler_params=pltpu.CompilerParams(vmem_limit_bytes=32 * 1024 * 1024),
        cost_estimate=pl.CostEstimate(flops=rows * cols, bytes_accessed=6 * rows * cols, transcendentals=0),
        name="place",
    )(*args)


def flip(value, bits, size):
    return lax.ppermute(value, AXES, [(i, i ^ bits) for i in range(size)])


def share(halves, me, size, shape, by_cols, block):
    first, second = halves
    x_first, y_second = flip(first, 2, size), flip(second, 4, size)
    x_second, y_first = flip(second, 2, size), flip(first, 4, size)
    d_second, d_first = flip(y_second, 2, size), flip(x_first, 4, size)
    have = [(0, 0, first), (0, 1, second), (2, 0, x_first), (4, 1, y_second), (2, 1, x_second), (4, 0, y_first), (6, 1, d_second), (6, 0, d_first)]
    other = [(bits | 1, half, flip(value, 1, size)) for bits, half, value in have]
    out = None
    for pair in zip(have, other):
        for bits, half, value in pair:
            owner = me ^ bits
            where = jnp.stack([jnp.int32(half), owner]) if by_cols else jnp.stack([2 * owner + half, jnp.int32(0)])
            out = place(out, value, where.astype(jnp.int32), shape, block)
    return out


def gelu_back(pre_act, grad_out):
    return jax.vjp(jax.nn.gelu, pre_act)[1](grad_out)[0]


def dot(a, b, dims):
    return lax.dot_general(a, b, (dims, ((), ())), preferred_element_type=jnp.float32)


def solution(mesh):
    size = mesh.shape["data"] * mesh.shape["model"]

    def step(teacher_in, student_in, teacher_gain, teacher_up_w, teacher_down, student_gain, student_up, student_down, student_proj):
        me = lax.axis_index("data") * 2 + lax.axis_index("model")
        n_layers = teacher_up_w.shape[0]
        t_width = teacher_in.shape[2]
        _, seq_len, s_width = student_in.shape
        s_hidden = student_up.shape[2]
        part = s_hidden // size
        t_part = t_width // size
        total = size * seq_len * s_width
        grad_scale = 2.0 / total
        gain = student_gain[0]
        v_up, v_down, q_proj = student_up[0], student_down[0], student_proj[0]

        targets, feats = [], []

        def finish(c):
            hidden[c] = (hidden[c].astype(jnp.float32) + delta[c].astype(jnp.float32)).astype(jnp.bfloat16)
            target = dot(hidden[c], q_proj, ((1,), (0,))).astype(jnp.bfloat16)
            targets.append(lax.all_gather(target, AXES, axis=0, tiled=True))
            return target

        def columns(source):
            rows = source.shape[0]
            feat = jnp.zeros((size * rows, t_part), jnp.bfloat16)
            for bits in range(size):
                other = me ^ bits
                piece = lax.dynamic_slice(source, (0, other * t_part), (rows, t_part))
                if bits:
                    piece = flip(piece, bits, size)
                feat = lax.dynamic_update_slice(feat, piece, (other * rows, 0))
            return feat

        own = student_in[0]
        all_in = lax.all_gather(own, AXES, axis=0, tiled=False)

        hidden = [teacher_in[c] for c in range(2)]
        delta = [None, None]
        for layer in range(n_layers):
            if layer == 1:
                own_act = (rms_unit(own.astype(jnp.float32)) * gain).astype(jnp.bfloat16)
                own_up = jax.nn.gelu(dot(own_act, v_up, ((1,), (0,)))).astype(jnp.bfloat16)
                own_out = (own.astype(jnp.float32) + dot(own_up, v_down, ((1,), (0,)))).astype(jnp.bfloat16)
                delta[1] = after(delta[1], (own_out, all_in))
                all_out = lax.all_gather(own_out, AXES, axis=0, tiled=False)
            if layer == 2:
                delta[1] = after(delta[1], all_out)
            for c in range(2):
                hidden[c], act = teacher_norm(hidden[c], delta[c], teacher_gain, layer)
                act = lax.all_gather(act, "model", axis=0, tiled=True)
                up_act = teacher_up(act, teacher_up_w, layer)
                if layer == n_layers - 1 and c == 1:
                    up_act = after(up_act, finish(0))
                partial = dot(up_act, teacher_down[layer], ((1,), (0,))).astype(jnp.bfloat16)
                delta[c] = lax.psum_scatter(partial, "model", scatter_dimension=0, tiled=True)

        target = finish(1)
        feats.append(columns(hidden[0]))
        feats.append(columns(after(hidden[1], targets[1])))

        all_in, all_out, targets[0] = after((all_in, all_out, targets[0]), target)
        up_part = lax.dynamic_slice(v_up, (0, me * part), (s_width, part))
        down_part = lax.dynamic_slice(v_down, (me * part, 0), (part, s_width))
        acts = [acts_of(all_in, student_gain, c) for c in range(2)]
        pre = [dot(acts[c], up_part, ((1,), (0,))) for c in range(2)]
        ups = [jax.nn.gelu(pre[c]).astype(jnp.bfloat16) for c in range(2)]
        errors, d_outs, squares = [], [], []
        for c in range(2):
            if c == 1:
                targets[1] = after(targets[1], (ups, errors[0]))
            error, d_out, square = errors_of(targets[c], all_out, c, grad_scale)
            errors.append(error.reshape(-1, s_width))
            d_outs.append(d_out.reshape(-1, s_width))
            squares.append(square)
        loss = (jnp.sum(squares[0]) + jnp.sum(squares[1])) / total

        def both(make):
            return (make(0) + make(1)).astype(jnp.bfloat16)

        halves_down = [both(lambda c: dot(ups[c][:, h * part // 2 : (h + 1) * part // 2], d_outs[c], ((0,), (0,)))) for h in range(2)]
        grad_down = share(halves_down, me, size, (s_hidden, s_width), False, 256)

        d_outs = after(d_outs, halves_down)
        d_pres = [gelu_back(pre[c], dot(d_outs[c], down_part, ((1,), (1,)))).astype(jnp.bfloat16) for c in range(2)]
        halves_up = [both(lambda c: dot(acts[c][:, h * s_width // 2 : (h + 1) * s_width // 2], d_pres[c], ((0,), (0,)))) for h in range(2)]
        grad_up = share(halves_up, me, size, (s_width, s_hidden), True, 512)

        errors = after(errors, halves_up)
        halves_proj = []
        for h in range(2):
            cols = slice(h * t_part // 2, (h + 1) * t_part // 2)
            halves_proj.append((grad_scale * (dot(feats[0][:, cols], errors[0], ((0,), (0,))) + dot(feats[1][:, cols], errors[1], ((0,), (0,))))).astype(jnp.bfloat16))
        grad_proj = share(halves_proj, me, size, (t_width, s_width), False, 256)

        d_pres = after(d_pres, halves_proj)
        gain_sum = jnp.zeros((s_width,), jnp.float32)
        seqs = all_in.reshape(size // 2, 2, seq_len, s_width)
        for c in range(2):
            d_act = dot(d_pres[c], up_part, ((1,), (1,))).reshape(size // 2, seq_len, s_width)
            gain_sum = gain_sum + jnp.sum(d_act * rms_unit(seqs[:, c].astype(jnp.float32)), axis=(0, 1))
        grad_gain = lax.psum(gain_sum, AXES)
        return (loss, grad_up[None], grad_down[None], grad_gain[None], grad_proj[None])

    return jax.shard_map(
        step,
        mesh=mesh,
        in_specs=(
            P("data", "model", None),
            P(("data", "model"), None, None),
            P(),
            P(None, None, "model"),
            P(None, "model", None),
            P(),
            P(),
            P(),
            P(),
        ),
        out_specs=(P(), P(), P(), P(), P()),
        check_vma=False,
    )
```

time: 3380 us -> 2320 us (0.69)
  waiting for transfers between devices: 1720 us -> 403 us
  Pallas kernels: 0 us -> 799 us
  matrix products: 1250 us -> 924 us
  other arithmetic: 198 us -> 31.1 us
  local copies, waits for them, and re-layouts: 143 us -> 55.7 us
  starting transfers between devices: 1.5 us -> 53.4 us
    psum x2 -> x0, waiting for transfers between devices: 1590 us -> none  [body(): lax.psum((loss_sum, grad_up, grad_down, grad_gain, jnp.stack(proj_list)),...]
    pallas_call x0 -> x64, Pallas kernels: none -> 799 us  [the longest x6 507 us: teacher_up(): pl.pallas_call(functools.partial(up_kernel, sub), grid=(cols // tn,), in_...]
    ppermute x0 -> x56, waiting for transfers between devices: none -> 352 us  [flip(): return lax.ppermute(value, AXES, [(i, i ^ bits) for i in range(size)])]
    dot_general x14 -> x28, matrix products: 1250 us -> 924 us  [dot(): lax.dot_general(a, b, (dims, ((), ())), preferred_element_type=jnp.float32)]
    dot_general x3 -> x0, other arithmetic: 101 us -> none  [body(): jnp.einsum('bsf,fd->bsd', up_act, teacher_down[layer], preferred_element_...]
    unnamed x23 -> x142, local copies, waits for them, and re-layouts: 133 us -> 33.7 us
    all_gather x3 -> x10, waiting for transfers between devices: 88.1 us -> 30.1 us  [the longest x6 20.9 us: step(): act = lax.all_gather(act, 'model', axis=0, tiled=True)]
    ppermute x0 -> x56, starting transfers between devices: none -> 51.7 us  [flip(): return lax.ppermute(value, AXES, [(i, i ^ bits) for i in range(size)])]
  transfers between devices with their start and end apart: 8 -> 72, of which waited for: 7 -> 27; matrix products, arithmetic and copies ran while one was open for 10% -> 32% of each run, Pallas kernels for 0% -> 29%
where the time goes in v1:
time: 2320 us; the launch traced here: 2310 us
  matrix products  924 us (40%)
  Pallas kernels  799 us (34%)
  waiting for transfers between devices  403 us (17%)
  local copies, waits for them, and re-layouts  55.7 us (2%)
  starting transfers between devices  53.4 us (2%)
  other arithmetic  31.1 us (1%)
    dot_general x28, matrix products, dot(): lax.dot_general(a, b, (dims, ((), ())), preferred_element_type=jnp.float32)  924 us
    pallas_call x6, Pallas kernels, teacher_up(): pl.pallas_call(functools.partial(up_kernel, sub), grid=(cols // tn,), in_...  507 us
    ppermute x56, waiting for transfers between devices, flip(): return lax.ppermute(value, AXES, [(i, i ^ bits) for i in range(size)])  352 us
    pallas_call x48, Pallas kernels, place(): pl.pallas_call(place_kernel, grid_spec=pltpu.PrefetchScalarGridSpec(num_s...  153 us
    pallas_call x2, Pallas kernels, errors_of(): pl.pallas_call(functools.partial(error_kernel, grad_scale), grid=(half, s...  61.2 us
    ppermute x56, starting transfers between devices, flip(): return lax.ppermute(value, AXES, [(i, i ^ bits) for i in range(size)])  51.7 us
  transfers between devices with their start and end apart: 72, of which 27 were waited for; matrix products, arithmetic and copies ran while one was open for 32% of the time, Pallas kernels for 29%

profile of v1, /device:TPU:1, one launch (start us, length us, event | category | flops | bytes accessed | tf_op | source)
XLA Modules:
  0.0 2305.7 jit_solution(11868768262089179480)
XLA Ops:
  40.7 84.1 %teacher_up.6 = bf16[1024,8192]{1,0:T(8,128)(2,1)} custom-call(bf16[1024,4096]{1,0:T(8,128)(2,1)} %all-gather.14.cloned.1.call-done.a_ref, bf16[3,4096,8192]{2,1,0:T(8,128)(2,1)} %w_ref.11), custom_call_target="tpu_custom_call" | custom-call | flops 68719476736 | bytes 92274688 | tf_op jit(solution)/shard_map/teacher_up/pallas_call | solution.py:34
  124.8 79.6 %fusion.76 = bf16[1024,4096]{1,0:T(8,128)(2,1)} fusion(bf16[1024,8192]{1,0:T(8,128)(2,1)} %teacher_up.6, bf16[3,8192,4096]{2,1,0:T(8,128)(2,1)} %param.13), kind=kOutput, calls=%fused_computation.88 | convolution fusion | flops 68723671040 | bytes 92274688 | tf_op jit(solution)/shard_map/dot_general | solution.py:199
  204.6 84.8 %teacher_up.9 = bf16[1024,8192]{1,0:T(8,128)(2,1)} custom-call(bf16[1024,4096]{1,0:T(8,128)(2,1)} %all-gather.22.cloned.1.call-done.a_ref, bf16[3,4096,8192]{2,1,0:T(8,128)(2,1)} %w_ref.11), custom_call_target="tpu_custom_call" | custom-call | flops 68719476736 | bytes 92274688 | tf_op jit(solution)/shard_map/teacher_up/pallas_call | solution.py:34
  299.4 81.8 %fusion.79 = bf16[1024,4096]{1,0:T(8,128)(2,1)} fusion(bf16[1024,8192]{1,0:T(8,128)(2,1)} %teacher_up.9, bf16[3,8192,4096]{2,1,0:T(8,128)(2,1)} %param.13), kind=kOutput, calls=%fused_computation.89 | convolution fusion | flops 68723671040 | bytes 92274688 | tf_op jit(solution)/shard_map/dot_general | solution.py:199
  382.0 85.0 %teacher_up.7 = bf16[1024,8192]{1,0:T(8,128)(2,1)} custom-call(bf16[1024,4096]{1,0:T(8,128)(2,1)} %all-gather.16.cloned.1.call-done.a_ref, bf16[3,4096,8192]{2,1,0:T(8,128)(2,1)} %w_ref.11), custom_call_target="tpu_custom_call" | custom-call | flops 68719476736 | bytes 92274688 | tf_op jit(solution)/shard_map/teacher_up/pallas_call | solution.py:34
  467.0 79.8 %fusion.82 = bf16[1024,4096]{1,0:T(8,128)(2,1)} fusion(bf16[1024,8192]{1,0:T(8,128)(2,1)} %teacher_up.7, bf16[3,8192,4096]{2,1,0:T(8,128)(2,1)} %param.13), kind=kOutput, calls=%fused_computation.90 | convolution fusion | flops 68723671040 | bytes 92274688 | tf_op jit(solution)/shard_map/dot_general | solution.py:199
  550.4 49.3 %fusion.216 = bf16[1024,8192]{1,0:T(8,128)(2,1)} fusion(bf16[1,2048,8192]{2,1,0:T(8,128)(2,1)} %param.15, bf16[1,1024,2048]{2,1,0:T(8,128)(2,1)} %param.10, f32[2048]{0:T(1024)S(1)} %bitcast.196, f32[1024]{0:T(1024)S(1)} %add_rsqrt_fusion.2), kind=kOutput, calls=%fused_computation.36.clone.clone.clone.clone.1 | convolution fusion | flops 34443624448 | bytes 54538240 | tf_op jit(solution)/shard_map/dot_general | solution.py:199
  599.8 44.7 %fusion.61 = bf16[1024,2048]{1,0:T(8,128)(2,1)} fusion(bf16[1,1024,2048]{2,1,0:T(8,128)(2,1)S(1)} %copy-done.55, bf16[1,8192,2048]{2,1,0:T(8,128)(2,1)} %param.16, bf16[1024,8192]{1,0:T(8,128)(2,1)} %fusion.216), kind=kOutput, calls=%fused_computation.75 | convolution fusion | flops 34366029824 | bytes 58720256 | tf_op jit(solution)/shard_map/dot_general | solution.py:199
  671.9 84.4 %teacher_up.10 = bf16[1024,8192]{1,0:T(8,128)(2,1)} custom-call(bf16[1024,4096]{1,0:T(8,128)(2,1)} %all-gather.24.cloned.1.call-done.a_ref, bf16[3,4096,8192]{2,1,0:T(8,128)(2,1)} %w_ref.11), custom_call_target="tpu_custom_call" | custom-call | flops 68719476736 | bytes 92274688 | tf_op jit(solution)/shard_map/teacher_up/pallas_call | solution.py:34
  756.3 83.5 %fusion.85 = bf16[1024,4096]{1,0:T(8,128)(2,1)} fusion(bf16[1024,8192]{1,0:T(8,128)(2,1)} %teacher_up.10, bf16[3,8192,4096]{2,1,0:T(8,128)(2,1)} %param.13), kind=kOutput, calls=%fused_computation.91 | convolution fusion | flops 68723671040 | bytes 92274688 | tf_op jit(solution)/shard_map/dot_general | solution.py:199
  839.9 84.5 %teacher_up.8 = bf16[1024,8192]{1,0:T(8,128)(2,1)} custom-call(bf16[1024,4096]{1,0:T(8,128)(2,1)} %all-gather.18.cloned.1.call-done.a_ref, bf16[3,4096,8192]{2,1,0:T(8,128)(2,1)} %w_ref.11), custom_call_target="tpu_custom_call" | custom-call | flops 68719476736 | bytes 92274688 | tf_op jit(solution)/shard_map/teacher_up/pallas_call | solution.py:34
  924.4 79.6 %fusion.88 = bf16[1024,4096]{1,0:T(8,128)(2,1)} fusion(bf16[1024,8192]{1,0:T(8,128)(2,1)} %teacher_up.8, bf16[3,8192,4096]{2,1,0:T(8,128)(2,1)} %param.13), kind=kOutput, calls=%fused_computation.92 | convolution fusion | flops 68723671040 | bytes 92274688 | tf_op jit(solution)/shard_map/dot_general | solution.py:199
  1041.1 84.1 %teacher_up.11 = bf16[1024,8192]{1,0:T(8,128)(2,1)} custom-call(bf16[1024,4096]{1,0:T(8,128)(2,1)} %all-gather.26.cloned.1.call-done.a_ref, bf16[3,4096,8192]{2,1,0:T(8,128)(2,1)} %w_ref.11), custom_call_target="tpu_custom_call" | custom-call | flops 68719476736 | bytes 92274688 | tf_op jit(solution)/shard_map/teacher_up/pallas_call | solution.py:34
  1125.2 79.8 %fusion.91 = bf16[1024,4096]{1,0:T(8,128)(2,1)} fusion(bf16[1024,8192]{1,0:T(8,128)(2,1)} %teacher_up.11, bf16[3,8192,4096]{2,1,0:T(8,128)(2,1)} %param.13), kind=kOutput, calls=%fused_computation.93 | convolution fusion | flops 68723671040 | bytes 92274688 | tf_op jit(solution)/shard_map/dot_general | solution.py:199
  1387.7 30.9 %errors.2 = (bf16[4,1024,2048]{2,1,0:T(8,128)(2,1)}, bf16[4,1024,2048]{2,1,0:T(8,128)(2,1)}, f32[8,2048]{1,0:T(8,128)S(1)}) custom-call(bf16[4,1024,2048]{2,1,0:T(8,128)(2,1)} %bitcast.209, bf16[8,1024,2048]{2,1,0:T(8,128)(2,1)} %bitcast.201), custom_call_target="tpu_custom_call" | custom-call | flops 134217728 | bytes 67108864 | tf_op jit(solution)/shard_map/errors/pallas_call | solution.py:107
  1418.6 29.3 %multiply_convert_fusion.1 = (bf16[4096,1024]{1,0:T(8,128)(2,1)}, f32[4096,1024]{1,0:T(8,128)}) fusion(bf16[4096,2048]{1,0:T(8,128)(2,1)} %bitcast.211, bf16[1,2048,8192]{2,1,0:T(8,128)(2,1)} %param.15, s32[]{:T(128)S(6)} %select_n.18), kind=kOutput, calls=%fused_computation.66 | convolution fusion | flops 17217617920 | bytes 46137348 | tf_op jit(solution)/shard_map/dot_general | solution.py:199
  1447.9 27.8 %multiply_convert_fusion = (bf16[4096,1024]{1,0:T(8,128)(2,1)}, f32[4096,1024]{1,0:T(8,128)}) fusion(bf16[4096,2048]{1,0:T(8,128)(2,1)S(1)} %bitcast.218, bf16[1,2048,8192]{2,1,0:T(8,128)(2,1)} %param.15, s32[]{:T(128)S(6)} %select_n.18), kind=kOutput, calls=%fused_computation.65 | convolution fusion | flops 17217617920 | bytes 46137348 | tf_op jit(solution)/shard_map/dot_general | solution.py:199
  1475.7 30.3 %errors.3 = (bf16[4,1024,2048]{2,1,0:T(8,128)(2,1)}, bf16[4,1024,2048]{2,1,0:T(8,128)(2,1)}, f32[8,2048]{1,0:T(8,128)S(1)}) custom-call(bf16[4,1024,2048]{2,1,0:T(8,128)(2,1)} %bitcast.210, bf16[8,1024,2048]{2,1,0:T(8,128)(2,1)} %bitcast.202), custom_call_target="tpu_custom_call" | custom-call | flops 134217728 | bytes 67108864 | tf_op jit(solution)/shard_map/errors/pallas_call | solution.py:107
  1560.5 32.9 %fusion.49 = bf16[4096,1024]{1,0:T(8,128)(2,1)S(1)} fusion(f32[4096,1024]{1,0:T(8,128)} %get-tuple-element.87, bf16[4096,2048]{1,0:T(8,128)(2,1)} %bitcast.227, bf16[1,8192,2048]{2,1,0:T(8,128)(2,1)} %param.16, s32[]{:T(128)S(6)} %select_n.18), kind=kOutput, calls=%fused_computation.58 | convolution fusion | flops 17263755264 | bytes 46137348 | tf_op jit(solution)/shard_map/dot_general | solution.py:199
  1630.8 34.5 %fusion.42 = bf16[4096,1024]{1,0:T(8,128)(2,1)} fusion(f32[4096,1024]{1,0:T(8,128)} %get-tuple-element.85, bf16[4096,2048]{1,0:T(8,128)(2,1)} %bitcast.220, bf16[1,8192,2048]{2,1,0:T(8,128)(2,1)} %param.16, s32[]{:T(128)S(6)} %select_n.18), kind=kOutput, calls=%fused_computation.51 | convolution fusion | flops 17263755264 | bytes 46137348 | tf_op jit(solution)/shard_map/dot_general | solution.py:199
  1812.5 36.2 %collective-permute-done.14.piece_ref = bf16[512,2048]{1,0:T(8,128)(2,1)S(1)} collective-permute-done((bf16[512,2048]{1,0:T(8,128)(2,1)}, bf16[512,2048]{1,0:T(8,128)(2,1)S(1)}, u32[]{:S(2)}, u32[]{:S(2)}) %collective-permute-start.14) | collective-permute-done | bytes 2097184 | tf_op jit(solution)/shard_map/ppermute | solution.py:175
  1851.8 41.8 %collective-permute-done.22.piece_ref = bf16[512,2048]{1,0:T(8,128)(2,1)S(1)} collective-permute-done((bf16[512,2048]{1,0:T(8,128)(2,1)S(1)}, bf16[512,2048]{1,0:T(8,128)(2,1)S(1)}, u32[]{:S(2)}, u32[]{:S(2)}) %collective-permute-start.22) | collective-permute-done | bytes 2097184 | tf_op jit(solution)/shard_map/ppermute | solution.py:175
  1903.2 35.4 %collective-permute-done.piece_ref = bf16[1024,1024]{1,0:T(8,128)(2,1)S(1)} collective-permute-done((bf16[1024,1024]{1,0:T(8,128)(2,1)}, bf16[1024,1024]{1,0:T(8,128)(2,1)S(1)}, u32[]{:S(2)}, u32[]{:S(2)}) %collective-permute-start) | collective-permute-done | bytes 2097184 | tf_op jit(solution)/shard_map/ppermute | solution.py:175
  1943.7 39.9 %collective-permute-done.8.piece_ref = bf16[1024,1024]{1,0:T(8,128)(2,1)S(1)} collective-permute-done((bf16[1024,1024]{1,0:T(8,128)(2,1)S(1)}, bf16[1024,1024]{1,0:T(8,128)(2,1)S(1)}, u32[]{:S(2)}, u32[]{:S(2)}) %collective-permute-start.8) | collective-permute-done | bytes 2097184 | tf_op jit(solution)/shard_map/ppermute | solution.py:175
  (434 shorter events, 864.3 us)
Async XLA Ops:
  21.2 183.4 %all-gather.22.cloned.1.call-start = ((), (), s32[]{:S(2)}) async-start(), calls=%async_computation.14 | async-start | bytes 12582912 | tf_op jit(solution)/shard_map/all_gather | solution.py:253
  27.8 261.7 %reduce-scatter.7.cloned.1.call-start = ((), (), s32[]{:S(2)}) async-start(), calls=%async_computation.8 | async-start | bytes 12582912 | tf_op jit(solution)/shard_map/reduce_scatter | solution.py:258
  204.4 177.6 %all-gather.16.cloned.1.call-start = ((), (), s32[]{:S(2)}) async-start(), calls=%async_computation.9 | async-start | bytes 12582912 | tf_op jit(solution)/shard_map/all_gather | solution.py:253
  299.3 345.1 %reduce-scatter.13.cloned.1.call-start = ((), (), s32[]{:S(2)}) async-start(), calls=%async_computation.15 | async-start | bytes 12582912 | tf_op jit(solution)/shard_map/reduce_scatter | solution.py:258
  381.2 263.3 %all-gather.12.cloned.1.call-start = ((), (), s32[]{:S(2)}) async-start(), calls=%async_computation.6 | async-start | bytes 37748736 | tf_op jit(solution)/shard_map/all_gather | solution.py:238
  381.7 271.9 %reduce-scatter.9.cloned.1.call-start = ((), (), s32[]{:S(2)}) async-start(), calls=%async_computation.10 | async-start | bytes 12582912 | tf_op jit(solution)/shard_map/reduce_scatter | solution.py:258
  546.9 125.0 %all-gather.24.cloned.1.call-start = ((), (), s32[]{:S(2)}) async-start(), calls=%async_computation.16 | async-start | bytes 12582912 | tf_op jit(solution)/shard_map/all_gather | solution.py:253
  653.5 186.4 %all-gather.18.cloned.1.call-start = ((), (), s32[]{:S(2)}) async-start(), calls=%async_computation.11 | async-start | bytes 12582912 | tf_op jit(solution)/shard_map/all_gather | solution.py:253
  663.3 340.9 %all-gather.30.cloned.1.call-start = ((), (), s32[]{:S(2)}) async-start(), calls=%async_computation.21 | async-start | bytes 37748736 | tf_op jit(solution)/shard_map/all_gather | solution.py:248
  663.8 340.3 %reduce-scatter.15.cloned.1.call-start = ((), (), s32[]{:S(2)}) async-start(), calls=%async_computation.17 | async-start | bytes 12582912 | tf_op jit(solution)/shard_map/reduce_scatter | solution.py:258
  839.8 179.3 %reduce-scatter.11.cloned.1.call-start = ((), (), s32[]{:S(2)}) async-start(), calls=%async_computation.12 | async-start | bytes 12582912 | tf_op jit(solution)/shard_map/reduce_scatter | solution.py:258
  1014.5 205.6 %reduce-scatter.17.cloned.1.call-start = ((), (), s32[]{:S(2)}) async-start(), calls=%async_computation.19 | async-start | bytes 12582912 | tf_op jit(solution)/shard_map/reduce_scatter | solution.py:258
  1205.1 142.3 %all-gather.20.cloned.1.call-start = ((), (), s32[]{:S(2)}) async-start(), calls=%async_computation.13 | async-start | bytes 18874368 | tf_op jit(solution)/shard_map/all_gather | solution.py:223
  1205.7 270.0 %all-gather.28.cloned.1.call-start = ((), (), s32[]{:S(2)}) async-start(), calls=%async_computation.20 | async-start | bytes 18874368 | tf_op jit(solution)/shard_map/all_gather | solution.py:223
  1806.1 87.5 %collective-permute-start.22 = (bf16[512,2048]{1,0:T(8,128)(2,1)S(1)}, bf16[512,2048]{1,0:T(8,128)(2,1)S(1)}, u32[]{:S(2)}, u32[]{:S(2)}) collective-permute-start(bf16[512,2048]{1,0:T(8,128)(2,1)S(1)} %copy-done.8), channel_id=1, source_target_pairs={{0,2},{1,3},{2,0},{3,1},{4,6},{5,7},{6,4},{7,5}} | collective-permute-start | bytes 6291464 | tf_op jit(solution)/shard_map/ppermute | solution.py:175
  1807.6 88.4 %collective-permute-start.20 = (bf16[512,2048]{1,0:T(8,128)(2,1)}, bf16[512,2048]{1,0:T(8,128)(2,1)S(1)}, u32[]{:S(2)}, u32[]{:S(2)}) collective-permute-start(bf16[512,2048]{1,0:T(8,128)(2,1)} %add_convert_fusion.5.piece_ref), channel_id=1, source_target_pairs={{0,4},{1,5},{2,6},{3,7},{4,0},{5,1},{6,2},{7,3}} | collective-permute-start | bytes 6291464 | tf_op jit(solution)/shard_map/ppermute | solution.py:175
  1896.0 87.6 %collective-permute-start.8 = (bf16[1024,1024]{1,0:T(8,128)(2,1)S(1)}, bf16[1024,1024]{1,0:T(8,128)(2,1)S(1)}, u32[]{:S(2)}, u32[]{:S(2)}) collective-permute-start(bf16[1024,1024]{1,0:T(8,128)(2,1)S(1)} %add_convert_fusion.2.piece_ref), channel_id=1, source_target_pairs={{0,2},{1,3},{2,0},{3,1},{4,6},{5,7},{6,4},{7,5}} | collective-permute-start | bytes 6291464 | tf_op jit(solution)/shard_map/ppermute | solution.py:175
  1897.4 88.6 %collective-permute-start.6 = (bf16[1024,1024]{1,0:T(8,128)(2,1)}, bf16[1024,1024]{1,0:T(8,128)(2,1)}, u32[]{:S(2)}, u32[]{:S(2)}) collective-permute-start(bf16[1024,1024]{1,0:T(8,128)(2,1)} %add_convert_fusion.3.piece_ref), channel_id=1, source_target_pairs={{0,4},{1,5},{2,6},{3,7},{4,0},{5,1},{6,2},{7,3}} | collective-permute-start | bytes 6291464 | tf_op jit(solution)/shard_map/ppermute | solution.py:175
  1900.2 88.6 %collective-permute-start.52 = (bf16[256,2048]{1,0:T(8,128)(2,1)}, bf16[256,2048]{1,0:T(8,128)(2,1)}, u32[]{:S(2)}, u32[]{:S(2)}) collective-permute-start(bf16[256,2048]{1,0:T(8,128)(2,1)} %collective-permute-done.45.piece_ref), channel_id=1, source_target_pairs={{0,1},{1,0},{2,3},{3,2},{4,5},{5,4},{6,7},{7,6}} | collective-permute-start | bytes 3145736 | tf_op jit(solution)/shard_map/ppermute | solution.py:175
  2085.2 181.2 %collective-permute-start.7 = (bf16[1024,1024]{1,0:T(8,128)(2,1)}, bf16[1024,1024]{1,0:T(8,128)(2,1)}, u32[]{:S(2)}, u32[]{:S(2)}) collective-permute-start(bf16[1024,1024]{1,0:T(8,128)(2,1)} %collective-permute-done.6.piece_ref), channel_id=1, source_target_pairs={{0,1},{1,0},{2,3},{3,2},{4,5},{5,4},{6,7},{7,6}} | collective-permute-start | bytes 6291464 | tf_op jit(solution)/shard_map/ppermute | solution.py:175
  2085.3 189.0 %collective-permute-start.19 = (bf16[512,2048]{1,0:T(8,128)(2,1)}, bf16[512,2048]{1,0:T(8,128)(2,1)}, u32[]{:S(2)}, u32[]{:S(2)}) collective-permute-start(bf16[512,2048]{1,0:T(8,128)(2,1)} %collective-permute-done.18.piece_ref), channel_id=1, source_target_pairs={{0,1},{1,0},{2,3},{3,2},{4,5},{5,4},{6,7},{7,6}} | collective-permute-start | bytes 6291464 | tf_op jit(solution)/shard_map/ppermute | solution.py:175
  2085.8 196.4 %collective-permute-start.16 = (bf16[512,2048]{1,0:T(8,128)(2,1)}, bf16[512,2048]{1,0:T(8,128)(2,1)}, u32[]{:S(2)}, u32[]{:S(2)}) collective-permute-start(bf16[512,2048]{1,0:T(8,128)(2,1)} %collective-permute-done.15.piece_ref), channel_id=1, source_target_pairs={{0,1},{1,0},{2,3},{3,2},{4,5},{5,4},{6,7},{7,6}} | collective-permute-start | bytes 6291464 | tf_op jit(solution)/shard_map/ppermute | solution.py:175
  2103.4 182.7 %collective-permute-start.5 = (bf16[1024,1024]{1,0:T(8,128)(2,1)}, bf16[1024,1024]{1,0:T(8,128)(2,1)}, u32[]{:S(2)}, u32[]{:S(2)}) collective-permute-start(bf16[1024,1024]{1,0:T(8,128)(2,1)} %collective-permute-done.4.piece_ref), channel_id=1, source_target_pairs={{0,1},{1,0},{2,3},{3,2},{4,5},{5,4},{6,7},{7,6}} | collective-permute-start | bytes 6291464 | tf_op jit(solution)/shard_map/ppermute | solution.py:175
  2104.8 189.2 %collective-permute-start.2 = (bf16[1024,1024]{1,0:T(8,128)(2,1)}, bf16[1024,1024]{1,0:T(8,128)(2,1)}, u32[]{:S(2)}, u32[]{:S(2)}) collective-permute-start(bf16[1024,1024]{1,0:T(8,128)(2,1)} %collective-permute-done.1.piece_ref), channel_id=1, source_target_pairs={{0,1},{1,0},{2,3},{3,2},{4,5},{5,4},{6,7},{7,6}} | collective-permute-start | bytes 6291464 | tf_op jit(solution)/shard_map/ppermute | solution.py:175
  (119 other events, 3653.7 us)
Sparse Core Ops, SparseCore 0:
  21.4 19.2 all-gather.13
  42.2 18.2 all-gather.21
  204.5 14.8 reduce-scatter.6
  299.4 18.2 all-gather.15
  381.3 14.9 reduce-scatter.12
  397.9 156.3 all-gather.11
  557.1 13.6 reduce-scatter.8
  653.6 18.2 all-gather.23
  674.0 18.2 all-gather.17
  694.0 156.2 all-gather.29
  853.1 13.6 reduce-scatter.14
  1004.2 14.8 reduce-scatter.10
  1021.2 18.2 all-gather.25
  1205.2 14.8 reduce-scatter.16
  1221.8 125.5 all-gather.19
  1349.6 84.1 all-gather.27

commit v2 on v0

v2 whole, which is shorter than its diff:
```python
import functools

import jax
import jax.numpy as jnp
from jax import lax
from jax.experimental import pallas as pl
from jax.experimental.pallas import tpu as pltpu
from jax.sharding import PartitionSpec as P


EPS = 1e-6
VMEM_CAP = 64 * 1024 * 1024 - 65536
AXES = ("data", "model")


def after(values, dep):
    return lax.optimization_barrier((values, dep))[0]


def rms_unit(values):
    return values * lax.rsqrt(jnp.mean(values * values, axis=-1, keepdims=True) + EPS)


def mlp_kernel(layer, steps, wide, residual, where_ref, *refs):
    if residual:
        a_hbm, up_hbm, down_hbm, s_hbm, o_hbm, a_ref, up_ref, down_ref, first, second, act, acc, out, a_sem, up_sem, down_sem, o_sem, s_ref, s_sem = refs
    else:
        a_hbm, up_hbm, down_hbm, o_hbm, a_ref, up_ref, down_ref, first, second, act, acc, out, a_sem, up_sem, down_sem, o_sem = refs
    j = pl.program_id(0)
    rows, width = acc.shape
    tile = act.shape[2]
    half = tile // 2
    parts = 4
    size = rows // parts
    now = lax.rem(j, 2)

    def a_copy(r):
        source = pl.ds(pl.multiple_of(where_ref[0] * rows + r * size, size), size)
        return pltpu.make_async_copy(a_hbm.at[source], a_ref.at[pl.ds(r * size, size)], a_sem.at[r])

    def up_copy(k):
        return pltpu.make_async_copy(up_hbm.at[layer, :, pl.ds(pl.multiple_of(k * tile, tile), tile)], up_ref.at[lax.rem(k, 2)], up_sem.at[lax.rem(k, 2)])

    def down_copy(k):
        return pltpu.make_async_copy(down_hbm.at[layer, pl.ds(pl.multiple_of(k * tile, tile), tile)], down_ref.at[lax.rem(k, 2)], down_sem.at[lax.rem(k, 2)])

    def out_copy(k):
        cols = pl.ds(k * wide, wide)
        return pltpu.make_async_copy(out.at[:, cols], o_hbm.at[:, cols], o_sem.at[k])

    @pl.when(j == 0)
    def _():
        up_copy(0).start()
        for r in range(parts):
            a_copy(r).start()
        up_copy(1).start()
        down_copy(0).start()
        if residual:
            pltpu.make_async_copy(s_hbm, s_ref, s_sem.at[0]).start()
        up_copy(0).wait()
        for r in range(parts):
            part = slice(r * size, (r + 1) * size)
            a_copy(r).wait()
            first[part, :] = jnp.dot(a_ref[part, :], up_ref[0, :, :half], preferred_element_type=jnp.float32)
            second[part, :] = jnp.dot(a_ref[part, :], up_ref[0, :, half:], preferred_element_type=jnp.float32)
        act[0, :, :half] = jax.nn.gelu(first[...]).astype(jnp.bfloat16)

    @pl.when((j > 0) & (j < steps))
    def _():
        @pl.when(j + 1 < steps)
        def _():
            up_copy(j + 1).start()

        down_copy(j).start()
        up_copy(j).wait()
        act[1 - now, :, half:] = jax.nn.gelu(second[...]).astype(jnp.bfloat16)
        first[...] = jnp.dot(a_ref[...], up_ref[now, :, :half], preferred_element_type=jnp.float32)
        for r in range(parts):
            part = slice(r * size, (r + 1) * size)
            act[now, part, :half] = jax.nn.gelu(first[part, :]).astype(jnp.bfloat16)
            second[part, :] = jnp.dot(a_ref[part, :], up_ref[now, :, half:], preferred_element_type=jnp.float32)

    @pl.when(j == steps)
    def _():
        act[1 - now, :, half:] = jax.nn.gelu(second[...]).astype(jnp.bfloat16)

    def down(first_tile, last_tile):
        down_copy(j - 1).wait()
        if last_tile and residual:
            pltpu.make_async_copy(s_hbm, s_ref, s_sem.at[0]).wait()
        for k in range(width // wide):
            cols = slice(k * wide, (k + 1) * wide)
            total = jnp.dot(act[1 - now], down_ref[1 - now, :, cols], preferred_element_type=jnp.float32)
            if not first_tile:
                total = acc[:, cols] + total
            if not last_tile:
                acc[:, cols] = total
            else:
                if residual:
                    total = s_ref[:, cols].astype(jnp.float32) + total
                out[:, cols] = total.astype(jnp.bfloat16)
                out_copy(k).start()
        if last_tile:
            for k in range(width // wide):
                out_copy(k).wait()

    @pl.when(j == 1)
    def _():
        down(True, False)

    @pl.when((j > 1) & (j < steps))
    def _():
        down(False, False)

    @pl.when(j == steps)
    def _():
        down(False, True)


def mlp(a, up, down, layer, state=None, rows=None, where=None, tile=512, wide=512):
    depth = a.shape[1]
    rows = rows or a.shape[0]
    where = jnp.zeros((1,), jnp.int32) if where is None else where.astype(jnp.int32).reshape(1)
    hidden = up.shape[2]
    width = down.shape[2]
    steps = hidden // tile
    hbm = pl.BlockSpec(memory_space=pl.ANY)
    scratch = [
        pltpu.VMEM((rows, depth), jnp.bfloat16),
        pltpu.VMEM((2, depth, tile), jnp.bfloat16),
        pltpu.VMEM((2, tile, width), jnp.bfloat16),
        pltpu.VMEM((rows, tile // 2), jnp.float32),
        pltpu.VMEM((rows, tile // 2), jnp.float32),
        pltpu.VMEM((2, rows, tile), jnp.bfloat16),
        pltpu.VMEM((rows, width), jnp.float32),
        pltpu.VMEM((rows, width), jnp.bfloat16),
        pltpu.SemaphoreType.DMA((4,)),
        pltpu.SemaphoreType.DMA((2,)),
        pltpu.SemaphoreType.DMA((2,)),
        pltpu.SemaphoreType.DMA((width // wide,)),
    ]
    args = [a, up, down]
    if state is not None:
        args.append(state)
        scratch += [pltpu.VMEM((rows, width), jnp.bfloat16), pltpu.SemaphoreType.DMA((1,))]
    return pl.pallas_call(
        functools.partial(mlp_kernel, layer, steps, wide, state is not None),
        grid_spec=pltpu.PrefetchScalarGridSpec(
            num_scalar_prefetch=1,
            grid=(steps + 1,),
            in_specs=[hbm] * len(args),
            out_specs=hbm,
            scratch_shapes=scratch,
        ),
        out_shape=jax.ShapeDtypeStruct((rows, width), jnp.bfloat16),
        compiler_params=pltpu.CompilerParams(vmem_limit_bytes=VMEM_CAP),
        cost_estimate=pl.CostEstimate(
            flops=2 * rows * hidden * (depth + width),
            bytes_accessed=2 * (rows * (depth + width) + hidden * (depth + width)),
            transcendentals=rows * hidden,
        ),
        name="mlp",
    )(where, *args)


def norm_kernel(h_ref, g_ref, a_ref):
    state = h_ref[...].astype(jnp.float32)
    inv = lax.rsqrt(jnp.mean(state * state, axis=-1, keepdims=True) + EPS)
    a_ref[...] = (state * inv * g_ref[...]).astype(jnp.bfloat16)


def step_kernel(h_ref, *refs):
    *parts, g_ref, o_ref, a_ref = refs
    delta = parts[0][...].astype(jnp.float32)
    if len(parts) > 1:
        delta = (delta + parts[1][...].astype(jnp.float32)).astype(jnp.bfloat16).astype(jnp.float32)
    state = (h_ref[...].astype(jnp.float32) + delta).astype(jnp.bfloat16)
    o_ref[...] = state
    state = state.astype(jnp.float32)
    inv = lax.rsqrt(jnp.mean(state * state, axis=-1, keepdims=True) + EPS)
    a_ref[...] = (state * inv * g_ref[...]).astype(jnp.bfloat16)


def teacher_norm(hidden, delta, gains, layer, which=0, block=128):
    rows, width = hidden.shape[-2:]
    spec = pl.BlockSpec((block, width), lambda i: (i, 0))
    source = spec if hidden.ndim == 2 else pl.BlockSpec((None, block, width), lambda i: (which, i, 0))
    gain_spec = pl.BlockSpec((1, width), lambda i: (0, 0))
    shape = jax.ShapeDtypeStruct((rows, width), jnp.bfloat16)
    count = rows * width
    common = dict(
        grid=(rows // block,),
        compiler_params=pltpu.CompilerParams(vmem_limit_bytes=VMEM_CAP),
    )
    gain = gains[layer : layer + 1]
    if not delta:
        cost = pl.CostEstimate(flops=8 * count, bytes_accessed=4 * count, transcendentals=0)
        return hidden, pl.pallas_call(norm_kernel, in_specs=[source, gain_spec], out_specs=spec, out_shape=shape, cost_estimate=cost, name="norm", **common)(hidden, gain)
    cost = pl.CostEstimate(flops=10 * count, bytes_accessed=8 * count, transcendentals=0)
    return pl.pallas_call(step_kernel, in_specs=[source] + [spec] * len(delta) + [gain_spec], out_specs=[spec, spec], out_shape=[shape, shape], cost_estimate=cost, name="step", **common)(hidden, *delta, gain)


def pre_kernel(sub, s_ref, g_ref, w_ref, a_ref, p_ref, u_ref):
    for r in range(s_ref.shape[0] // sub):
        part = slice(r * sub, (r + 1) * sub)
        state = s_ref[part, :].astype(jnp.float32)
        inv = lax.rsqrt(jnp.mean(state * state, axis=-1, keepdims=True) + EPS)
        a_ref[part, :] = (state * inv * g_ref[...]).astype(jnp.bfloat16)
    for r in range(s_ref.shape[0] // sub):
        part = slice(r * sub, (r + 1) * sub)
        pre = jnp.dot(a_ref[part, :], w_ref[...], preferred_element_type=jnp.float32)
        p_ref[part, :] = pre
        u_ref[part, :] = jax.nn.gelu(pre).astype(jnp.bfloat16)


def pre_of(states, gain, weights, parity, block=512, sub=256):
    n_seq, seq_len, width = states.shape
    cols = weights.shape[1]
    half = n_seq // 2
    rows = half * seq_len
    steps = seq_len // block
    out = lambda w: pl.BlockSpec((block, w), lambda i, j: (i * steps + j, 0))
    return pl.pallas_call(
        functools.partial(pre_kernel, sub),
        grid=(half, steps),
        in_specs=[
            pl.BlockSpec((None, block, width), lambda i, j: (2 * i + parity, j, 0)),
            pl.BlockSpec((1, width), lambda i, j: (0, 0)),
            pl.BlockSpec((width, cols), lambda i, j: (0, 0)),
        ],
        out_specs=[out(width), out(cols), out(cols)],
        out_shape=[
            jax.ShapeDtypeStruct((rows, width), jnp.bfloat16),
            jax.ShapeDtypeStruct((rows, cols), jnp.float32),
            jax.ShapeDtypeStruct((rows, cols), jnp.bfloat16),
        ],
        compiler_params=pltpu.CompilerParams(vmem_limit_bytes=VMEM_CAP),
        cost_estimate=pl.CostEstimate(flops=2 * rows * width * cols, bytes_accessed=rows * (4 * width + 6 * cols), transcendentals=rows * cols),
        name="pre",
    )(states, gain, weights)


def proj_kernel(scale, first, last, me_ref, f_ref, z_ref, s_ref, *refs):
    state = s_ref[...].astype(jnp.float32)
    inv = lax.rsqrt(jnp.mean(state * state, axis=-1, keepdims=True) + EPS)
    error = z_ref[...].astype(jnp.float32) - state * inv
    rows, width = error.shape
    out_ref, sq_ref = refs[-3:-1]
    total = refs[-1]
    k = pl.program_id(0)

    @pl.when(k == 0)
    def _():
        sq_ref[...] = jnp.zeros_like(sq_ref)
        if first:
            total[...] = jnp.zeros_like(total)
        else:
            total[...] = refs[0][...]

    sq_ref[...] += jnp.sum((error * error).reshape(rows // 8, 8, width), axis=0)
    total[...] += lax.dot_general(f_ref[...], error.astype(jnp.bfloat16), (((0,), (0,)), ((), ())), preferred_element_type=jnp.float32)

    @pl.when(k == pl.num_programs(0) - 1)
    def _():
        out_ref[...] = (scale * total[...]).astype(jnp.bfloat16) if last else total[...]


def proj_part(me, feat, targets, states, parity, scale, total, last):
    n_seq, _, width = states.shape
    size = n_seq
    cols = feat.shape[1]
    rows = feat.shape[0] // size
    whole = pl.BlockSpec((cols, width), lambda k, me: (0, 0))
    in_specs = [
        pl.BlockSpec((rows, cols), lambda k, me: (k, 0)),
        pl.BlockSpec((rows, width), lambda k, me: (me[0] ^ k, 0)),
        pl.BlockSpec((None, rows, width), lambda k, me: (2 * ((me[0] ^ k) // 2) + parity, (me[0] ^ k) % 2, 0)),
    ]
    args = [me.reshape(1), feat, targets, states]
    if total is not None:
        in_specs.append(whole)
        args.append(total)
    return pl.pallas_call(
        functools.partial(proj_kernel, scale, total is None, last),
        grid_spec=pltpu.PrefetchScalarGridSpec(
            num_scalar_prefetch=1,
            grid=(size,),
            in_specs=in_specs,
            out_specs=[whole, pl.BlockSpec((8, width), lambda k, me: (0, 0))],
            scratch_shapes=[pltpu.VMEM((cols, width), jnp.float32)],
        ),
        out_shape=[
            jax.ShapeDtypeStruct((cols, width), jnp.bfloat16 if last else jnp.float32),
            jax.ShapeDtypeStruct((8, width), jnp.float32),
        ],
        compiler_params=pltpu.CompilerParams(vmem_limit_bytes=VMEM_CAP),
        cost_estimate=pl.CostEstimate(flops=2 * size * rows * cols * width, bytes_accessed=size * rows * (4 * width + 2 * cols), transcendentals=0),
        name="proj",
    )(*args)


def down_kernel(scale, first, z_ref, s_ref, u_ref, *refs):
    d_ref, out_ref, total = refs[-3:]
    k = pl.program_id(0) * pl.num_programs(1) + pl.program_id(1)

    @pl.when(k == 0)
    def _():
        total[...] = jnp.zeros_like(total) if first else refs[0][...]

    state = s_ref[...].astype(jnp.float32)
    inv = lax.rsqrt(jnp.mean(state * state, axis=-1, keepdims=True) + EPS)
    unit = state * inv
    error = z_ref[...].astype(jnp.float32) - unit
    lean = jnp.mean(error * unit, axis=-1, keepdims=True)
    d_out = ((error - unit * lean) * (-scale * inv)).astype(jnp.bfloat16)
    d_ref[...] = d_out
    cols = total.shape[0]
    for h in range(4):
        part = slice(h * cols // 4, (h + 1) * cols // 4)
        total[part, :] += lax.dot_general(u_ref[:, part], d_out, (((0,), (0,)), ((), ())), preferred_element_type=jnp.float32)

    @pl.when(k == pl.num_programs(0) * pl.num_programs(1) - 1)
    def _():
        out_ref[...] = total[...].astype(out_ref.dtype)


def down_part_of(ups, targets, states, parity, scale, total, last, block=512):
    n_seq, seq_len, width = states.shape
    half = n_seq // 2
    cols = ups.shape[1]
    rows = half * seq_len
    steps = seq_len // block
    spec = lambda w: pl.BlockSpec((block, w), lambda i, j: (i * steps + j, 0))
    whole = pl.BlockSpec((cols, width), lambda i, j: (0, 0), pipeline_mode=pl.Buffered(1))
    in_specs = [spec(width), pl.BlockSpec((None, block, width), lambda i, j: (2 * i + parity, j, 0)), spec(cols)]
    args = [targets, states, ups]
    if total is not None:
        in_specs.append(whole)
        args.append(total)
    return pl.pallas_call(
        functools.partial(down_kernel, scale, total is None),
        grid=(half, steps),
        in_specs=in_specs,
        out_specs=[spec(width), whole],
        out_shape=[
            jax.ShapeDtypeStruct((rows, width), jnp.bfloat16),
            jax.ShapeDtypeStruct((cols, width), jnp.bfloat16 if last else jnp.float32),
        ],
        scratch_shapes=[pltpu.VMEM((cols, width), jnp.float32)],
        compiler_params=pltpu.CompilerParams(vmem_limit_bytes=VMEM_CAP),
        cost_estimate=pl.CostEstimate(flops=2 * rows * width * cols, bytes_accessed=rows * (6 * width + 2 * cols), transcendentals=0),
        name="down",
    )(*args)


def spread_kernel(piece_ref, *rest):
    rest[-1][...] = piece_ref[...].astype(jnp.float32)


def spread(out, pieces, first_row, shape, block=512):
    count, rows, cols = pieces.shape
    specs = [pl.BlockSpec((None, block, cols), lambda k, i: (k, i, 0))]
    args = [pieces]
    alias = {}
    if out is not None:
        specs.append(pl.BlockSpec(memory_space=pl.ANY))
        args.append(out)
        alias = {1: 0}
    return pl.pallas_call(
        spread_kernel,
        grid=(count, rows // block),
        in_specs=specs,
        out_specs=pl.BlockSpec((block, cols), lambda k, i: (first_row // block + i, k)),
        out_shape=jax.ShapeDtypeStruct(shape, jnp.float32),
        input_output_aliases=alias,
        compiler_params=pltpu.CompilerParams(vmem_limit_bytes=VMEM_CAP),
        cost_estimate=pl.CostEstimate(flops=count * rows * cols, bytes_accessed=6 * count * rows * cols, transcendentals=0),
        name="spread",
    )(*args)


def flip(value, bits, size):
    return lax.ppermute(value, AXES, [(i, i ^ bits) for i in range(size)])


def gelu_back(pre_act, grad_out):
    return jax.vjp(jax.nn.gelu, pre_act)[1](grad_out)[0]


def dot(a, b, dims):
    return lax.dot_general(a, b, (dims, ((), ())), preferred_element_type=jnp.float32)


def solution(mesh):
    size = mesh.shape["data"] * mesh.shape["model"]

    def step(teacher_in, student_in, teacher_gain, teacher_up_w, teacher_down, student_gain, student_up, student_down, student_proj):
        me = lax.axis_index("data") * 2 + lax.axis_index("model")
        n_layers = teacher_up_w.shape[0]
        t_width = teacher_in.shape[2]
        _, seq_len, s_width = student_in.shape
        s_hidden = student_up.shape[2]
        part = s_hidden // size
        t_part = t_width // size
        total = size * seq_len * s_width
        grad_scale = 2.0 / total
        v_up, v_down, q_proj = student_up[0], student_down[0], student_proj[0]

        own = student_in[0]
        side = lax.axis_index("model")
        last = n_layers - 1
        hidden = [teacher_in, teacher_in]

        def finish(c, delta):
            total = sum(part.astype(jnp.float32) for part in delta).astype(jnp.bfloat16)
            hidden[c] = (hidden[c].astype(jnp.float32) + total.astype(jnp.float32)).astype(jnp.bfloat16)
            target = dot(hidden[c], q_proj, ((1,), (0,))).astype(jnp.bfloat16)
            return target, lax.all_gather(target, AXES, axis=0, tiled=True)

        def columns(c):
            rows = hidden[c].shape[0]
            pieces = []
            for bits in range(size):
                piece = lax.dynamic_slice(hidden[c], (0, (me ^ bits) * t_part), (rows, t_part))
                pieces.append(flip(piece, bits, size) if bits else piece)
            return jnp.concatenate(pieces, axis=0)

        def normed(c, delta, layer):
            hidden[c], act = teacher_norm(hidden[c], delta, teacher_gain, layer, c)
            return act, lax.all_gather(act, "model", axis=0, tiled=True)

        def teach(act, layer, **window):
            return mlp(act, teacher_up_w, teacher_down, layer, **window)

        acts = [normed(c, (), 0)[1] for c in range(2)]
        for layer in range(n_layers):
            if layer == 0:
                all_in = lax.all_gather(after(own, acts[0]), AXES, axis=0, tiled=False)
            if layer == 1:
                all_out = lax.all_gather(after(own_out, acts[0]), AXES, axis=0, tiled=False)
            partial = teach(acts[0], layer)
            delta_0 = (lax.psum_scatter(partial, "model", scatter_dimension=0, tiled=True),)
            if layer == 0:
                partial = teach(acts[1], layer)
                delta_1 = (lax.psum_scatter(partial, "model", scatter_dimension=0, tiled=True),)
                act, acts[0] = normed(0, after(delta_0, partial), layer + 1)
                own_act = teacher_norm(after(own, act), (), student_gain, 0)[1]
                own_out = mlp(own_act, student_up, student_down, 0, own)
                delta_1 = after(delta_1, (own_out, all_in))
            else:
                rows = acts[1].shape[0] // 2
                partial = teach(acts[1], layer, rows=rows, where=1 - side)
                moved = flip(partial, 1, size)
                delta_0 = after(delta_0, partial)
                if layer < last:
                    ready, acts[0] = normed(0, delta_0, layer + 1)
                else:
                    ready, targets_0 = finish(0, delta_0)
                    feat_0 = columns(0)
                partial = teach(after(acts[1], ready), layer, rows=rows, where=side)
                delta_1 = (partial, moved)
            if layer < last:
                if layer == 1:
                    delta_1 = after(delta_1, all_out)
                acts[1] = normed(1, delta_1, layer + 1)[1]
        target_1, targets_1 = finish(1, delta_1)
        feat_1 = columns(1)

        all_in, all_out, targets_0 = after((all_in, all_out, targets_0), target_1)
        up_part = lax.dynamic_slice(v_up, (0, me * part), (s_width, part))
        down_part = lax.dynamic_slice(v_down, (me * part, 0), (part, s_width))
        proj_sum, square_0 = proj_part(me, feat_0, targets_0, all_out, 0, grad_scale, None, False)
        acts, pre, ups = zip(*[pre_of(all_in, student_gain, up_part, c) for c in range(2)])
        d_out_0, down_sum = down_part_of(ups[0], targets_0, all_out, 0, grad_scale, None, False)
        targets_1 = after(targets_1, (proj_sum, ups[1], down_sum))
        proj_piece, square_1 = proj_part(me, feat_1, targets_1, all_out, 1, grad_scale, proj_sum, True)
        proj_all = lax.all_gather(proj_piece, AXES, axis=0, tiled=True)
        loss = (jnp.sum(square_0) + jnp.sum(square_1)) / total
        d_out_1, down_piece = down_part_of(ups[1], after(targets_1, proj_piece), all_out, 1, grad_scale, down_sum, True)
        down_all = lax.all_gather(down_piece, AXES, axis=0, tiled=True)

        d_outs = after((d_out_0, d_out_1), down_piece)
        d_pres = [gelu_back(pre[c], dot(d_outs[c], down_part, ((1,), (1,)))).astype(jnp.bfloat16) for c in range(2)]

        def up_rows(first, count):
            cols = slice(first, first + count)
            return (dot(acts[0][:, cols], d_pres[0], ((0,), (0,))) + dot(acts[1][:, cols], d_pres[1], ((0,), (0,)))).astype(jnp.bfloat16)

        half = s_width // 2
        up_piece = up_rows(0, half)
        up_all_0 = lax.all_gather(up_piece, AXES, axis=0, tiled=False)
        up_piece = up_rows(half, half)
        up_all_1 = lax.all_gather(up_piece[: half // 2], AXES, axis=0, tiled=False)
        up_all_2 = lax.all_gather(up_piece[half // 2 :], AXES, axis=0, tiled=False)

        d_pres = after(d_pres, up_piece)
        gain_sum = jnp.zeros((s_width,), jnp.float32)
        seqs = all_in.reshape(size // 2, 2, seq_len, s_width)
        for c in range(2):
            d_act = dot(d_pres[c], up_part, ((1,), (1,))).reshape(size // 2, seq_len, s_width)
            gain_sum = gain_sum + jnp.sum(d_act * rms_unit(seqs[:, c].astype(jnp.float32)), axis=(0, 1))
        grad_gain = lax.psum(gain_sum, AXES)
        grad_proj = after(proj_all, gain_sum).astype(jnp.float32)
        grad_down = after(down_all, grad_gain).astype(jnp.float32)
        shape = (s_width, s_hidden)
        grad_up = spread(None, up_all_0, 0, shape)
        grad_up = spread(grad_up, up_all_1, half, shape)
        grad_up = spread(grad_up, up_all_2, half + half // 2, shape)
        return (loss, grad_up[None], grad_down[None], grad_gain[None], grad_proj[None])

    return jax.shard_map(
        step,
        mesh=mesh,
        in_specs=(
            P("data", "model", None),
            P(("data", "model"), None, None),
            P(),
            P(None, None, "model"),
            P(None, "model", None),
            P(),
            P(),
            P(),
            P(),
        ),
        out_specs=(P(), P(), P(), P(), P()),
        check_vma=False,
    )
```

time: 3380 us -> 2100 us (0.62)
  waiting for transfers between devices: 1720 us -> 399 us
  Pallas kernels: 0 us -> 1310 us
  matrix products: 1250 us -> 194 us
  other arithmetic: 198 us -> 81 us
  local copies, waits for them, and re-layouts: 143 us -> 33 us
    psum x2 -> x0, waiting for transfers between devices: 1590 us -> none  [body(): lax.psum((loss_sum, grad_up, grad_down, grad_gain, jnp.stack(proj_list)),...]
    pallas_call x0 -> x25, Pallas kernels: none -> 1310 us  [the longest x9 1020 us: mlp(): pl.pallas_call(functools.partial(mlp_kernel, layer, steps, wide, state is...]
    dot_general x14 -> x10, matrix products: 1250 us -> 194 us  [dot(): lax.dot_general(a, b, (dims, ((), ())), preferred_element_type=jnp.float32)]
    all_gather x3 -> x15, waiting for transfers between devices: 88.1 us -> 276 us  [the longest x1 127 us: step(): down_all = lax.all_gather(down_piece, AXES, axis=0, tiled=True)]
    ppermute x0 -> x16, waiting for transfers between devices: none -> 120 us  [flip(): return lax.ppermute(value, AXES, [(i, i ^ bits) for i in range(size)])]
    unnamed x23 -> x28, local copies, waits for them, and re-layouts: 133 us -> 17.3 us
    dot_general x3 -> x0, other arithmetic: 101 us -> none  [body(): jnp.einsum('bsf,fd->bsd', up_act, teacher_down[layer], preferred_element_...]
    broadcast_in_dim x0 -> x2, other arithmetic: none -> 50.8 us  [the longest x1 31.6 us: step(): grad_down[None]]
  transfers between devices with their start and end apart: 8 -> 35, of which waited for: 7 -> 16; matrix products, arithmetic and copies ran while one was open for 10% -> 12% of each run, Pallas kernels for 0% -> 61%
where the time goes in v2:
time: 2100 us; the launch traced here: 2080 us
  Pallas kernels  1310 us (62%)
  waiting for transfers between devices  399 us (19%)
  matrix products  194 us (9%)
  other arithmetic  81 us (4%)
  local copies, waits for them, and re-layouts  33 us (2%)
  starting transfers between devices  24.3 us (1%)
  blocking collectives  22.8 us (1%)
    pallas_call x9, Pallas kernels, mlp(): pl.pallas_call(functools.partial(mlp_kernel, layer, steps, wide, state is...  1020 us
    dot_general x10, matrix products, dot(): lax.dot_general(a, b, (dims, ((), ())), preferred_element_type=jnp.float32)  194 us
    all_gather x1, waiting for transfers between devices, step(): down_all = lax.all_gather(down_piece, AXES, axis=0, tiled=True)  127 us
    ppermute x16, waiting for transfers between devices, flip(): return lax.ppermute(value, AXES, [(i, i ^ bits) for i in range(size)])  120 us
    pallas_call x2, Pallas kernels, down_part_of(): pl.pallas_call(functools.partial(down_kernel, scale, total is None), grid...  83.1 us
    all_gather x1, waiting for transfers between devices, step(): all_in = lax.all_gather(after(own, acts[0]), AXES, axis=0, tiled=False)  74.3 us
    pallas_call x2, Pallas kernels, pre_of(): pl.pallas_call(functools.partial(pre_kernel, sub), grid=(half, steps), in...  59.8 us
    pallas_call x2, Pallas kernels, proj_part(): pl.pallas_call(functools.partial(proj_kernel, scale, total is None, last)...  54.9 us
  transfers between devices with their start and end apart: 35, of which 16 were waited for; matrix products, arithmetic and copies ran while one was open for 12% of the time, Pallas kernels for 61%

profile of v2, /device:TPU:1, one launch (start us, length us, event | category | flops | bytes accessed | tf_op | source)
XLA Modules:
  0.0 2083.6 jit_solution(13450781977581762462)
XLA Ops:
  34.0 152.4 %mlp.9 = bf16[1024,4096]{1,0:T(8,128)(2,1)} custom-call(s32[1]{0:T(128)} %constant.13.clone.1.where_ref, bf16[1024,4096]{1,0:T(8,128)(2,1)} %all-gather.21.cloned.1.call-done.refs_0_, bf16[3,4096,8192]{2,1,0:T(8,128)(2,1)} %refs_1_.17, bf16[3,8192,4096]{2,1,0:T(8,128)(2,1)} %refs_2_.17), custom_call_target="tpu_custom_call" | custom-call | flops 137438953472 | bytes 150994944 | tf_op jit(solution)/shard_map/mlp/pallas_call | solution.py:146
  186.5 152.9 %mlp.10 = bf16[1024,4096]{1,0:T(8,128)(2,1)} custom-call(s32[1]{0:T(128)} %constant.13.clone.1.where_ref, bf16[1024,4096]{1,0:T(8,128)(2,1)} %all-gather.23.cloned.1.call-done.refs_0_, bf16[3,4096,8192]{2,1,0:T(8,128)(2,1)} %refs_1_.17, bf16[3,8192,4096]{2,1,0:T(8,128)(2,1)} %refs_2_.17), custom_call_target="tpu_custom_call" | custom-call | flops 137438953472 | bytes 150994944 | tf_op jit(solution)/shard_map/mlp/pallas_call | solution.py:146
  356.1 82.0 %mlp.12 = bf16[1024,2048]{1,0:T(8,128)(2,1)} custom-call(s32[1]{0:T(128)} %constant.13.clone.1.where_ref, bf16[1024,2048]{1,0:T(8,128)(2,1)} %norm.5.refs_0_, bf16[1,2048,8192]{2,1,0:T(8,128)(2,1)} %refs_1_.12, bf16[1,8192,2048]{2,1,0:T(8,128)(2,1)} %refs_2_.12, bf16[1024,2048]{1,0:T(8,128)(2,1)} %bitcast.85), custom_call_target="tpu_custom_call" | custom-call | flops 68719476736 | bytes 75497472 | tf_op jit(solution)/shard_map/mlp/pallas_call | solution.py:146
  438.2 74.3 %all-gather.41.cloned.1.call-done = bf16[8192,2048]{1,0:T(8,128)(2,1)} async-done(((bf16[1024,2048]{1,0:T(8,128)(2,1)}), bf16[8192,2048]{1,0:T(8,128)(2,1)}) %all-gather.41.cloned.1.call-update) | async-done | bytes 33554448 | tf_op jit(solution)/shard_map/all_gather | solution.py:438
  531.5 153.5 %mlp.11 = bf16[1024,4096]{1,0:T(8,128)(2,1)} custom-call(s32[1]{0:T(128)} %constant.13.clone.1.where_ref, bf16[1024,4096]{1,0:T(8,128)(2,1)} %all-gather.25.cloned.1.call-done.refs_0_, bf16[3,4096,8192]{2,1,0:T(8,128)(2,1)} %refs_1_.17, bf16[3,8192,4096]{2,1,0:T(8,128)(2,1)} %refs_2_.17), custom_call_target="tpu_custom_call" | custom-call | flops 137438953472 | bytes 150994944 | tf_op jit(solution)/shard_map/mlp/pallas_call | solution.py:146
  685.8 81.5 %mlp.13 = bf16[512,4096]{1,0:T(8,128)(2,1)} custom-call(s32[1]{0:T(128)} %bitcast.1.where_ref, bf16[1024,4096]{1,0:T(8,128)(2,1)} %all-gather.27.cloned.1.call-done.refs_0_, bf16[3,4096,8192]{2,1,0:T(8,128)(2,1)} %refs_1_.17, bf16[3,8192,4096]{2,1,0:T(8,128)(2,1)} %refs_2_.17), custom_call_target="tpu_custom_call" | custom-call | flops 68719476736 | bytes 142606336 | tf_op jit(solution)/shard_map/mlp/pallas_call | solution.py:146
  775.8 81.9 %mlp.15.refs_0_ = bf16[512,4096]{1,0:T(8,128)(2,1)} custom-call(s32[1]{0:T(128)} %bitcast.4.where_ref, bf16[1024,4096]{1,0:T(8,128)(2,1)} %all-gather.27.cloned.1.call-done.refs_0_, bf16[3,4096,8192]{2,1,0:T(8,128)(2,1)} %refs_1_.17, bf16[3,8192,4096]{2,1,0:T(8,128)(2,1)} %refs_2_.17), custom_call_target="tpu_custom_call" | custom-call | flops 68719476736 | bytes 142606336 | tf_op jit(solution)/shard_map/mlp/pallas_call | solution.py:146
  877.2 153.5 %mlp.14 = bf16[1024,4096]{1,0:T(8,128)(2,1)} custom-call(s32[1]{0:T(128)} %constant.13.clone.1.where_ref, bf16[1024,4096]{1,0:T(8,128)(2,1)} %all-gather.29.cloned.1.call-done.refs_0_, bf16[3,4096,8192]{2,1,0:T(8,128)(2,1)} %refs_1_.17, bf16[3,8192,4096]{2,1,0:T(8,128)(2,1)} %refs_2_.17), custom_call_target="tpu_custom_call" | custom-call | flops 137438953472 | bytes 150994944 | tf_op jit(solution)/shard_map/mlp/pallas_call | solution.py:146
  1030.8 81.5 %mlp.16 = bf16[512,4096]{1,0:T(8,128)(2,1)} custom-call(s32[1]{0:T(128)} %bitcast.1.where_ref, bf16[1024,4096]{1,0:T(8,128)(2,1)} %all-gather.31.cloned.1.call-done.refs_0_, bf16[3,4096,8192]{2,1,0:T(8,128)(2,1)} %refs_1_.17, bf16[3,8192,4096]{2,1,0:T(8,128)(2,1)} %refs_2_.17), custom_call_target="tpu_custom_call" | custom-call | flops 68719476736 | bytes 142606336 | tf_op jit(solution)/shard_map/mlp/pallas_call | solution.py:146
  1133.4 81.6 %mlp.17 = bf16[512,4096]{1,0:T(8,128)(2,1)} custom-call(s32[1]{0:T(128)} %bitcast.4.where_ref, bf16[1024,4096]{1,0:T(8,128)(2,1)} %all-gather.31.cloned.1.call-done.refs_0_, bf16[3,4096,8192]{2,1,0:T(8,128)(2,1)} %refs_1_.17, bf16[3,8192,4096]{2,1,0:T(8,128)(2,1)} %refs_2_.17), custom_call_target="tpu_custom_call" | custom-call | flops 68719476736 | bytes 142606336 | tf_op jit(solution)/shard_map/mlp/pallas_call | solution.py:146
  1404.0 27.1 %proj.2 = (f32[512,2048]{1,0:T(8,128)}, f32[8,2048]{1,0:T(8,128)}) custom-call(s32[1]{0:T(128)} %bitcast.me_ref, bf16[4096,512]{1,0:T(8,128)(2,1)} %constant_dynamic-update-slice_fusion.f_ref, bf16[4096,2048]{1,0:T(8,128)(2,1)} %all-gather.33.cloned.1.call-done.z_ref, bf16[8,1024,2048]{2,1,0:T(8,128)(2,1)} %bitcast.73), custom_call_target="tpu_custom_call" | custom-call | flops 8589934592 | bytes 37748736 | tf_op jit(solution)/shard_map/proj/pallas_call | solution.py:283
  1431.0 29.9 %pre.2 = (bf16[4096,2048]{1,0:T(8,128)(2,1)}, f32[4096,1024]{1,0:T(8,128)}, bf16[4096,1024]{1,0:T(8,128)(2,1)}) custom-call(bf16[8,1024,2048]{2,1,0:T(8,128)(2,1)} %bitcast.77, f32[1,2048]{1,0:T(1,128)} %g_ref.5, bf16[2048,1024]{1,0:T(8,128)(2,1)} %dynamic-slice_bitcast_fusion.w_ref), custom_call_target="tpu_custom_call" | custom-call | flops 17179869184 | bytes 58720256 | tf_op jit(solution)/shard_map/pre/pallas_call | solution.py:223
  1460.9 29.9 %pre.3 = (bf16[4096,2048]{1,0:T(8,128)(2,1)}, f32[4096,1024]{1,0:T(8,128)}, bf16[4096,1024]{1,0:T(8,128)(2,1)}) custom-call(bf16[8,1024,2048]{2,1,0:T(8,128)(2,1)} %bitcast.78, f32[1,2048]{1,0:T(1,128)} %g_ref.5, bf16[2048,1024]{1,0:T(8,128)(2,1)} %dynamic-slice_bitcast_fusion.w_ref), custom_call_target="tpu_custom_call" | custom-call | flops 17179869184 | bytes 58720256 | tf_op jit(solution)/shard_map/pre/pallas_call | solution.py:223
  1490.8 40.2 %down.2 = (bf16[4096,2048]{1,0:T(8,128)(2,1)}, f32[1024,2048]{1,0:T(8,128)}) custom-call(bf16[4096,2048]{1,0:T(8,128)(2,1)} %all-gather.33.cloned.1.call-done.z_ref, bf16[8,1024,2048]{2,1,0:T(8,128)(2,1)} %bitcast.74, bf16[4096,1024]{1,0:T(8,128)(2,1)} %get-tuple-element.74.u_ref), custom_call_target="tpu_custom_call" | custom-call | flops 17179869184 | bytes 58720256 | tf_op jit(solution)/shard_map/down/pallas_call | solution.py:340
  1531.0 27.9 %proj.3 = (bf16[512,2048]{1,0:T(8,128)(2,1)}, f32[8,2048]{1,0:T(8,128)}) custom-call(s32[1]{0:T(128)} %bitcast.me_ref, bf16[4096,512]{1,0:T(8,128)(2,1)} %constant_dynamic-update-slice_fusion.7.f_ref, bf16[4096,2048]{1,0:T(8,128)(2,1)} %all-gather.35.cloned.1.call-done.z_ref, bf16[8,1024,2048]{2,1,0:T(8,128)(2,1)} %bitcast.75, ...), custom_call_target="tpu_custom_call" | custom-call | flops 8589934592 | bytes 37748736 | tf_op jit(solution)/shard_map/proj/pallas_call | solution.py:283
  1558.9 42.9 %down.3 = (bf16[4096,2048]{1,0:T(8,128)(2,1)}, bf16[1024,2048]{1,0:T(8,128)(2,1)}) custom-call(bf16[4096,2048]{1,0:T(8,128)(2,1)} %all-gather.35.cloned.1.call-done.z_ref, bf16[8,1024,2048]{2,1,0:T(8,128)(2,1)} %bitcast.76, bf16[4096,1024]{1,0:T(8,128)(2,1)} %get-tuple-element.73.u_ref, f32[1024,2048]{1,0:T(8,128)} %get-tuple-element.75.refs_0_), custom_call_target="tpu_custom_call" | custom-call | flops 17179869184 | bytes 58720256 | tf_op jit(solution)/shard_map/down/pallas_call | solution.py:340
  1601.9 33.1 %fusion.19 = bf16[4096,1024]{1,0:T(8,128)(2,1)S(1)} fusion(f32[4096,1024]{1,0:T(8,128)} %get-tuple-element.88, bf16[4096,2048]{1,0:T(8,128)(2,1)} %get-tuple-element.87, bf16[1,8192,2048]{2,1,0:T(8,128)(2,1)} %refs_2_.12, s32[]{:T(128)S(6)} %select_n.44), kind=kOutput, calls=%fused_computation.28 | convolution fusion | flops 17263755264 | bytes 46137348 | tf_op jit(solution)/shard_map/dot_general | solution.py:391
  1650.7 33.3 %fusion.12 = bf16[4096,1024]{1,0:T(8,128)(2,1)S(1)} fusion(f32[4096,1024]{1,0:T(8,128)} %get-tuple-element.85, bf16[4096,2048]{1,0:T(8,128)(2,1)} %get-tuple-element.84, bf16[1,8192,2048]{2,1,0:T(8,128)(2,1)} %refs_2_.12, s32[]{:T(128)S(6)} %select_n.44), kind=kOutput, calls=%fused_computation.21 | convolution fusion | flops 17263755264 | bytes 46137348 | tf_op jit(solution)/shard_map/dot_general | solution.py:391
  1746.8 23.7 %fusion.2 = f32[2048]{0:T(1024)S(1)} fusion(bf16[4,1024,1024]{2,1,0:T(8,128)(2,1)} %bitcast.90, f32[4,1024]{1,0:T(4,128)S(1)} %get-tuple-element.117, bf16[4,2,1024,2048]{3,2,1,0:T(8,128)(2,1)} %bitcast.80, bf16[1,2048,8192]{2,1,0:T(8,128)(2,1)} %refs_1_.12, s32[]{:T(128)S(6)} %select_n.44), kind=kOutput, calls=%fused_computation.6 | convolution fusion | flops 17213421568 | bytes 29384708 | tf_op jit(solution)/shard_map/dot_general | solution.py:391
  1770.5 23.7 %fusion.5 = f32[2048]{0:T(1024)S(1)} fusion(bf16[4,1024,1024]{2,1,0:T(8,128)(2,1)} %bitcast.89, f32[4,1024]{1,0:T(4,128)S(1)} %get-tuple-element.116, bf16[4,2,1024,2048]{3,2,1,0:T(8,128)(2,1)} %bitcast.81, bf16[1,2048,8192]{2,1,0:T(8,128)(2,1)} %refs_1_.12, s32[]{:T(128)S(6)} %select_n.44), kind=kOutput, calls=%fused_computation.9 | convolution fusion | flops 17213421568 | bytes 29384708 | tf_op jit(solution)/shard_map/dot_general | solution.py:391
  1794.2 22.8 %psum.7 = f32[2048]{0:T(1024)} all-reduce(f32[2048]{0:T(1024)S(1)} %add.122), channel_id=1, replica_groups=mesh['data'=4,'model'=2] {'data','model'}, use_global_device_ids=true, to_apply=%region_10.0 | all-reduce | flops 2048 | bytes 16384 | tf_op jit(solution)/shard_map/psum | solution.py:502
  1847.3 39.7 %all-gather.45.cloned.1.call-done = bf16[4096,1024]{1,0:T(8,128)(2,1)} async-done(((bf16[512,1024]{1,0:T(8,128)(2,1)}), bf16[4096,1024]{1,0:T(8,128)(2,1)}) %all-gather.45.cloned.1.call-update) | async-done | bytes 8388624 | tf_op jit(solution)/shard_map/all_gather | solution.py:494
  1917.1 126.9 %all-gather.37.cloned.1.call-done = bf16[8192,2048]{1,0:T(8,128)(2,1)} async-done(((bf16[1024,2048]{1,0:T(8,128)(2,1)}), bf16[8192,2048]{1,0:T(8,128)(2,1)}) %all-gather.37.cloned.1.call-update) | async-done | bytes 33554448 | tf_op jit(solution)/shard_map/all_gather | solution.py:480
  2044.0 31.6 %bitcast_convert_fusion = f32[1,8192,2048]{2,1,0:T(8,128)} fusion(bf16[8192,2048]{1,0:T(8,128)(2,1)} %all-gather.37.cloned.1.call-done), kind=kLoop, calls=%fused_computation.10 | loop fusion | flops 16777216 | bytes 100663296 | tf_op jit(solution)/shard_map/broadcast_in_dim | solution.py:509
  (145 shorter events, 438.9 us)
Async XLA Ops:
  14.6 171.9 %all-gather.23.cloned.1.call-start = ((), (), s32[]{:S(2)}) async-start(), calls=%async_computation.6 | async-start | bytes 12582912 | tf_op jit(solution)/shard_map/all_gather | solution.py:430
  20.5 319.5 %reduce-scatter.5.cloned.1.call-start = ((), (), s32[]{:S(2)}) async-start(), calls=%async_computation.5 | async-start | bytes 12582912 | tf_op jit(solution)/shard_map/reduce_scatter | solution.py:442
  186.4 251.7 %reduce-scatter.9.cloned.1.call-start = ((), (), s32[]{:S(2)}) async-start(), calls=%async_computation.9 | async-start | bytes 12582912 | tf_op jit(solution)/shard_map/reduce_scatter | solution.py:445
  339.4 173.1 %all-gather.41.cloned.1.call-start = ((), (), s32[]{:S(2)}) async-start(), calls=%async_computation.18 | async-start | bytes 37748736 | tf_op jit(solution)/shard_map/all_gather | solution.py:438
  340.0 191.5 %all-gather.25.cloned.1.call-start = ((), (), s32[]{:S(2)}) async-start(), calls=%async_computation.7 | async-start | bytes 12582912 | tf_op jit(solution)/shard_map/all_gather | solution.py:430
  348.3 337.5 %all-gather.27.cloned.1.call-start = ((), (), s32[]{:S(2)}) async-start(), calls=%async_computation.10 | async-start | bytes 12582912 | tf_op jit(solution)/shard_map/all_gather | solution.py:430
  520.2 247.2 %reduce-scatter.7.cloned.1.call-start = ((), (), s32[]{:S(2)}) async-start(), calls=%async_computation.8 | async-start | bytes 12582912 | tf_op jit(solution)/shard_map/reduce_scatter | solution.py:442
  685.0 173.2 %all-gather.43.cloned.1.call-start = ((), (), s32[]{:S(2)}) async-start(), calls=%async_computation.19 | async-start | bytes 37748736 | tf_op jit(solution)/shard_map/all_gather | solution.py:440
  685.7 191.5 %all-gather.29.cloned.1.call-start = ((), (), s32[]{:S(2)}) async-start(), calls=%async_computation.11 | async-start | bytes 12582912 | tf_op jit(solution)/shard_map/all_gather | solution.py:430
  775.5 255.2 %all-gather.31.cloned.1.call-start = ((), (), s32[]{:S(2)}) async-start(), calls=%async_computation.13 | async-start | bytes 12582912 | tf_op jit(solution)/shard_map/all_gather | solution.py:430
  775.6 82.1 %collective-permute-start = (bf16[512,4096]{1,0:T(8,128)(2,1)}, bf16[512,4096]{1,0:T(8,128)(2,1)}, u32[]{:S(2)}, u32[]{:S(2)}) collective-permute-start(bf16[512,4096]{1,0:T(8,128)(2,1)} %mlp.13), channel_id=1, source_target_pairs={{0,1},{1,0},{2,3},{3,2},{4,5},{5,4},{6,7},{7,6}} | collective-permute-start | bytes 12582920 | tf_op jit(solution)/shard_map/ppermute | solution.py:383
  868.2 244.0 %reduce-scatter.11.cloned.1.call-start = ((), (), s32[]{:S(2)}) async-start(), calls=%async_computation.12 | async-start | bytes 12582912 | tf_op jit(solution)/shard_map/reduce_scatter | solution.py:442
  1030.7 373.3 %all-gather.33.cloned.1.call-start = ((), (), s32[]{:S(2)}) async-start(), calls=%async_computation.14 | async-start | bytes 18874368 | tf_op jit(solution)/shard_map/all_gather | solution.py:418
  1133.0 398.0 %all-gather.35.cloned.1.call-start = ((), (), s32[]{:S(2)}) async-start(), calls=%async_computation.15 | async-start | bytes 18874368 | tf_op jit(solution)/shard_map/all_gather | solution.py:418
  1133.0 82.0 %collective-permute-start.8 = (bf16[512,4096]{1,0:T(8,128)(2,1)}, bf16[512,4096]{1,0:T(8,128)(2,1)}, u32[]{:S(2)}, u32[]{:S(2)}) collective-permute-start(bf16[512,4096]{1,0:T(8,128)(2,1)} %mlp.16), channel_id=1, source_target_pairs={{0,1},{1,0},{2,3},{3,2},{4,5},{5,4},{6,7},{7,6}} | collective-permute-start | bytes 12582920 | tf_op jit(solution)/shard_map/ppermute | solution.py:383
  1237.8 579.1 %all-gather.39.cloned.1.call-start = ((), (), s32[]{:S(2)}) async-start(), calls=%async_computation.17 | async-start | bytes 18874368 | tf_op jit(solution)/shard_map/all_gather | solution.py:477
  1263.8 65.3 %collective-permute-start.7 = (bf16[512,512]{1,0:T(8,128)(2,1)S(1)}, bf16[512,512]{1,0:T(8,128)(2,1)S(1)}, u32[]{:S(2)}, u32[]{:S(2)}) collective-permute-start(bf16[512,512]{1,0:T(8,128)(2,1)S(1)} %get-tuple-element.103), channel_id=1, source_target_pairs={{0,7},{1,6},{2,5},{3,4},{4,3},{5,2},{6,1},{7,0}} | collective-permute-start | bytes 1572872 | tf_op jit(solution)/shard_map/ppermute | solution.py:383
  1308.5 64.8 %collective-permute-start.11 = (bf16[512,512]{1,0:T(8,128)(2,1)S(1)}, bf16[512,512]{1,0:T(8,128)(2,1)S(1)}, u32[]{:S(2)}, u32[]{:S(2)}) collective-permute-start(bf16[512,512]{1,0:T(8,128)(2,1)S(1)} %get-tuple-element.99), channel_id=1, source_target_pairs={{0,3},{1,2},{2,1},{3,0},{4,7},{5,6},{6,5},{7,4}} | collective-permute-start | bytes 1572872 | tf_op jit(solution)/shard_map/ppermute | solution.py:383
  1309.3 64.8 %collective-permute-start.12 = (bf16[512,512]{1,0:T(8,128)(2,1)S(1)}, bf16[512,512]{1,0:T(8,128)(2,1)S(1)}, u32[]{:S(2)}, u32[]{:S(2)}) collective-permute-start(bf16[512,512]{1,0:T(8,128)(2,1)S(1)} %get-tuple-element.98), channel_id=1, source_target_pairs={{0,4},{1,5},{2,6},{3,7},{4,0},{5,1},{6,2},{7,3}} | collective-permute-start | bytes 1572872 | tf_op jit(solution)/shard_map/ppermute | solution.py:383
  1330.5 61.1 %collective-permute-start.14 = (bf16[512,512]{1,0:T(8,128)(2,1)S(1)}, bf16[512,512]{1,0:T(8,128)(2,1)S(1)}, u32[]{:S(2)}, u32[]{:S(2)}) collective-permute-start(bf16[512,512]{1,0:T(8,128)(2,1)S(1)} %get-tuple-element.96), channel_id=1, source_target_pairs={{0,6},{1,7},{2,4},{3,5},{4,2},{5,3},{6,0},{7,1}} | collective-permute-start | bytes 1572872 | tf_op jit(solution)/shard_map/ppermute | solution.py:383
  1558.9 258.1 %all-gather.49.cloned.1.call-start = ((), (), s32[]{:S(2)}) async-start(), calls=%async_computation.22 | async-start | bytes 18874368 | tf_op jit(solution)/shard_map/all_gather | solution.py:491
  1700.3 136.3 %all-gather.47.cloned.1.call-start = ((), (), s32[]{:S(2)}) async-start(), calls=%async_computation.21 | async-start | bytes 9437184 | tf_op jit(solution)/shard_map/all_gather | solution.py:493
  1726.2 160.8 %all-gather.45.cloned.1.call-start = ((), (), s32[]{:S(2)}) async-start(), calls=%async_computation.20 | async-start | bytes 9437184 | tf_op jit(solution)/shard_map/all_gather | solution.py:494
  1726.8 317.2 %all-gather.37.cloned.1.call-start = ((), (), s32[]{:S(2)}) async-start(), calls=%async_computation.16 | async-start | bytes 37748736 | tf_op jit(solution)/shard_map/all_gather | solution.py:480
  (19 other events, 542.0 us)
Sparse Core Ops, SparseCore 0:
  14.8 19.2 all-gather.20
  36.1 18.2 all-gather.22
  186.6 14.8 reduce-scatter.4
  339.5 14.8 reduce-scatter.8
  356.1 156.3 all-gather.40
  514.4 17.0 all-gather.24
  533.6 18.2 all-gather.26
  685.1 14.8 reduce-scatter.6
  701.8 156.3 all-gather.42
  860.1 17.0 all-gather.28
  878.7 18.2 all-gather.30
  1030.8 14.8 reduce-scatter.10
  1133.1 85.3 all-gather.32
  1237.9 170.4 all-gather.34
  1559.0 84.1 all-gather.38
  1700.5 84.0 all-gather.48
  1786.8 49.8 all-gather.46
  1838.3 48.6 all-gather.44
  1888.9 155.0 all-gather.36

commit v3 on v2

--- a/solution.py
+++ b/solution.py
@@ -200,7 +200,7 @@
     return pl.pallas_call(step_kernel, in_specs=[source] + [spec] * len(delta) + [gain_spec], out_specs=[spec, spec], out_shape=[shape, shape], cost_estimate=cost, name="step", **common)(hidden, *delta, gain)
 
 
-def pre_kernel(sub, s_ref, g_ref, w_ref, a_ref, p_ref, u_ref):
+def pre_kernel(sub, me_ref, s_ref, g_ref, w_ref, a_ref, p_ref, u_ref):
     for r in range(s_ref.shape[0] // sub):
         part = slice(r * sub, (r + 1) * sub)
         state = s_ref[part, :].astype(jnp.float32)
@@ -213,22 +213,24 @@
         u_ref[part, :] = jax.nn.gelu(pre).astype(jnp.bfloat16)
 
 
-def pre_of(states, gain, weights, parity, block=512, sub=256):
+def pre_of(me, states, gain, weights, parity, cols, block=512, sub=256):
     n_seq, seq_len, width = states.shape
-    cols = weights.shape[1]
     half = n_seq // 2
     rows = half * seq_len
     steps = seq_len // block
-    out = lambda w: pl.BlockSpec((block, w), lambda i, j: (i * steps + j, 0))
+    out = lambda w: pl.BlockSpec((block, w), lambda i, j, me: (i * steps + j, 0))
     return pl.pallas_call(
         functools.partial(pre_kernel, sub),
-        grid=(half, steps),
-        in_specs=[
-            pl.BlockSpec((None, block, width), lambda i, j: (2 * i + parity, j, 0)),
-            pl.BlockSpec((1, width), lambda i, j: (0, 0)),
-            pl.BlockSpec((width, cols), lambda i, j: (0, 0)),
-        ],
-        out_specs=[out(width), out(cols), out(cols)],
+        grid_spec=pltpu.PrefetchScalarGridSpec(
+            num_scalar_prefetch=1,
+            grid=(half, steps),
+            in_specs=[
+                pl.BlockSpec((None, block, width), lambda i, j, me: (2 * i + parity, j, 0)),
+                pl.BlockSpec((1, width), lambda i, j, me: (0, 0)),
+                pl.BlockSpec((None, width, cols), lambda i, j, me: (0, 0, me[0])),
+            ],
+            out_specs=[out(width), out(cols), out(cols)],
+        ),
         out_shape=[
             jax.ShapeDtypeStruct((rows, width), jnp.bfloat16),
             jax.ShapeDtypeStruct((rows, cols), jnp.float32),
@@ -237,17 +239,73 @@
         compiler_params=pltpu.CompilerParams(vmem_limit_bytes=VMEM_CAP),
         cost_estimate=pl.CostEstimate(flops=2 * rows * width * cols, bytes_accessed=rows * (4 * width + 6 * cols), transcendentals=rows * cols),
         name="pre",
-    )(states, gain, weights)
-
-
-def proj_kernel(scale, first, last, me_ref, f_ref, z_ref, s_ref, *refs):
-    state = s_ref[...].astype(jnp.float32)
+    )(me.reshape(1), states, gain, weights)
+
+
+def errors_at(z_ref, s_ref, part):
+    state = s_ref[part, :].astype(jnp.float32)
     inv = lax.rsqrt(jnp.mean(state * state, axis=-1, keepdims=True) + EPS)
-    error = z_ref[...].astype(jnp.float32) - state * inv
-    rows, width = error.shape
-    out_ref, sq_ref = refs[-3:-1]
-    total = refs[-1]
+    unit = state * inv
+    return z_ref[part, :].astype(jnp.float32) - unit, unit, inv
+
+
+def finish_kernel(count, me_ref, h_ref, *refs):
+    parts = refs[:count]
+    q_ref, f_ref, z_ref, acc = refs[count:]
     k = pl.program_id(0)
+    delta = parts[0][...].astype(jnp.float32)
+    if count > 1:
+        delta = (delta + parts[1][...].astype(jnp.float32)).astype(jnp.bfloat16).astype(jnp.float32)
+    feat = (h_ref[...].astype(jnp.float32) + delta).astype(jnp.bfloat16)
+    f_ref[...] = feat
+    term = jnp.dot(feat, q_ref[...], preferred_element_type=jnp.float32)
+
+    @pl.when(k == 0)
+    def _():
+        acc[...] = term
+
+    @pl.when((k > 0) & (k < pl.num_programs(0) - 1))
+    def _():
+        acc[...] += term
+
+    @pl.when(k == pl.num_programs(0) - 1)
+    def _():
+        z_ref[...] = (acc[...] + term).astype(jnp.bfloat16)
+
+
+def finish_part(me, hidden, delta, proj, size):
+    rows, width = hidden.shape
+    cols = width // size
+    out = proj.shape[2]
+    spec = pl.BlockSpec((rows, cols), lambda k, me: (0, k))
+    return pl.pallas_call(
+        functools.partial(finish_kernel, len(delta)),
+        grid_spec=pltpu.PrefetchScalarGridSpec(
+            num_scalar_prefetch=1,
+            grid=(size,),
+            in_specs=[spec] * (1 + len(delta)) + [pl.BlockSpec((None, cols, out), lambda k, me: (0, k, 0))],
+            out_specs=[
+                pl.BlockSpec((None, rows, cols), lambda k, me: (me[0] ^ k, 0, 0)),
+                pl.BlockSpec((rows, out), lambda k, me: (0, 0)),
+            ],
+            scratch_shapes=[pltpu.VMEM((rows, out), jnp.float32)],
+        ),
+        out_shape=[
+            jax.ShapeDtypeStruct((size, rows, cols), jnp.bfloat16),
+            jax.ShapeDtypeStruct((rows, out), jnp.bfloat16),
+        ],
+        compiler_params=pltpu.CompilerParams(vmem_limit_bytes=VMEM_CAP),
+        cost_estimate=pl.CostEstimate(flops=2 * rows * width * out, bytes_accessed=2 * width * (4 * rows + out), transcendentals=0),
+        name="finish",
+    )(me.reshape(1), hidden, *delta, proj)
+
+
+def proj_kernel(scale, first, last, count, chunk, me_ref, *refs):
+    pieces = refs[:count]
+    z_ref, s_ref = refs[count : count + 2]
+    out_ref, sq_ref, total, feat, error_buf = refs[-5:]
+    k = pl.program_id(0)
+    rows, width = z_ref.shape
 
     @pl.when(k == 0)
     def _():
@@ -255,39 +313,51 @@
         if first:
             total[...] = jnp.zeros_like(total)
         else:
-            total[...] = refs[0][...]
-
-    sq_ref[...] += jnp.sum((error * error).reshape(rows // 8, 8, width), axis=0)
-    total[...] += lax.dot_general(f_ref[...], error.astype(jnp.bfloat16), (((0,), (0,)), ((), ())), preferred_element_type=jnp.float32)
+            total[...] = refs[count + 2][...]
+
+    for i in range(count):
+
+        @pl.when(k == i)
+        def _():
+            feat[...] = pieces[i][...]
+
+    for r in range(rows // chunk):
+        part = slice(r * chunk, (r + 1) * chunk)
+        error = errors_at(z_ref, s_ref, part)[0]
+        error_buf[part, :] = error.astype(jnp.bfloat16)
+        sq_ref[...] += jnp.sum((error * error).reshape(chunk // 8, 8, width), axis=0)
+    total[...] += lax.dot_general(feat[...], error_buf[...], (((0,), (0,)), ((), ())), preferred_element_type=jnp.float32)
 
     @pl.when(k == pl.num_programs(0) - 1)
     def _():
         out_ref[...] = (scale * total[...]).astype(jnp.bfloat16) if last else total[...]
 
 
-def proj_part(me, feat, targets, states, parity, scale, total, last):
+def proj_part(me, pieces, targets, states, parity, scale, total, last, chunk=16):
     n_seq, _, width = states.shape
     size = n_seq
-    cols = feat.shape[1]
-    rows = feat.shape[0] // size
+    rows, cols = pieces[0].shape
     whole = pl.BlockSpec((cols, width), lambda k, me: (0, 0))
-    in_specs = [
-        pl.BlockSpec((rows, cols), lambda k, me: (k, 0)),
+    in_specs = [pl.BlockSpec((rows, cols), lambda k, me: (0, 0))] * size + [
         pl.BlockSpec((rows, width), lambda k, me: (me[0] ^ k, 0)),
         pl.BlockSpec((None, rows, width), lambda k, me: (2 * ((me[0] ^ k) // 2) + parity, (me[0] ^ k) % 2, 0)),
     ]
-    args = [me.reshape(1), feat, targets, states]
+    args = [me.reshape(1), *pieces, targets, states]
     if total is not None:
         in_specs.append(whole)
         args.append(total)
     return pl.pallas_call(
-        functools.partial(proj_kernel, scale, total is None, last),
+        functools.partial(proj_kernel, scale, total is None, last, size, chunk),
         grid_spec=pltpu.PrefetchScalarGridSpec(
             num_scalar_prefetch=1,
             grid=(size,),
             in_specs=in_specs,
             out_specs=[whole, pl.BlockSpec((8, width), lambda k, me: (0, 0))],
-            scratch_shapes=[pltpu.VMEM((cols, width), jnp.float32)],
+            scratch_shapes=[
+                pltpu.VMEM((cols, width), jnp.float32),
+                pltpu.VMEM((rows, cols), jnp.bfloat16),
+                pltpu.VMEM((rows, width), jnp.bfloat16),
+            ],
         ),
         out_shape=[
             jax.ShapeDtypeStruct((cols, width), jnp.bfloat16 if last else jnp.float32),
@@ -299,32 +369,38 @@
     )(*args)
 
 
-def down_kernel(scale, first, z_ref, s_ref, u_ref, *refs):
-    d_ref, out_ref, total = refs[-3:]
+def down_kernel(scale, first, chunk, cuts, z_ref, s_ref, u_ref, *refs):
+    d_ref, out_ref, total, z_scale, s_scale = refs[-5:]
     k = pl.program_id(0) * pl.num_programs(1) + pl.program_id(1)
 
     @pl.when(k == 0)
     def _():
         total[...] = jnp.zeros_like(total) if first else refs[0][...]
 
-    state = s_ref[...].astype(jnp.float32)
-    inv = lax.rsqrt(jnp.mean(state * state, axis=-1, keepdims=True) + EPS)
-    unit = state * inv
-    error = z_ref[...].astype(jnp.float32) - unit
-    lean = jnp.mean(error * unit, axis=-1, keepdims=True)
-    d_out = ((error - unit * lean) * (-scale * inv)).astype(jnp.bfloat16)
-    d_ref[...] = d_out
+    width = z_ref.shape[1]
+    for r in range(z_ref.shape[0] // chunk):
+        part = slice(r * chunk, (r + 1) * chunk)
+        state = s_ref[part, :].astype(jnp.float32)
+        square = jnp.sum(state * state, axis=-1, keepdims=True) / width
+        cross = jnp.sum(state * z_ref[part, :].astype(jnp.float32), axis=-1, keepdims=True) / width
+        inv = lax.rsqrt(square + EPS)
+        lean = inv * cross - inv * inv * square
+        z_scale[part, :] = jnp.broadcast_to(-scale * inv, (chunk, 128))
+        s_scale[part, :] = jnp.broadcast_to(scale * inv * inv * (1.0 + lean), (chunk, 128))
+    for r in range(z_ref.shape[0] // chunk):
+        part = slice(r * chunk, (r + 1) * chunk)
+        d_ref[part, :] = (s_ref[part, :].astype(jnp.float32) * s_scale[part, :1] + z_ref[part, :].astype(jnp.float32) * z_scale[part, :1]).astype(jnp.bfloat16)
     cols = total.shape[0]
-    for h in range(4):
-        part = slice(h * cols // 4, (h + 1) * cols // 4)
-        total[part, :] += lax.dot_general(u_ref[:, part], d_out, (((0,), (0,)), ((), ())), preferred_element_type=jnp.float32)
+    for h in range(cuts):
+        part = slice(h * cols // cuts, (h + 1) * cols // cuts)
+        total[part, :] += lax.dot_general(u_ref[:, part], d_ref[...], (((0,), (0,)), ((), ())), preferred_element_type=jnp.float32)
 
     @pl.when(k == pl.num_programs(0) * pl.num_programs(1) - 1)
     def _():
         out_ref[...] = total[...].astype(out_ref.dtype)
 
 
-def down_part_of(ups, targets, states, parity, scale, total, last, block=512):
+def down_part_of(ups, targets, states, parity, scale, total, last, block=512, chunk=16, cuts=1):
     n_seq, seq_len, width = states.shape
     half = n_seq // 2
     cols = ups.shape[1]
@@ -338,7 +414,7 @@
         in_specs.append(whole)
         args.append(total)
     return pl.pallas_call(
-        functools.partial(down_kernel, scale, total is None),
+        functools.partial(down_kernel, scale, total is None, chunk, cuts),
         grid=(half, steps),
         in_specs=in_specs,
         out_specs=[spec(width), whole],
@@ -346,7 +422,7 @@
             jax.ShapeDtypeStruct((rows, width), jnp.bfloat16),
             jax.ShapeDtypeStruct((cols, width), jnp.bfloat16 if last else jnp.float32),
         ],
-        scratch_shapes=[pltpu.VMEM((cols, width), jnp.float32)],
+        scratch_shapes=[pltpu.VMEM((cols, width), jnp.float32), pltpu.VMEM((block, 128), jnp.float32), pltpu.VMEM((block, 128), jnp.float32)],
         compiler_params=pltpu.CompilerParams(vmem_limit_bytes=VMEM_CAP),
         cost_estimate=pl.CostEstimate(flops=2 * rows * width * cols, bytes_accessed=rows * (6 * width + 2 * cols), transcendentals=0),
         name="down",
@@ -397,14 +473,12 @@
     def step(teacher_in, student_in, teacher_gain, teacher_up_w, teacher_down, student_gain, student_up, student_down, student_proj):
         me = lax.axis_index("data") * 2 + lax.axis_index("model")
         n_layers = teacher_up_w.shape[0]
-        t_width = teacher_in.shape[2]
         _, seq_len, s_width = student_in.shape
         s_hidden = student_up.shape[2]
         part = s_hidden // size
-        t_part = t_width // size
         total = size * seq_len * s_width
         grad_scale = 2.0 / total
-        v_up, v_down, q_proj = student_up[0], student_down[0], student_proj[0]
+        v_up, v_down = student_up[0], student_down[0]
 
         own = student_in[0]
         side = lax.axis_index("model")
@@ -412,18 +486,10 @@
         hidden = [teacher_in, teacher_in]
 
         def finish(c, delta):
-            total = sum(part.astype(jnp.float32) for part in delta).astype(jnp.bfloat16)
-            hidden[c] = (hidden[c].astype(jnp.float32) + total.astype(jnp.float32)).astype(jnp.bfloat16)
-            target = dot(hidden[c], q_proj, ((1,), (0,))).astype(jnp.bfloat16)
-            return target, lax.all_gather(target, AXES, axis=0, tiled=True)
-
-        def columns(c):
-            rows = hidden[c].shape[0]
-            pieces = []
-            for bits in range(size):
-                piece = lax.dynamic_slice(hidden[c], (0, (me ^ bits) * t_part), (rows, t_part))
-                pieces.append(flip(piece, bits, size) if bits else piece)
-            return jnp.concatenate(pieces, axis=0)
+            feats, target = finish_part(me, hidden[c], delta, student_proj, size)
+            targets = lax.all_gather(target, AXES, axis=0, tiled=True)
+            pieces = [flip(feats[bits], bits, size) if bits else feats[0] for bits in range(size)]
+            return target, targets, pieces
 
         def normed(c, delta, layer):
             hidden[c], act = teacher_norm(hidden[c], delta, teacher_gain, layer, c)
@@ -455,24 +521,20 @@
                 if layer < last:
                     ready, acts[0] = normed(0, delta_0, layer + 1)
                 else:
-                    ready, targets_0 = finish(0, delta_0)
-                    feat_0 = columns(0)
+                    ready, targets_0, feat_0 = finish(0, delta_0)
                 partial = teach(after(acts[1], ready), layer, rows=rows, where=side)
                 delta_1 = (partial, moved)
             if layer < last:
                 if layer == 1:
                     delta_1 = after(delta_1, all_out)
                 acts[1] = normed(1, delta_1, layer + 1)[1]
-        target_1, targets_1 = finish(1, delta_1)
-        feat_1 = columns(1)
+        target_1, targets_1, feat_1 = finish(1, delta_1)
 
         all_in, all_out, targets_0 = after((all_in, all_out, targets_0), target_1)
-        up_part = lax.dynamic_slice(v_up, (0, me * part), (s_width, part))
-        down_part = lax.dynamic_slice(v_down, (me * part, 0), (part, s_width))
         proj_sum, square_0 = proj_part(me, feat_0, targets_0, all_out, 0, grad_scale, None, False)
-        acts, pre, ups = zip(*[pre_of(all_in, student_gain, up_part, c) for c in range(2)])
-        d_out_0, down_sum = down_part_of(ups[0], targets_0, all_out, 0, grad_scale, None, False)
-        targets_1 = after(targets_1, (proj_sum, ups[1], down_sum))
+        acts, pre, ups = zip(*[pre_of(me, all_in, student_gain, student_up, c, part) for c in range(2)])
+        d_out_0, down_sum = down_part_of(ups[0], after(targets_0, (proj_sum, ups[1])), all_out, 0, grad_scale, None, False)
+        targets_1 = after(targets_1, down_sum)
         proj_piece, square_1 = proj_part(me, feat_1, targets_1, all_out, 1, grad_scale, proj_sum, True)
         proj_all = lax.all_gather(proj_piece, AXES, axis=0, tiled=True)
         loss = (jnp.sum(square_0) + jnp.sum(square_1)) / total
@@ -480,18 +542,19 @@
         down_all = lax.all_gather(down_piece, AXES, axis=0, tiled=True)
 
         d_outs = after((d_out_0, d_out_1), down_piece)
+        up_part = lax.dynamic_slice(after(v_up, proj_piece), (0, me * part), (s_width, part))
+        down_part = lax.dynamic_slice(after(v_down, proj_piece), (me * part, 0), (part, s_width))
         d_pres = [gelu_back(pre[c], dot(d_outs[c], down_part, ((1,), (1,)))).astype(jnp.bfloat16) for c in range(2)]
 
         def up_rows(first, count):
             cols = slice(first, first + count)
             return (dot(acts[0][:, cols], d_pres[0], ((0,), (0,))) + dot(acts[1][:, cols], d_pres[1], ((0,), (0,)))).astype(jnp.bfloat16)
 
-        half = s_width // 2
-        up_piece = up_rows(0, half)
-        up_all_0 = lax.all_gather(up_piece, AXES, axis=0, tiled=False)
-        up_piece = up_rows(half, half)
-        up_all_1 = lax.all_gather(up_piece[: half // 2], AXES, axis=0, tiled=False)
-        up_all_2 = lax.all_gather(up_piece[half // 2 :], AXES, axis=0, tiled=False)
+        most = s_width * 3 // 4
+        up_piece_0 = up_rows(0, most)
+        up_all_0 = lax.all_gather(up_piece_0, AXES, axis=0, tiled=False)
+        up_piece = up_rows(most, s_width - most)
+        up_all_1 = lax.all_gather(up_piece, AXES, axis=0, tiled=False)
 
         d_pres = after(d_pres, up_piece)
         gain_sum = jnp.zeros((s_width,), jnp.float32)
@@ -504,8 +567,7 @@
         grad_down = after(down_all, grad_gain).astype(jnp.float32)
         shape = (s_width, s_hidden)
         grad_up = spread(None, up_all_0, 0, shape)
-        grad_up = spread(grad_up, up_all_1, half, shape)
-        grad_up = spread(grad_up, up_all_2, half + half // 2, shape)
+        grad_up = spread(grad_up, up_all_1, most, shape)
         return (loss, grad_up[None], grad_down[None], grad_gain[None], grad_proj[None])
 
     return jax.shard_map(

time: 2100 us -> 1970 us (0.938)
  waiting for transfers between devices: 399 us -> 271 us
  Pallas kernels: 1310 us -> 1350 us
  matrix products: 194 us -> 171 us
    ppermute x16, waiting for transfers between devices: 120 us -> 0.04 us  [flip(): return lax.ppermute(value, AXES, [(i, i ^ bits) for i in range(size)])]
    pallas_call x6 -> x8, Pallas kernels: 198 us -> 221 us  [the longest x2 74.7 us: down_part_of(): pl.pallas_call(functools.partial(down_kernel, scale, total is None, chunk...]
    dot_general x10 -> x8, matrix products: 194 us -> 171 us  [dot(): lax.dot_general(a, b, (dims, ((), ())), preferred_element_type=jnp.float32)]
    convert_element_type x2 -> x1, other arithmetic: 12.4 us -> 34.4 us  [step(): seqs[:, c].astype(jnp.float32)]
  transfers between devices with their start and end apart: 35 -> 34, of which waited for: 16 -> 7; matrix products, arithmetic and copies ran while one was open for 12% -> 13% of each run, Pallas kernels for 61% -> 66%
where the time goes in v3:
time: 1970 us; the launch traced here: 1960 us
  Pallas kernels  1350 us (69%)
  waiting for transfers between devices  271 us (14%)
  matrix products  171 us (9%)
  other arithmetic  100 us (5%)
  blocking collectives  23.6 us (1%)
    pallas_call x9, Pallas kernels, mlp(): pl.pallas_call(functools.partial(mlp_kernel, layer, steps, wide, state is...  1030 us
    dot_general x8, matrix products, dot(): lax.dot_general(a, b, (dims, ((), ())), preferred_element_type=jnp.float32)  171 us
    all_gather x1, waiting for transfers between devices, step(): down_all = lax.all_gather(down_piece, AXES, axis=0, tiled=True)  128 us
    pallas_call x2, Pallas kernels, down_part_of(): pl.pallas_call(functools.partial(down_kernel, scale, total is None, chunk...  74.7 us
    all_gather x1, waiting for transfers between devices, step(): all_in = lax.all_gather(after(own, acts[0]), AXES, axis=0, tiled=False)  74.3 us
    pallas_call x2, Pallas kernels, pre_of(): pl.pallas_call(functools.partial(pre_kernel, sub), grid_spec=pltpu.Prefet...  61.2 us
    pallas_call x2, Pallas kernels, proj_part(): pl.pallas_call(functools.partial(proj_kernel, scale, total is None, last,...  47.1 us
  transfers between devices with their start and end apart: 34, of which 7 were waited for; matrix products, arithmetic and copies ran while one was open for 13% of the time, Pallas kernels for 66%

profile of v3, /device:TPU:1, one launch (start us, length us, event | category | flops | bytes accessed | tf_op | source)
XLA Modules:
  0.0 1957.1 jit_solution(7793105578910417177)
XLA Ops:
  34.1 152.3 %mlp.9 = bf16[1024,4096]{1,0:T(8,128)(2,1)} custom-call(s32[1]{0:T(128)} %constant.11.clone.1.where_ref, bf16[1024,4096]{1,0:T(8,128)(2,1)} %all-gather.19.cloned.1.call-done.refs_0_, bf16[3,4096,8192]{2,1,0:T(8,128)(2,1)} %refs_1_.19, bf16[3,8192,4096]{2,1,0:T(8,128)(2,1)} %refs_2_.18), custom_call_target="tpu_custom_call" | custom-call | flops 137438953472 | bytes 150994944 | tf_op jit(solution)/shard_map/mlp/pallas_call | solution.py:146
  186.5 165.0 %mlp.10 = bf16[1024,4096]{1,0:T(8,128)(2,1)} custom-call(s32[1]{0:T(128)} %constant.11.clone.1.where_ref, bf16[1024,4096]{1,0:T(8,128)(2,1)} %all-gather.21.cloned.1.call-done.refs_0_, bf16[3,4096,8192]{2,1,0:T(8,128)(2,1)} %refs_1_.19, bf16[3,8192,4096]{2,1,0:T(8,128)(2,1)} %refs_2_.18), custom_call_target="tpu_custom_call" | custom-call | flops 137438953472 | bytes 150994944 | tf_op jit(solution)/shard_map/mlp/pallas_call | solution.py:146
  368.2 82.1 %mlp.12 = bf16[1024,2048]{1,0:T(8,128)(2,1)} custom-call(s32[1]{0:T(128)} %constant.11.clone.1.where_ref, bf16[1024,2048]{1,0:T(8,128)(2,1)} %norm.5.refs_0_, bf16[1,2048,8192]{2,1,0:T(8,128)(2,1)} %w_ref.3, bf16[1,8192,2048]{2,1,0:T(8,128)(2,1)} %refs_2_.13, bf16[1024,2048]{1,0:T(8,128)(2,1)} %bitcast.94), custom_call_target="tpu_custom_call" | custom-call | flops 68719476736 | bytes 75497472 | tf_op jit(solution)/shard_map/mlp/pallas_call | solution.py:146
  450.3 74.3 %all-gather.39.cloned.1.call-done = bf16[8192,2048]{1,0:T(8,128)(2,1)} async-done(((bf16[1024,2048]{1,0:T(8,128)(2,1)}), bf16[8192,2048]{1,0:T(8,128)(2,1)}) %all-gather.39.cloned.1.call-update) | async-done | bytes 33554448 | tf_op jit(solution)/shard_map/all_gather | solution.py:504
  543.6 153.5 %mlp.11 = bf16[1024,4096]{1,0:T(8,128)(2,1)} custom-call(s32[1]{0:T(128)} %constant.11.clone.1.where_ref, bf16[1024,4096]{1,0:T(8,128)(2,1)} %all-gather.23.cloned.1.call-done.refs_0_, bf16[3,4096,8192]{2,1,0:T(8,128)(2,1)} %refs_1_.19, bf16[3,8192,4096]{2,1,0:T(8,128)(2,1)} %refs_2_.18), custom_call_target="tpu_custom_call" | custom-call | flops 137438953472 | bytes 150994944 | tf_op jit(solution)/shard_map/mlp/pallas_call | solution.py:146
  697.9 81.5 %mlp.13 = bf16[512,4096]{1,0:T(8,128)(2,1)} custom-call(s32[1]{0:T(128)} %bitcast.1.where_ref, bf16[1024,4096]{1,0:T(8,128)(2,1)} %all-gather.25.cloned.1.call-done.refs_0_, bf16[3,4096,8192]{2,1,0:T(8,128)(2,1)} %refs_1_.19, bf16[3,8192,4096]{2,1,0:T(8,128)(2,1)} %refs_2_.18), custom_call_target="tpu_custom_call" | custom-call | flops 68719476736 | bytes 142606336 | tf_op jit(solution)/shard_map/mlp/pallas_call | solution.py:146
  787.9 81.7 %mlp.15.refs_0_ = bf16[512,4096]{1,0:T(8,128)(2,1)} custom-call(s32[1]{0:T(128)} %bitcast.4.where_ref, bf16[1024,4096]{1,0:T(8,128)(2,1)} %all-gather.25.cloned.1.call-done.refs_0_, bf16[3,4096,8192]{2,1,0:T(8,128)(2,1)} %refs_1_.19, bf16[3,8192,4096]{2,1,0:T(8,128)(2,1)} %refs_2_.18), custom_call_target="tpu_custom_call" | custom-call | flops 68719476736 | bytes 142606336 | tf_op jit(solution)/shard_map/mlp/pallas_call | solution.py:146
  889.3 153.5 %mlp.14 = bf16[1024,4096]{1,0:T(8,128)(2,1)} custom-call(s32[1]{0:T(128)} %constant.11.clone.1.where_ref, bf16[1024,4096]{1,0:T(8,128)(2,1)} %all-gather.27.cloned.1.call-done.refs_0_, bf16[3,4096,8192]{2,1,0:T(8,128)(2,1)} %refs_1_.19, bf16[3,8192,4096]{2,1,0:T(8,128)(2,1)} %refs_2_.18), custom_call_target="tpu_custom_call" | custom-call | flops 137438953472 | bytes 150994944 | tf_op jit(solution)/shard_map/mlp/pallas_call | solution.py:146
  1042.9 81.5 %mlp.16 = bf16[512,4096]{1,0:T(8,128)(2,1)} custom-call(s32[1]{0:T(128)} %bitcast.1.where_ref, bf16[1024,4096]{1,0:T(8,128)(2,1)} %all-gather.29.cloned.1.call-done.refs_0_, bf16[3,4096,8192]{2,1,0:T(8,128)(2,1)} %refs_1_.19, bf16[3,8192,4096]{2,1,0:T(8,128)(2,1)} %refs_2_.18), custom_call_target="tpu_custom_call" | custom-call | flops 68719476736 | bytes 142606336 | tf_op jit(solution)/shard_map/mlp/pallas_call | solution.py:146
  1143.3 81.5 %mlp.17.refs_0_ = bf16[512,4096]{1,0:T(8,128)(2,1)} custom-call(s32[1]{0:T(128)} %bitcast.4.where_ref, bf16[1024,4096]{1,0:T(8,128)(2,1)} %all-gather.29.cloned.1.call-done.refs_0_, bf16[3,4096,8192]{2,1,0:T(8,128)(2,1)} %refs_1_.19, bf16[3,8192,4096]{2,1,0:T(8,128)(2,1)} %refs_2_.18), custom_call_target="tpu_custom_call" | custom-call | flops 68719476736 | bytes 142606336 | tf_op jit(solution)/shard_map/mlp/pallas_call | solution.py:146
  1257.4 30.6 %pre.2 = (bf16[4096,2048]{1,0:T(8,128)(2,1)}, f32[4096,1024]{1,0:T(8,128)}, bf16[4096,1024]{1,0:T(8,128)(2,1)}) custom-call(s32[1]{0:T(128)} %bitcast.me_ref, bf16[8,1024,2048]{2,1,0:T(8,128)(2,1)} %bitcast.81, f32[1,2048]{1,0:T(1,128)} %g_ref.5, bf16[1,2048,8192]{2,1,0:T(8,128)(2,1)} %w_ref.3), custom_call_target="tpu_custom_call" | custom-call | flops 17179869184 | bytes 58720256 | tf_op jit(solution)/shard_map/pre/pallas_call | solution.py:222
  1290.6 30.6 %pre.3 = (bf16[4096,2048]{1,0:T(8,128)(2,1)}, f32[4096,1024]{1,0:T(8,128)}, bf16[4096,1024]{1,0:T(8,128)(2,1)}) custom-call(s32[1]{0:T(128)} %bitcast.me_ref, bf16[8,1024,2048]{2,1,0:T(8,128)(2,1)} %bitcast.82, f32[1,2048]{1,0:T(1,128)} %g_ref.5, bf16[1,2048,8192]{2,1,0:T(8,128)(2,1)} %w_ref.3), custom_call_target="tpu_custom_call" | custom-call | flops 17179869184 | bytes 58720256 | tf_op jit(solution)/shard_map/pre/pallas_call | solution.py:222
  1325.1 24.2 %proj.2 = (f32[512,2048]{1,0:T(8,128)}, f32[8,2048]{1,0:T(8,128)}) custom-call(s32[1]{0:T(128)} %bitcast.me_ref, bf16[512,512]{1,0:T(8,128)(2,1)} %get-tuple-element.126.refs_0_, bf16[512,512]{1,0:T(8,128)(2,1)} %collective-permute-done.1.refs_1_, bf16[512,512]{1,0:T(8,128)(2,1)} %collective-permute-done.2.refs_2_, ...), custom_call_target="tpu_custom_call" | custom-call | flops 8589934592 | bytes 37748736 | tf_op jit(solution)/shard_map/proj/pallas_call | solution.py:349
  1352.1 35.5 %down.2 = (bf16[4096,2048]{1,0:T(8,128)(2,1)}, f32[1024,2048]{1,0:T(8,128)}) custom-call(bf16[4096,2048]{1,0:T(8,128)(2,1)} %all-gather.31.cloned.1.call-done.refs_8_.z_ref, bf16[8,1024,2048]{2,1,0:T(8,128)(2,1)} %bitcast.86, bf16[4096,1024]{1,0:T(8,128)(2,1)} %get-tuple-element.86.u_ref), custom_call_target="tpu_custom_call" | custom-call | flops 17179869184 | bytes 58720256 | tf_op jit(solution)/shard_map/down/pallas_call | solution.py:416
  1387.5 31.3 %all-gather.33.cloned.1.call-done.refs_8_.z_ref = bf16[4096,2048]{1,0:T(8,128)(2,1)} async-done(((bf16[512,2048]{1,0:T(8,128)(2,1)}), bf16[4096,2048]{1,0:T(8,128)(2,1)}) %all-gather.33.cloned.1.call-update) | async-done | bytes 16777232 | tf_op jit(solution)/shard_map/all_gather | solution.py:490
  1441.8 39.2 %down.3 = (bf16[4096,2048]{1,0:T(8,128)(2,1)}, bf16[1024,2048]{1,0:T(8,128)(2,1)}) custom-call(bf16[4096,2048]{1,0:T(8,128)(2,1)} %all-gather.33.cloned.1.call-done.refs_8_.z_ref, bf16[8,1024,2048]{2,1,0:T(8,128)(2,1)} %bitcast.88, bf16[4096,1024]{1,0:T(8,128)(2,1)} %get-tuple-element.84.u_ref, f32[1024,2048]{1,0:T(8,128)} %get-tuple-element.87.refs_0_), custom_call_target="tpu_custom_call" | custom-call | flops 17179869184 | bytes 58720256 | tf_op jit(solution)/shard_map/down/pallas_call | solution.py:416
  1481.0 33.2 %fusion.17 = bf16[4096,1024]{1,0:T(8,128)(2,1)S(1)} fusion(f32[4096,1024]{1,0:T(8,128)} %get-tuple-element.101, bf16[4096,2048]{1,0:T(8,128)(2,1)} %get-tuple-element.100, bf16[8192,2048]{1,0:T(8,128)(2,1)} %bitcast.99, s32[]{:T(128)S(6)} %select_n.4), kind=kOutput, calls=%fused_computation.26 | convolution fusion | flops 17263755264 | bytes 46137348 | tf_op jit(solution)/shard_map/dot_general | solution.py:467
  1534.5 33.3 %fusion.10 = bf16[4096,1024]{1,0:T(8,128)(2,1)S(1)} fusion(f32[4096,1024]{1,0:T(8,128)} %get-tuple-element.98, bf16[4096,2048]{1,0:T(8,128)(2,1)} %get-tuple-element.96, bf16[8192,2048]{1,0:T(8,128)(2,1)} %bitcast.100, s32[]{:T(128)S(6)} %select_n.4), kind=kOutput, calls=%fused_computation.19 | convolution fusion | flops 17263755264 | bytes 46137348 | tf_op jit(solution)/shard_map/dot_general | solution.py:467
  1621.5 34.4 %slice_convert_fusion = (f32[4,1,1024,2048]{3,2,1,0:T(8,128)}, f32[4,1,1024,2048]{3,2,1,0:T(8,128)}) fusion(bf16[4,2,1024,2048]{3,2,1,0:T(8,128)(2,1)} %bitcast.84), kind=kLoop, calls=%fused_computation.27 | loop fusion | flops 16777216 | bytes 100663296 | tf_op jit(solution)/shard_map/convert_element_type | solution.py:564
  1657.8 24.7 %fusion.3 = f32[2048]{0:T(1024)S(1)} fusion(f32[4,1,1024,2048]{3,2,1,0:T(8,128)} %get-tuple-element.110, bf16[4096,1024]{1,0:T(8,128)(2,1)} %copy-done.2, f32[4096]{0:T(1024)S(1)} %bitcast.97, bf16[2048,8192]{1,0:T(8,128)(2,1)} %bitcast.89, s32[]{:T(128)S(6)} %select_n.4), kind=kOutput, calls=%fused_computation.6 | convolution fusion | flops 17205032960 | bytes 46161924 | tf_op jit(solution)/shard_map/dot_general | solution.py:467
  1682.5 24.9 %fusion.1 = f32[2048]{0:T(1024)S(1)} fusion(f32[4,1,1024,2048]{3,2,1,0:T(8,128)} %get-tuple-element.109, bf16[4096,1024]{1,0:T(8,128)(2,1)} %copy-done.4, f32[4096]{0:T(1024)S(1)} %bitcast.96, bf16[2048,8192]{1,0:T(8,128)(2,1)} %bitcast.90, s32[]{:T(128)S(6)} %select_n.4), kind=kOutput, calls=%fused_computation.3 | convolution fusion | flops 17205032960 | bytes 46161924 | tf_op jit(solution)/shard_map/dot_general | solution.py:467
  1749.9 28.5 %spread.2.rest_0_ = f32[2048,8192]{1,0:T(8,128)} custom-call(bf16[8,1536,1024]{2,1,0:T(8,128)(2,1)} %bitcast.91), custom_call_target="tpu_custom_call" | custom-call | flops 12582912 | bytes 75497472 | tf_op jit(solution)/shard_map/spread/pallas_call | solution.py:445
  1788.7 128.4 %all-gather.35.cloned.1.call-done = bf16[8192,2048]{1,0:T(8,128)(2,1)} async-done(((bf16[1024,2048]{1,0:T(8,128)(2,1)}), bf16[8192,2048]{1,0:T(8,128)(2,1)}) %all-gather.35.cloned.1.call-update) | async-done | bytes 33554448 | tf_op jit(solution)/shard_map/all_gather | solution.py:542
  1917.1 31.6 %bitcast_convert_fusion = f32[1,8192,2048]{2,1,0:T(8,128)} fusion(bf16[8192,2048]{1,0:T(8,128)(2,1)} %all-gather.35.cloned.1.call-done), kind=kLoop, calls=%fused_computation | loop fusion | flops 16777216 | bytes 100663296 | tf_op jit(solution)/shard_map/broadcast_in_dim | solution.py:571
  (120 shorter events, 302.5 us)
Async XLA Ops:
  14.6 171.9 %all-gather.21.cloned.1.call-start = ((), (), s32[]{:S(2)}) async-start(), calls=%async_computation.6 | async-start | bytes 12582912 | tf_op jit(solution)/shard_map/all_gather | solution.py:496
  20.5 331.7 %reduce-scatter.5.cloned.1.call-start = ((), (), s32[]{:S(2)}) async-start(), calls=%async_computation.5 | async-start | bytes 12582912 | tf_op jit(solution)/shard_map/reduce_scatter | solution.py:508
  186.4 263.9 %reduce-scatter.9.cloned.1.call-start = ((), (), s32[]{:S(2)}) async-start(), calls=%async_computation.9 | async-start | bytes 12582912 | tf_op jit(solution)/shard_map/reduce_scatter | solution.py:511
  351.6 173.0 %all-gather.39.cloned.1.call-start = ((), (), s32[]{:S(2)}) async-start(), calls=%async_computation.18 | async-start | bytes 37748736 | tf_op jit(solution)/shard_map/all_gather | solution.py:504
  352.2 191.5 %all-gather.23.cloned.1.call-start = ((), (), s32[]{:S(2)}) async-start(), calls=%async_computation.7 | async-start | bytes 12582912 | tf_op jit(solution)/shard_map/all_gather | solution.py:496
  360.4 337.5 %all-gather.25.cloned.1.call-start = ((), (), s32[]{:S(2)}) async-start(), calls=%async_computation.10 | async-start | bytes 12582912 | tf_op jit(solution)/shard_map/all_gather | solution.py:496
  532.3 247.2 %reduce-scatter.7.cloned.1.call-start = ((), (), s32[]{:S(2)}) async-start(), calls=%async_computation.8 | async-start | bytes 12582912 | tf_op jit(solution)/shard_map/reduce_scatter | solution.py:508
  697.1 173.2 %all-gather.41.cloned.1.call-start = ((), (), s32[]{:S(2)}) async-start(), calls=%async_computation.19 | async-start | bytes 37748736 | tf_op jit(solution)/shard_map/all_gather | solution.py:506
  697.8 191.5 %all-gather.27.cloned.1.call-start = ((), (), s32[]{:S(2)}) async-start(), calls=%async_computation.11 | async-start | bytes 12582912 | tf_op jit(solution)/shard_map/all_gather | solution.py:496
  787.6 255.2 %all-gather.29.cloned.1.call-start = ((), (), s32[]{:S(2)}) async-start(), calls=%async_computation.13 | async-start | bytes 12582912 | tf_op jit(solution)/shard_map/all_gather | solution.py:496
  787.7 81.9 %collective-permute-start = (bf16[512,4096]{1,0:T(8,128)(2,1)}, bf16[512,4096]{1,0:T(8,128)(2,1)}, u32[]{:S(2)}, u32[]{:S(2)}) collective-permute-start(bf16[512,4096]{1,0:T(8,128)(2,1)} %mlp.13), channel_id=1, source_target_pairs={{0,1},{1,0},{2,3},{3,2},{4,5},{5,4},{6,7},{7,6}} | collective-permute-start | bytes 12582920 | tf_op jit(solution)/shard_map/ppermute | solution.py:459
  880.3 244.1 %reduce-scatter.11.cloned.1.call-start = ((), (), s32[]{:S(2)}) async-start(), calls=%async_computation.12 | async-start | bytes 12582912 | tf_op jit(solution)/shard_map/reduce_scatter | solution.py:508
  1042.8 214.6 %all-gather.31.cloned.1.call-start = ((), (), s32[]{:S(2)}) async-start(), calls=%async_computation.14 | async-start | bytes 18874368 | tf_op jit(solution)/shard_map/all_gather | solution.py:490
  1143.0 275.9 %all-gather.33.cloned.1.call-start = ((), (), s32[]{:S(2)}) async-start(), calls=%async_computation.15 | async-start | bytes 18874368 | tf_op jit(solution)/shard_map/all_gather | solution.py:490
  1143.0 81.8 %collective-permute-start.8 = (bf16[512,4096]{1,0:T(8,128)(2,1)}, bf16[512,4096]{1,0:T(8,128)(2,1)}, u32[]{:S(2)}, u32[]{:S(2)}) collective-permute-start(bf16[512,4096]{1,0:T(8,128)(2,1)} %mlp.16), channel_id=1, source_target_pairs={{0,1},{1,0},{2,3},{3,2},{4,5},{5,4},{6,7},{7,6}} | collective-permute-start | bytes 12582920 | tf_op jit(solution)/shard_map/ppermute | solution.py:459
  1244.5 486.5 %all-gather.37.cloned.1.call-start = ((), (), s32[]{:S(2)}) async-start(), calls=%async_computation.17 | async-start | bytes 18874368 | tf_op jit(solution)/shard_map/all_gather | solution.py:539
  1250.5 70.8 %collective-permute-start.3 = (bf16[512,512]{1,0:T(8,128)(2,1)}, bf16[512,512]{1,0:T(8,128)(2,1)}, u32[]{:S(2)}, u32[]{:S(2)}) collective-permute-start(bf16[512,512]{1,0:T(8,128)(2,1)} %get-tuple-element.123), channel_id=1, source_target_pairs={{0,3},{1,2},{2,1},{3,0},{4,7},{5,6},{6,5},{7,4}} | collective-permute-start | bytes 1572872 | tf_op jit(solution)/shard_map/ppermute | solution.py:459
  1252.1 70.5 %collective-permute-start.5 = (bf16[512,512]{1,0:T(8,128)(2,1)}, bf16[512,512]{1,0:T(8,128)(2,1)}, u32[]{:S(2)}, u32[]{:S(2)}) collective-permute-start(bf16[512,512]{1,0:T(8,128)(2,1)} %get-tuple-element.121), channel_id=1, source_target_pairs={{0,5},{1,4},{2,7},{3,6},{4,1},{5,0},{6,3},{7,2}} | collective-permute-start | bytes 1572872 | tf_op jit(solution)/shard_map/ppermute | solution.py:459
  1322.7 96.2 %collective-permute-start.11 = (bf16[512,512]{1,0:T(8,128)(2,1)}, bf16[512,512]{1,0:T(8,128)(2,1)}, u32[]{:S(2)}, u32[]{:S(2)}) collective-permute-start(bf16[512,512]{1,0:T(8,128)(2,1)} %get-tuple-element.115), channel_id=1, source_target_pairs={{0,3},{1,2},{2,1},{3,0},{4,7},{5,6},{6,5},{7,4}} | collective-permute-start | bytes 1572872 | tf_op jit(solution)/shard_map/ppermute | solution.py:459
  1323.4 95.5 %collective-permute-start.12 = (bf16[512,512]{1,0:T(8,128)(2,1)}, bf16[512,512]{1,0:T(8,128)(2,1)}, u32[]{:S(2)}, u32[]{:S(2)}) collective-permute-start(bf16[512,512]{1,0:T(8,128)(2,1)} %get-tuple-element.114), channel_id=1, source_target_pairs={{0,4},{1,5},{2,6},{3,7},{4,0},{5,1},{6,2},{7,3}} | collective-permute-start | bytes 1572872 | tf_op jit(solution)/shard_map/ppermute | solution.py:459
  1324.6 94.3 %collective-permute-start.13 = (bf16[512,512]{1,0:T(8,128)(2,1)}, bf16[512,512]{1,0:T(8,128)(2,1)}, u32[]{:S(2)}, u32[]{:S(2)}) collective-permute-start(bf16[512,512]{1,0:T(8,128)(2,1)} %get-tuple-element.113), channel_id=1, source_target_pairs={{0,5},{1,4},{2,7},{3,6},{4,1},{5,0},{6,3},{7,2}} | collective-permute-start | bytes 1572872 | tf_op jit(solution)/shard_map/ppermute | solution.py:459
  1441.8 308.2 %all-gather.45.cloned.1.call-start = ((), (), s32[]{:S(2)}) async-start(), calls=%async_computation.21 | async-start | bytes 28311552 | tf_op jit(solution)/shard_map/all_gather | solution.py:555
  1588.7 189.8 %all-gather.43.cloned.1.call-start = ((), (), s32[]{:S(2)}) async-start(), calls=%async_computation.20 | async-start | bytes 9437184 | tf_op jit(solution)/shard_map/all_gather | solution.py:557
  1605.9 311.2 %all-gather.35.cloned.1.call-start = ((), (), s32[]{:S(2)}) async-start(), calls=%async_computation.16 | async-start | bytes 37748736 | tf_op jit(solution)/shard_map/all_gather | solution.py:542
  (15 other events, 524.2 us)
Sparse Core Ops, SparseCore 0:
  14.8 19.2 all-gather.18
  36.1 18.2 all-gather.20
  186.6 14.8 reduce-scatter.4
  351.7 14.8 reduce-scatter.8
  368.2 156.3 all-gather.38
  526.5 17.0 all-gather.22
  545.7 18.2 all-gather.24
  697.2 14.8 reduce-scatter.6
  713.9 156.3 all-gather.40
  872.2 17.0 all-gather.26
  890.8 18.2 all-gather.28
  1042.9 14.8 reduce-scatter.10
  1143.1 85.3 all-gather.30
  1244.6 174.1 all-gather.32
  1441.9 84.7 all-gather.36
  1588.8 120.3 all-gather.44
  1710.8 49.4 all-gather.42
  1762.0 155.0 all-gather.34

commit v4 on v3

--- a/solution.py
+++ b/solution.py
@@ -15,10 +15,6 @@
 
 def after(values, dep):
     return lax.optimization_barrier((values, dep))[0]
-
-
-def rms_unit(values):
-    return values * lax.rsqrt(jnp.mean(values * values, axis=-1, keepdims=True) + EPS)
 
 
 def mlp_kernel(layer, steps, wide, residual, where_ref, *refs):
@@ -303,7 +299,8 @@
 def proj_kernel(scale, first, last, count, chunk, me_ref, *refs):
     pieces = refs[:count]
     z_ref, s_ref = refs[count : count + 2]
-    out_ref, sq_ref, total, feat, error_buf = refs[-5:]
+    outs = refs[count + (2 if first else 3) : -4]
+    sq_ref, total, feat, error_buf = refs[-4:]
     k = pl.program_id(0)
     rows, width = z_ref.shape
 
@@ -330,7 +327,12 @@
 
     @pl.when(k == pl.num_programs(0) - 1)
     def _():
-        out_ref[...] = (scale * total[...]).astype(jnp.bfloat16) if last else total[...]
+        if last:
+            half = total.shape[0] // 2
+            outs[0][...] = (scale * total[:half, :]).astype(jnp.bfloat16)
+            outs[1][...] = (scale * total[half:, :]).astype(jnp.bfloat16)
+        else:
+            outs[0][...] = total[...]
 
 
 def proj_part(me, pieces, targets, states, parity, scale, total, last, chunk=16):
@@ -346,31 +348,30 @@
     if total is not None:
         in_specs.append(whole)
         args.append(total)
+    outs = [(cols // 2, jnp.bfloat16)] * 2 if last else [(cols, jnp.float32)]
     return pl.pallas_call(
         functools.partial(proj_kernel, scale, total is None, last, size, chunk),
         grid_spec=pltpu.PrefetchScalarGridSpec(
             num_scalar_prefetch=1,
             grid=(size,),
             in_specs=in_specs,
-            out_specs=[whole, pl.BlockSpec((8, width), lambda k, me: (0, 0))],
+            out_specs=[pl.BlockSpec((h, width), lambda k, me: (0, 0)) for h, _ in outs] + [pl.BlockSpec((8, width), lambda k, me: (0, 0))],
             scratch_shapes=[
                 pltpu.VMEM((cols, width), jnp.float32),
                 pltpu.VMEM((rows, cols), jnp.bfloat16),
                 pltpu.VMEM((rows, width), jnp.bfloat16),
             ],
         ),
-        out_shape=[
-            jax.ShapeDtypeStruct((cols, width), jnp.bfloat16 if last else jnp.float32),
-            jax.ShapeDtypeStruct((8, width), jnp.float32),
-        ],
+        out_shape=[jax.ShapeDtypeStruct((h, width), t) for h, t in outs] + [jax.ShapeDtypeStruct((8, width), jnp.float32)],
         compiler_params=pltpu.CompilerParams(vmem_limit_bytes=VMEM_CAP),
         cost_estimate=pl.CostEstimate(flops=2 * size * rows * cols * width, bytes_accessed=size * rows * (4 * width + 2 * cols), transcendentals=0),
         name="proj",
     )(*args)
 
 
-def down_kernel(scale, first, chunk, cuts, z_ref, s_ref, u_ref, *refs):
-    d_ref, out_ref, total, z_scale, s_scale = refs[-5:]
+def down_kernel(scale, first, last, chunk, cuts, z_ref, s_ref, u_ref, *refs):
+    d_ref, *outs = refs[0 if first else 1 : -3]
+    total, z_scale, s_scale = refs[-3:]
     k = pl.program_id(0) * pl.num_programs(1) + pl.program_id(1)
 
     @pl.when(k == 0)
@@ -397,7 +398,11 @@
 
     @pl.when(k == pl.num_programs(0) * pl.num_programs(1) - 1)
     def _():
-        out_ref[...] = total[...].astype(out_ref.dtype)
+        if last:
+            outs[0][...] = total[: cols // 2, :].astype(jnp.bfloat16)
+            outs[1][...] = total[cols // 2 :, :].astype(jnp.bfloat16)
+        else:
+            outs[0][...] = total[...]
 
 
 def down_part_of(ups, targets, states, parity, scale, total, last, block=512, chunk=16, cuts=1):
@@ -413,15 +418,13 @@
     if total is not None:
         in_specs.append(whole)
         args.append(total)
+    outs = [(cols // 2, jnp.bfloat16)] * 2 if last else [(cols, jnp.float32)]
     return pl.pallas_call(
-        functools.partial(down_kernel, scale, total is None, chunk, cuts),
+        functools.partial(down_kernel, scale, total is None, last, chunk, cuts),
         grid=(half, steps),
         in_specs=in_specs,
-        out_specs=[spec(width), whole],
-        out_shape=[
-            jax.ShapeDtypeStruct((rows, width), jnp.bfloat16),
-            jax.ShapeDtypeStruct((cols, width), jnp.bfloat16 if last else jnp.float32),
-        ],
+        out_specs=[spec(width)] + [pl.BlockSpec((h, width), lambda i, j: (0, 0), pipeline_mode=pl.Buffered(1)) for h, _ in outs],
+        out_shape=[jax.ShapeDtypeStruct((rows, width), jnp.bfloat16)] + [jax.ShapeDtypeStruct((h, width), t) for h, t in outs],
         scratch_shapes=[pltpu.VMEM((cols, width), jnp.float32), pltpu.VMEM((block, 128), jnp.float32), pltpu.VMEM((block, 128), jnp.float32)],
         compiler_params=pltpu.CompilerParams(vmem_limit_bytes=VMEM_CAP),
         cost_estimate=pl.CostEstimate(flops=2 * rows * width * cols, bytes_accessed=rows * (6 * width + 2 * cols), transcendentals=0),
@@ -429,29 +432,121 @@
     )(*args)
 
 
-def spread_kernel(piece_ref, *rest):
-    rest[-1][...] = piece_ref[...].astype(jnp.float32)
-
-
-def spread(out, pieces, first_row, shape, block=512):
-    count, rows, cols = pieces.shape
-    specs = [pl.BlockSpec((None, block, cols), lambda k, i: (k, i, 0))]
-    args = [pieces]
+def place_kernel(count, owner_ref, half_ref, *refs):
+    for h in range(count):
+
+        @pl.when(pl.program_id(0) == h)
+        def _():
+            refs[-1][...] = refs[h][...].astype(jnp.float32)
+
+
+def place(out, pieces, owners, halves, shape, by_cols, block=512):
+    rows, cols = pieces[0].shape
+    block = min(block, rows)
+    steps = rows // block
+    count = len(pieces)
+    specs = [pl.BlockSpec((block, cols), lambda h, i, owner, half, own=own: (jnp.where(h < own, 0, jnp.where(h > own, steps - 1, i)), 0)) for own in range(count)]
+    if by_cols:
+        where = lambda h, i, owner, half: (half[h] * steps + i, owner[h])
+    else:
+        where = lambda h, i, owner, half: ((owner[h] * 2 + half[h]) * steps + i, 0)
+    args = [jnp.stack(owners).astype(jnp.int32), jnp.array(halves, jnp.int32), *pieces]
     alias = {}
     if out is not None:
         specs.append(pl.BlockSpec(memory_space=pl.ANY))
         args.append(out)
-        alias = {1: 0}
+        alias = {count + 2: 0}
     return pl.pallas_call(
-        spread_kernel,
-        grid=(count, rows // block),
-        in_specs=specs,
-        out_specs=pl.BlockSpec((block, cols), lambda k, i: (first_row // block + i, k)),
+        functools.partial(place_kernel, count),
+        grid_spec=pltpu.PrefetchScalarGridSpec(
+            num_scalar_prefetch=2,
+            grid=(count, steps),
+            in_specs=specs,
+            out_specs=pl.BlockSpec((block, cols), where),
+        ),
         out_shape=jax.ShapeDtypeStruct(shape, jnp.float32),
         input_output_aliases=alias,
         compiler_params=pltpu.CompilerParams(vmem_limit_bytes=VMEM_CAP),
         cost_estimate=pl.CostEstimate(flops=count * rows * cols, bytes_accessed=6 * count * rows * cols, transcendentals=0),
-        name="spread",
+        name="place",
+    )(*args)
+
+
+def gelu_slope(pre):
+    scale = 0.7978845608028654
+    square = pre * pre
+    bend = jnp.tanh(scale * pre * (1.0 + 0.044715 * square))
+    return 0.5 * (1.0 + bend) + (0.5 * scale) * pre * (1.0 - bend * bend) * (1.0 + 0.134145 * square)
+
+
+def rest_kernel(first, last, sub, me_ref, d_ref, p_ref, a_ref, s_ref, up_ref, down_ref, *refs):
+    outs, (gain_ref, total, dp) = refs[:-3], refs[-3:]
+    outs = outs[0 if first else 1 :]
+    k = pl.program_id(0) * pl.num_programs(1) + pl.program_id(1)
+    rows, width = s_ref.shape
+
+    @pl.when(k == 0)
+    def _():
+        gain_ref[...] = jnp.zeros_like(gain_ref)
+        total[...] = jnp.zeros_like(total) if first else refs[0][...]
+
+    for r in range(rows // sub):
+        part = slice(r * sub, (r + 1) * sub)
+        d_up = lax.dot_general(d_ref[part, :], down_ref[...], (((1,), (1,)), ((), ())), preferred_element_type=jnp.float32)
+        dp[part, :] = (gelu_slope(p_ref[part, :]) * d_up).astype(jnp.bfloat16)
+    total[...] += lax.dot_general(a_ref[...], dp[...], (((0,), (0,)), ((), ())), preferred_element_type=jnp.float32)
+    for r in range(rows // sub):
+        part = slice(r * sub, (r + 1) * sub)
+        state = s_ref[part, :].astype(jnp.float32)
+        inv = lax.rsqrt(jnp.mean(state * state, axis=-1, keepdims=True) + EPS)
+        d_act = lax.dot_general(dp[part, :], up_ref[...], (((1,), (1,)), ((), ())), preferred_element_type=jnp.float32)
+        gain_ref[...] += jnp.sum((d_act * (s_ref[part, :].astype(jnp.float32) * inv)).reshape(sub // 8, 8, width), axis=0)
+
+    @pl.when(k == pl.num_programs(0) * pl.num_programs(1) - 1)
+    def _():
+        if last:
+            half = width // 2
+            outs[0][...] = total[:half, :].astype(jnp.bfloat16)
+            outs[1][...] = total[half:, :].astype(jnp.bfloat16)
+        else:
+            outs[0][...] = total[...]
+
+
+def rest_part(me, d_out, pre, act, states, up, down, parity, total, last, block=512, sub=256):
+    n_seq, seq_len, width = states.shape
+    cols = pre.shape[1]
+    half = n_seq // 2
+    rows = half * seq_len
+    steps = seq_len // block
+    spec = lambda w: pl.BlockSpec((block, w), lambda i, j, me: (i * steps + j, 0))
+    once = pl.Buffered(1)
+    whole = lambda h: pl.BlockSpec((h, cols), lambda i, j, me: (0, 0), pipeline_mode=once)
+    in_specs = [
+        spec(width),
+        spec(cols),
+        spec(width),
+        pl.BlockSpec((None, block, width), lambda i, j, me: (2 * i + parity, j, 0)),
+        pl.BlockSpec((None, width, cols), lambda i, j, me: (0, 0, me[0]), pipeline_mode=once),
+        pl.BlockSpec((None, cols, width), lambda i, j, me: (0, me[0], 0), pipeline_mode=once),
+    ]
+    args = [me.reshape(1), d_out, pre, act, states, up, down]
+    if total is not None:
+        in_specs.append(whole(width))
+        args.append(total)
+    outs = [(width // 2, jnp.bfloat16)] * 2 if last else [(width, jnp.float32)]
+    return pl.pallas_call(
+        functools.partial(rest_kernel, total is None, last, sub),
+        grid_spec=pltpu.PrefetchScalarGridSpec(
+            num_scalar_prefetch=1,
+            grid=(half, steps),
+            in_specs=in_specs,
+            out_specs=[whole(h) for h, _ in outs] + [pl.BlockSpec((8, width), lambda i, j, me: (0, 0))],
+            scratch_shapes=[pltpu.VMEM((width, cols), jnp.float32), pltpu.VMEM((block, cols), jnp.bfloat16)],
+        ),
+        out_shape=[jax.ShapeDtypeStruct((h, cols), t) for h, t in outs] + [jax.ShapeDtypeStruct((8, width), jnp.float32)],
+        compiler_params=pltpu.CompilerParams(vmem_limit_bytes=VMEM_CAP),
+        cost_estimate=pl.CostEstimate(flops=6 * rows * width * cols, bytes_accessed=rows * (6 * width + 4 * cols), transcendentals=rows * cols),
+        name="rest",
     )(*args)
 
 
@@ -459,12 +554,29 @@
     return lax.ppermute(value, AXES, [(i, i ^ bits) for i in range(size)])
 
 
-def gelu_back(pre_act, grad_out):
-    return jax.vjp(jax.nn.gelu, pre_act)[1](grad_out)[0]
-
-
-def dot(a, b, dims):
-    return lax.dot_general(a, b, (dims, ((), ())), preferred_element_type=jnp.float32)
+def send(halves, size):
+    first, second = halves
+    have = {(0, 0): first, (0, 1): second}
+    have[2, 0], have[4, 1] = flip(first, 2, size), flip(second, 4, size)
+    have[2, 1], have[4, 0] = flip(second, 2, size), flip(first, 4, size)
+    have[1, 0], have[1, 1] = flip(first, 1, size), flip(second, 1, size)
+    return have
+
+
+def relay(have, size):
+    diag = {(6, 1): flip(have[4, 1], 2, size), (6, 0): flip(have[2, 0], 4, size)}
+    near = {(bits | 1, half): flip(have[bits, half], 1, size) for bits in (2, 4) for half in range(2)}
+    far = {(7, half): flip(diag[6, half], 1, size) for half in range(2)}
+    return {**have, **diag, **near, **far}
+
+
+def collect(out, have, me, chips, dep, shape, by_cols):
+    for bits in chips:
+        keys = [(bits | core, half) for half in range(2) for core in range(2)]
+        pieces = after([have[key] for key in keys], dep)
+        out = place(out, pieces, [me ^ key[0] for key in keys], [key[1] for key in keys], shape, by_cols)
+        dep = ()
+    return out
 
 
 def solution(mesh):
@@ -473,12 +585,12 @@
     def step(teacher_in, student_in, teacher_gain, teacher_up_w, teacher_down, student_gain, student_up, student_down, student_proj):
         me = lax.axis_index("data") * 2 + lax.axis_index("model")
         n_layers = teacher_up_w.shape[0]
+        t_width = teacher_in.shape[2]
         _, seq_len, s_width = student_in.shape
         s_hidden = student_up.shape[2]
         part = s_hidden // size
         total = size * seq_len * s_width
         grad_scale = 2.0 / total
-        v_up, v_down = student_up[0], student_down[0]
 
         own = student_in[0]
         side = lax.axis_index("model")
@@ -535,39 +647,22 @@
         acts, pre, ups = zip(*[pre_of(me, all_in, student_gain, student_up, c, part) for c in range(2)])
         d_out_0, down_sum = down_part_of(ups[0], after(targets_0, (proj_sum, ups[1])), all_out, 0, grad_scale, None, False)
         targets_1 = after(targets_1, down_sum)
-        proj_piece, square_1 = proj_part(me, feat_1, targets_1, all_out, 1, grad_scale, proj_sum, True)
-        proj_all = lax.all_gather(proj_piece, AXES, axis=0, tiled=True)
+        *proj_halves, square_1 = proj_part(me, feat_1, targets_1, all_out, 1, grad_scale, proj_sum, True)
+        proj_have = relay(send(proj_halves, size), size)
         loss = (jnp.sum(square_0) + jnp.sum(square_1)) / total
-        d_out_1, down_piece = down_part_of(ups[1], after(targets_1, proj_piece), all_out, 1, grad_scale, down_sum, True)
-        down_all = lax.all_gather(down_piece, AXES, axis=0, tiled=True)
-
-        d_outs = after((d_out_0, d_out_1), down_piece)
-        up_part = lax.dynamic_slice(after(v_up, proj_piece), (0, me * part), (s_width, part))
-        down_part = lax.dynamic_slice(after(v_down, proj_piece), (me * part, 0), (part, s_width))
-        d_pres = [gelu_back(pre[c], dot(d_outs[c], down_part, ((1,), (1,)))).astype(jnp.bfloat16) for c in range(2)]
-
-        def up_rows(first, count):
-            cols = slice(first, first + count)
-            return (dot(acts[0][:, cols], d_pres[0], ((0,), (0,))) + dot(acts[1][:, cols], d_pres[1], ((0,), (0,)))).astype(jnp.bfloat16)
-
-        most = s_width * 3 // 4
-        up_piece_0 = up_rows(0, most)
-        up_all_0 = lax.all_gather(up_piece_0, AXES, axis=0, tiled=False)
-        up_piece = up_rows(most, s_width - most)
-        up_all_1 = lax.all_gather(up_piece, AXES, axis=0, tiled=False)
-
-        d_pres = after(d_pres, up_piece)
-        gain_sum = jnp.zeros((s_width,), jnp.float32)
-        seqs = all_in.reshape(size // 2, 2, seq_len, s_width)
-        for c in range(2):
-            d_act = dot(d_pres[c], up_part, ((1,), (1,))).reshape(size // 2, seq_len, s_width)
-            gain_sum = gain_sum + jnp.sum(d_act * rms_unit(seqs[:, c].astype(jnp.float32)), axis=(0, 1))
-        grad_gain = lax.psum(gain_sum, AXES)
-        grad_proj = after(proj_all, gain_sum).astype(jnp.float32)
-        grad_down = after(down_all, grad_gain).astype(jnp.float32)
-        shape = (s_width, s_hidden)
-        grad_up = spread(None, up_all_0, 0, shape)
-        grad_up = spread(grad_up, up_all_1, most, shape)
+        d_out_1, *down_halves = down_part_of(ups[1], after(targets_1, proj_halves), all_out, 1, grad_scale, down_sum, True)
+        down_have = relay(send(down_halves, size), size)
+        up_sum, gain_0 = rest_part(me, after(d_out_0, down_halves), pre[0], acts[0], all_in, student_up, student_down, 0, None, False)
+        *up_halves, gain_1 = rest_part(me, d_out_1, pre[1], acts[1], all_in, student_up, student_down, 1, up_sum, True)
+        up_have = relay(send(up_halves, size), size)
+
+        proj_shape, down_shape, up_shape = (t_width, s_width), (s_hidden, s_width), (s_width, s_hidden)
+        grad_proj = collect(None, proj_have, me, (0, 2, 4, 6), up_halves, proj_shape, False)
+        grad_down = collect(None, down_have, me, (0, 2, 4), grad_proj, down_shape, False)
+        grad_down = collect(grad_down, down_have, me, (6,), grad_down, down_shape, False)
+        gain_sum = jnp.sum(gain_0, axis=0) + jnp.sum(gain_1, axis=0)
+        grad_gain = lax.psum(after(gain_sum, grad_down), AXES)
+        grad_up = collect(None, up_have, me, (0, 2, 4, 6), (grad_down, grad_gain), up_shape, True)
         return (loss, grad_up[None], grad_down[None], grad_gain[None], grad_proj[None])
 
     return jax.shard_map(

time: 1970 us -> 2060 us (1.046)
  Pallas kernels: 1350 us -> 1560 us
  matrix products: 171 us -> 0 us
  waiting for transfers between devices: 271 us -> 375 us
  other arithmetic: 100 us -> 7.64 us
  starting transfers between devices: 14.4 us -> 50.1 us
    ppermute x16 -> x58, waiting for transfers between devices: 0.04 us -> 247 us  [flip(): return lax.ppermute(value, AXES, [(i, i ^ bits) for i in range(size)])]
    pallas_call x4 -> x16, Pallas kernels: 113 us -> 337 us  [the longest x2 148 us: rest_part(): pl.pallas_call(functools.partial(rest_kernel, total is None, last, sub),...]
    dot_general x8 -> x0, matrix products: 171 us -> none  [dot(): lax.dot_general(a, b, (dims, ((), ())), preferred_element_type=jnp.float32)]
    all_gather x4 -> x0, waiting for transfers between devices: 128 us -> none  [the longest x1 128 us: step(): down_all = lax.all_gather(down_piece, AXES, axis=0, tiled=True)]
    broadcast_in_dim x2 -> x0, other arithmetic: 50.5 us -> none  [the longest x1 31.6 us: step(): grad_down[None]]
    ppermute x16 -> x58, starting transfers between devices: 13.6 us -> 49.5 us  [flip(): return lax.ppermute(value, AXES, [(i, i ^ bits) for i in range(size)])]
    convert_element_type x1 -> x0, other arithmetic: 34.4 us -> none  [step(): seqs[:, c].astype(jnp.float32)]
  transfers between devices with their start and end apart: 34 -> 72, of which waited for: 7 -> 20; matrix products, arithmetic and copies ran while one was open for 13% -> 1% of each run, Pallas kernels for 66% -> 72%
where the time goes in v4:
time: 2060 us; the launch traced here: 2040 us
  Pallas kernels  1560 us (76%)
  waiting for transfers between devices  375 us (18%)
  starting transfers between devices  50.1 us (2%)
  blocking collectives  21.8 us (1%)
    pallas_call x9, Pallas kernels, mlp(): pl.pallas_call(functools.partial(mlp_kernel, layer, steps, wide, state is...  1020 us
    ppermute x58, waiting for transfers between devices, flip(): return lax.ppermute(value, AXES, [(i, i ^ bits) for i in range(size)])  247 us
    pallas_call x2, Pallas kernels, rest_part(): pl.pallas_call(functools.partial(rest_kernel, total is None, last, sub),...  148 us
    pallas_call x12, Pallas kernels, place(): pl.pallas_call(functools.partial(place_kernel, count), grid_spec=pltpu.Pr...  116 us
    all_gather x1, waiting for transfers between devices, step(): all_in = lax.all_gather(after(own, acts[0]), AXES, axis=0, tiled=False)  74.4 us
    pallas_call x2, Pallas kernels, down_part_of(): pl.pallas_call(functools.partial(down_kernel, scale, total is None, last,...  72.8 us
    pallas_call x2, Pallas kernels, pre_of(): pl.pallas_call(functools.partial(pre_kernel, sub), grid_spec=pltpu.Prefet...  61 us
    ppermute x58, starting transfers between devices, flip(): return lax.ppermute(value, AXES, [(i, i ^ bits) for i in range(size)])  49.5 us
  transfers between devices with their start and end apart: 72, of which 20 were waited for; matrix products, arithmetic and copies ran while one was open for 1% of the time, Pallas kernels for 72%

profile of v4, /device:TPU:1, one launch (start us, length us, event | category | flops | bytes accessed | tf_op | source)
XLA Modules:
  0.0 2039.6 jit_solution(6167725339531739020)
XLA Ops:
  34.1 152.3 %mlp.9 = bf16[1024,4096]{1,0:T(8,128)(2,1)} custom-call(s32[1]{0:T(128)} %constant.7.clone.1.where_ref, bf16[1024,4096]{1,0:T(8,128)(2,1)} %all-gather.13.cloned.1.call-done.refs_0_, bf16[3,4096,8192]{2,1,0:T(8,128)(2,1)} %refs_1_.19, bf16[3,8192,4096]{2,1,0:T(8,128)(2,1)} %refs_2_.18), custom_call_target="tpu_custom_call" | custom-call | flops 137438953472 | bytes 150994944 | tf_op jit(solution)/shard_map/mlp/pallas_call | solution.py:142
  186.5 152.9 %mlp.10 = bf16[1024,4096]{1,0:T(8,128)(2,1)} custom-call(s32[1]{0:T(128)} %constant.7.clone.1.where_ref, bf16[1024,4096]{1,0:T(8,128)(2,1)} %all-gather.15.cloned.1.call-done.refs_0_, bf16[3,4096,8192]{2,1,0:T(8,128)(2,1)} %refs_1_.19, bf16[3,8192,4096]{2,1,0:T(8,128)(2,1)} %refs_2_.18), custom_call_target="tpu_custom_call" | custom-call | flops 137438953472 | bytes 150994944 | tf_op jit(solution)/shard_map/mlp/pallas_call | solution.py:142
  356.1 82.0 %mlp.12 = bf16[1024,2048]{1,0:T(8,128)(2,1)} custom-call(s32[1]{0:T(128)} %constant.7.clone.1.where_ref, bf16[1024,2048]{1,0:T(8,128)(2,1)} %norm.5.refs_0_, bf16[1,2048,8192]{2,1,0:T(8,128)(2,1)} %up_ref.3, bf16[1,8192,2048]{2,1,0:T(8,128)(2,1)} %down_ref.3, bf16[1024,2048]{1,0:T(8,128)(2,1)} %bitcast.60), custom_call_target="tpu_custom_call" | custom-call | flops 68719476736 | bytes 75497472 | tf_op jit(solution)/shard_map/mlp/pallas_call | solution.py:142
  438.1 74.4 %all-gather.29.cloned.1.call-done = bf16[8192,2048]{1,0:T(8,128)(2,1)} async-done(((bf16[1024,2048]{1,0:T(8,128)(2,1)}), bf16[8192,2048]{1,0:T(8,128)(2,1)}) %all-gather.29.cloned.1.call-update) | async-done | bytes 33554448 | tf_op jit(solution)/shard_map/all_gather | solution.py:616
  531.5 153.5 %mlp.11 = bf16[1024,4096]{1,0:T(8,128)(2,1)} custom-call(s32[1]{0:T(128)} %constant.7.clone.1.where_ref, bf16[1024,4096]{1,0:T(8,128)(2,1)} %all-gather.17.cloned.1.call-done.refs_0_, bf16[3,4096,8192]{2,1,0:T(8,128)(2,1)} %refs_1_.19, bf16[3,8192,4096]{2,1,0:T(8,128)(2,1)} %refs_2_.18), custom_call_target="tpu_custom_call" | custom-call | flops 137438953472 | bytes 150994944 | tf_op jit(solution)/shard_map/mlp/pallas_call | solution.py:142
  685.8 81.5 %mlp.13 = bf16[512,4096]{1,0:T(8,128)(2,1)} custom-call(s32[1]{0:T(128)} %bitcast.1.where_ref, bf16[1024,4096]{1,0:T(8,128)(2,1)} %all-gather.19.cloned.1.call-done.refs_0_, bf16[3,4096,8192]{2,1,0:T(8,128)(2,1)} %refs_1_.19, bf16[3,8192,4096]{2,1,0:T(8,128)(2,1)} %refs_2_.18), custom_call_target="tpu_custom_call" | custom-call | flops 68719476736 | bytes 142606336 | tf_op jit(solution)/shard_map/mlp/pallas_call | solution.py:142
  775.8 81.9 %mlp.15.refs_0_ = bf16[512,4096]{1,0:T(8,128)(2,1)} custom-call(s32[1]{0:T(128)} %bitcast.4.where_ref, bf16[1024,4096]{1,0:T(8,128)(2,1)} %all-gather.19.cloned.1.call-done.refs_0_, bf16[3,4096,8192]{2,1,0:T(8,128)(2,1)} %refs_1_.19, bf16[3,8192,4096]{2,1,0:T(8,128)(2,1)} %refs_2_.18), custom_call_target="tpu_custom_call" | custom-call | flops 68719476736 | bytes 142606336 | tf_op jit(solution)/shard_map/mlp/pallas_call | solution.py:142
  877.2 153.5 %mlp.14 = bf16[1024,4096]{1,0:T(8,128)(2,1)} custom-call(s32[1]{0:T(128)} %constant.7.clone.1.where_ref, bf16[1024,4096]{1,0:T(8,128)(2,1)} %all-gather.21.cloned.1.call-done.refs_0_, bf16[3,4096,8192]{2,1,0:T(8,128)(2,1)} %refs_1_.19, bf16[3,8192,4096]{2,1,0:T(8,128)(2,1)} %refs_2_.18), custom_call_target="tpu_custom_call" | custom-call | flops 137438953472 | bytes 150994944 | tf_op jit(solution)/shard_map/mlp/pallas_call | solution.py:142
  1030.8 81.5 %mlp.16 = bf16[512,4096]{1,0:T(8,128)(2,1)} custom-call(s32[1]{0:T(128)} %bitcast.1.where_ref, bf16[1024,4096]{1,0:T(8,128)(2,1)} %all-gather.23.cloned.1.call-done.refs_0_, bf16[3,4096,8192]{2,1,0:T(8,128)(2,1)} %refs_1_.19, bf16[3,8192,4096]{2,1,0:T(8,128)(2,1)} %refs_2_.18), custom_call_target="tpu_custom_call" | custom-call | flops 68719476736 | bytes 142606336 | tf_op jit(solution)/shard_map/mlp/pallas_call | solution.py:142
  1131.2 81.4 %mlp.17.refs_0_ = bf16[512,4096]{1,0:T(8,128)(2,1)} custom-call(s32[1]{0:T(128)} %bitcast.4.where_ref, bf16[1024,4096]{1,0:T(8,128)(2,1)} %all-gather.23.cloned.1.call-done.refs_0_, bf16[3,4096,8192]{2,1,0:T(8,128)(2,1)} %refs_1_.19, bf16[3,8192,4096]{2,1,0:T(8,128)(2,1)} %refs_2_.18), custom_call_target="tpu_custom_call" | custom-call | flops 68719476736 | bytes 142606336 | tf_op jit(solution)/shard_map/mlp/pallas_call | solution.py:142
  1242.6 30.5 %pre.2 = (bf16[4096,2048]{1,0:T(8,128)(2,1)}, f32[4096,1024]{1,0:T(8,128)}, bf16[4096,1024]{1,0:T(8,128)(2,1)}) custom-call(s32[1]{0:T(128)} %bitcast.me_ref, bf16[8,1024,2048]{2,1,0:T(8,128)(2,1)} %bitcast.54, f32[1,2048]{1,0:T(1,128)} %g_ref.5, bf16[1,2048,8192]{2,1,0:T(8,128)(2,1)} %up_ref.3), custom_call_target="tpu_custom_call" | custom-call | flops 17179869184 | bytes 58720256 | tf_op jit(solution)/shard_map/pre/pallas_call | solution.py:218
  1275.8 30.5 %pre.3 = (bf16[4096,2048]{1,0:T(8,128)(2,1)}, f32[4096,1024]{1,0:T(8,128)}, bf16[4096,1024]{1,0:T(8,128)(2,1)}) custom-call(s32[1]{0:T(128)} %bitcast.me_ref, bf16[8,1024,2048]{2,1,0:T(8,128)(2,1)} %bitcast.55, f32[1,2048]{1,0:T(1,128)} %g_ref.5, bf16[1,2048,8192]{2,1,0:T(8,128)(2,1)} %up_ref.3), custom_call_target="tpu_custom_call" | custom-call | flops 17179869184 | bytes 58720256 | tf_op jit(solution)/shard_map/pre/pallas_call | solution.py:218
  1312.3 24.8 %proj.2 = (f32[512,2048]{1,0:T(8,128)}, f32[8,2048]{1,0:T(8,128)}) custom-call(s32[1]{0:T(128)} %bitcast.me_ref, bf16[512,512]{1,0:T(8,128)(2,1)} %get-tuple-element.220.refs_0_, bf16[512,512]{1,0:T(8,128)(2,1)} %collective-permute-done.1.refs_1_, bf16[512,512]{1,0:T(8,128)(2,1)} %collective-permute-done.2.refs_2_, ...), custom_call_target="tpu_custom_call" | custom-call | flops 8589934592 | bytes 37748736 | tf_op jit(solution)/shard_map/proj/pallas_call | solution.py:352
  1350.3 35.7 %down.2 = (bf16[4096,2048]{1,0:T(8,128)(2,1)}, f32[1024,2048]{1,0:T(8,128)}) custom-call(bf16[4096,2048]{1,0:T(8,128)(2,1)} %all-gather.25.cloned.1.call-done.refs_8_.z_ref, bf16[8,1024,2048]{2,1,0:T(8,128)(2,1)} %bitcast.51, bf16[4096,1024]{1,0:T(8,128)(2,1)} %get-tuple-element.135.u_ref), custom_call_target="tpu_custom_call" | custom-call | flops 17179869184 | bytes 58720256 | tf_op jit(solution)/shard_map/down/pallas_call | solution.py:422
  1404.5 22.8 %proj.3 = (bf16[256,2048]{1,0:T(8,128)(2,1)}, bf16[256,2048]{1,0:T(8,128)(2,1)}, f32[8,2048]{1,0:T(8,128)}) custom-call(s32[1]{0:T(128)} %bitcast.me_ref, bf16[512,512]{1,0:T(8,128)(2,1)} %get-tuple-element.212.refs_0_, bf16[512,512]{1,0:T(8,128)(2,1)} %collective-permute-done.9.refs_1_, bf16[512,512]{1,0:T(8,128)(2,1)} %collective-permute-done.10.refs_2_, ...), custom_call_target="tpu_custom_call" | custom-call | flops 8589934592 | bytes 37748736 | tf_op jit(solution)/shard_map/proj/pallas_call | solution.py:352
  1454.2 37.0 %down.3 = (bf16[4096,2048]{1,0:T(8,128)(2,1)}, bf16[512,2048]{1,0:T(8,128)(2,1)}, bf16[512,2048]{1,0:T(8,128)(2,1)}) custom-call(bf16[4096,2048]{1,0:T(8,128)(2,1)} %all-gather.27.cloned.1.call-done.refs_8_.z_ref, bf16[8,1024,2048]{2,1,0:T(8,128)(2,1)} %bitcast.53, bf16[4096,1024]{1,0:T(8,128)(2,1)} %get-tuple-element.133.u_ref, ...), custom_call_target="tpu_custom_call" | custom-call | flops 17179869184 | bytes 58720256 | tf_op jit(solution)/shard_map/down/pallas_call | solution.py:422
  1494.5 73.4 %rest.2 = (f32[2048,1024]{1,0:T(8,128)}, f32[8,2048]{1,0:T(8,128)}) custom-call(s32[1]{0:T(128)} %bitcast.me_ref, bf16[4096,2048]{1,0:T(8,128)(2,1)} %get-tuple-element.148.d_ref, f32[4096,1024]{1,0:T(8,128)} %get-tuple-element.149.p_ref, bf16[4096,2048]{1,0:T(8,128)(2,1)} %get-tuple-element.150.a_ref, bf16[8,1024,2048]{2,1,0:T(8,128)(2,1)} %bitcast.56, ...), custom_call_target="tpu_custom_call" | custom-call | flops 51539607552 | bytes 67108864 | tf_op jit(solution)/shard_map/rest/pallas_call | solution.py:537
  1570.1 74.4 %rest.3 = (bf16[1024,1024]{1,0:T(8,128)(2,1)}, bf16[1024,1024]{1,0:T(8,128)(2,1)}, f32[8,2048]{1,0:T(8,128)}) custom-call(s32[1]{0:T(128)} %bitcast.me_ref, bf16[4096,2048]{1,0:T(8,128)(2,1)} %get-tuple-element.142.d_ref, f32[4096,1024]{1,0:T(8,128)} %get-tuple-element.143.p_ref, bf16[4096,2048]{1,0:T(8,128)(2,1)} %get-tuple-element.144.a_ref, ...), custom_call_target="tpu_custom_call" | custom-call | flops 51539607552 | bytes 67108864 | tf_op jit(solution)/shard_map/rest/pallas_call | solution.py:537
  1661.9 28.7 %collective-permute-done.33.refs_2_ = bf16[512,2048]{1,0:T(8,128)(2,1)S(1)} collective-permute-done((bf16[512,2048]{1,0:T(8,128)(2,1)}, bf16[512,2048]{1,0:T(8,128)(2,1)S(1)}, u32[]{:S(2)}, u32[]{:S(2)}) %collective-permute-start.33) | collective-permute-done | bytes 2097184 | tf_op jit(solution)/shard_map/ppermute | solution.py:554
  1707.6 42.7 %collective-permute-done.26.refs_2_ = bf16[1024,1024]{1,0:T(8,128)(2,1)S(1)} collective-permute-done((bf16[1024,1024]{1,0:T(8,128)(2,1)}, bf16[1024,1024]{1,0:T(8,128)(2,1)S(1)}, u32[]{:S(2)}, u32[]{:S(2)}) %collective-permute-start.26) | collective-permute-done | bytes 2097184 | tf_op jit(solution)/shard_map/ppermute | solution.py:554
  1751.6 28.9 %collective-permute-done.19.refs_2_ = bf16[1024,1024]{1,0:T(8,128)(2,1)S(1)} collective-permute-done((bf16[1024,1024]{1,0:T(8,128)(2,1)}, bf16[1024,1024]{1,0:T(8,128)(2,1)S(1)}, u32[]{:S(2)}, u32[]{:S(2)}) %collective-permute-start.19) | collective-permute-done | bytes 2097184 | tf_op jit(solution)/shard_map/ppermute | solution.py:554
  1788.7 43.8 %collective-permute-done.31.refs_0_ = bf16[512,2048]{1,0:T(8,128)(2,1)S(1)} collective-permute-done((bf16[512,2048]{1,0:T(8,128)(2,1)}, bf16[512,2048]{1,0:T(8,128)(2,1)S(1)}, u32[]{:S(2)}, u32[]{:S(2)}) %collective-permute-start.31) | collective-permute-done | bytes 2097184 | tf_op jit(solution)/shard_map/ppermute | solution.py:554
  1837.8 42.1 %collective-permute-done.17.refs_0_ = bf16[1024,1024]{1,0:T(8,128)(2,1)} collective-permute-done((bf16[1024,1024]{1,0:T(8,128)(2,1)S(1)}, bf16[1024,1024]{1,0:T(8,128)(2,1)}, u32[]{:S(2)}, u32[]{:S(2)}) %collective-permute-start.17) | collective-permute-done | bytes 2097184 | tf_op jit(solution)/shard_map/ppermute | solution.py:554
  1961.0 21.8 %psum.7 = f32[2048]{0:T(1024)} all-reduce(f32[2048]{0:T(1024)} %add.21), channel_id=1, replica_groups=mesh['data'=4,'model'=2] {'data','model'}, use_global_device_ids=true, to_apply=%region_8.0 | all-reduce | flops 2048 | bytes 16384 | tf_op jit(solution)/shard_map/psum | solution.py:664
  (217 shorter events, 390.4 us)
Async XLA Ops:
  14.6 171.9 %all-gather.15.cloned.1.call-start = ((), (), s32[]{:S(2)}) async-start(), calls=%async_computation.6 | async-start | bytes 12582912 | tf_op jit(solution)/shard_map/all_gather | solution.py:608
  20.5 319.5 %reduce-scatter.5.cloned.1.call-start = ((), (), s32[]{:S(2)}) async-start(), calls=%async_computation.5 | async-start | bytes 12582912 | tf_op jit(solution)/shard_map/reduce_scatter | solution.py:620
  186.4 251.7 %reduce-scatter.9.cloned.1.call-start = ((), (), s32[]{:S(2)}) async-start(), calls=%async_computation.9 | async-start | bytes 12582912 | tf_op jit(solution)/shard_map/reduce_scatter | solution.py:623
  339.4 173.1 %all-gather.29.cloned.1.call-start = ((), (), s32[]{:S(2)}) async-start(), calls=%async_computation.16 | async-start | bytes 37748736 | tf_op jit(solution)/shard_map/all_gather | solution.py:616
  340.0 191.5 %all-gather.17.cloned.1.call-start = ((), (), s32[]{:S(2)}) async-start(), calls=%async_computation.7 | async-start | bytes 12582912 | tf_op jit(solution)/shard_map/all_gather | solution.py:608
  348.3 337.5 %all-gather.19.cloned.1.call-start = ((), (), s32[]{:S(2)}) async-start(), calls=%async_computation.10 | async-start | bytes 12582912 | tf_op jit(solution)/shard_map/all_gather | solution.py:608
  520.2 247.2 %reduce-scatter.7.cloned.1.call-start = ((), (), s32[]{:S(2)}) async-start(), calls=%async_computation.8 | async-start | bytes 12582912 | tf_op jit(solution)/shard_map/reduce_scatter | solution.py:620
  685.0 173.2 %all-gather.31.cloned.1.call-start = ((), (), s32[]{:S(2)}) async-start(), calls=%async_computation.17 | async-start | bytes 37748736 | tf_op jit(solution)/shard_map/all_gather | solution.py:618
  685.7 191.5 %all-gather.21.cloned.1.call-start = ((), (), s32[]{:S(2)}) async-start(), calls=%async_computation.11 | async-start | bytes 12582912 | tf_op jit(solution)/shard_map/all_gather | solution.py:608
  775.5 255.2 %all-gather.23.cloned.1.call-start = ((), (), s32[]{:S(2)}) async-start(), calls=%async_computation.13 | async-start | bytes 12582912 | tf_op jit(solution)/shard_map/all_gather | solution.py:608
  868.2 244.1 %reduce-scatter.11.cloned.1.call-start = ((), (), s32[]{:S(2)}) async-start(), calls=%async_computation.12 | async-start | bytes 12582912 | tf_op jit(solution)/shard_map/reduce_scatter | solution.py:620
  1030.7 211.9 %all-gather.25.cloned.1.call-start = ((), (), s32[]{:S(2)}) async-start(), calls=%async_computation.14 | async-start | bytes 18874368 | tf_op jit(solution)/shard_map/all_gather | solution.py:602
  1130.8 273.6 %all-gather.27.cloned.1.call-start = ((), (), s32[]{:S(2)}) async-start(), calls=%async_computation.15 | async-start | bytes 18874368 | tf_op jit(solution)/shard_map/all_gather | solution.py:602
  1308.4 96.0 %collective-permute-start.12 = (bf16[512,512]{1,0:T(8,128)(2,1)}, bf16[512,512]{1,0:T(8,128)(2,1)}, u32[]{:S(2)}, u32[]{:S(2)}) collective-permute-start(bf16[512,512]{1,0:T(8,128)(2,1)} %get-tuple-element.208), channel_id=1, source_target_pairs={{0,4},{1,5},{2,6},{3,7},{4,0},{5,1},{6,2},{7,3}} | collective-permute-start | bytes 1572872 | tf_op jit(solution)/shard_map/ppermute | solution.py:554
  1310.4 94.0 %collective-permute-start.13 = (bf16[512,512]{1,0:T(8,128)(2,1)}, bf16[512,512]{1,0:T(8,128)(2,1)}, u32[]{:S(2)}, u32[]{:S(2)}) collective-permute-start(bf16[512,512]{1,0:T(8,128)(2,1)} %get-tuple-element.207), channel_id=1, source_target_pairs={{0,5},{1,4},{2,7},{3,6},{4,1},{5,0},{6,3},{7,2}} | collective-permute-start | bytes 1572872 | tf_op jit(solution)/shard_map/ppermute | solution.py:554
  1310.6 93.8 %collective-permute-start.14 = (bf16[512,512]{1,0:T(8,128)(2,1)}, bf16[512,512]{1,0:T(8,128)(2,1)}, u32[]{:S(2)}, u32[]{:S(2)}) collective-permute-start(bf16[512,512]{1,0:T(8,128)(2,1)} %get-tuple-element.206), channel_id=1, source_target_pairs={{0,6},{1,7},{2,4},{3,5},{4,2},{5,3},{6,0},{7,1}} | collective-permute-start | bytes 1572872 | tf_op jit(solution)/shard_map/ppermute | solution.py:554
  1646.4 103.9 %collective-permute-start.26 = (bf16[1024,1024]{1,0:T(8,128)(2,1)}, bf16[1024,1024]{1,0:T(8,128)(2,1)S(1)}, u32[]{:S(2)}, u32[]{:S(2)}) collective-permute-start(bf16[1024,1024]{1,0:T(8,128)(2,1)} %get-tuple-element.203.refs_2_), channel_id=1, source_target_pairs={{0,2},{1,3},{2,0},{3,1},{4,6},{5,7},{6,4},{7,5}} | collective-permute-start | bytes 6291464 | tf_op jit(solution)/shard_map/ppermute | solution.py:554
  1660.6 119.9 %collective-permute-start.19 = (bf16[1024,1024]{1,0:T(8,128)(2,1)}, bf16[1024,1024]{1,0:T(8,128)(2,1)S(1)}, u32[]{:S(2)}, u32[]{:S(2)}) collective-permute-start(bf16[1024,1024]{1,0:T(8,128)(2,1)} %get-tuple-element.203.refs_2_), channel_id=1, source_target_pairs={{0,4},{1,5},{2,6},{3,7},{4,0},{5,1},{6,2},{7,3}} | collective-permute-start | bytes 6291464 | tf_op jit(solution)/shard_map/ppermute | solution.py:554
  1690.7 96.0 %collective-permute-start.39 = (bf16[512,2048]{1,0:T(8,128)(2,1)}, bf16[512,2048]{1,0:T(8,128)(2,1)S(1)}, u32[]{:S(2)}, u32[]{:S(2)}) collective-permute-start(bf16[512,2048]{1,0:T(8,128)(2,1)} %collective-permute-done.30.refs_0_), channel_id=1, source_target_pairs={{0,1},{1,0},{2,3},{3,2},{4,5},{5,4},{6,7},{7,6}} | collective-permute-start | bytes 6291464 | tf_op jit(solution)/shard_map/ppermute | solution.py:554
  1836.0 114.6 %collective-permute-start.35 = (bf16[512,2048]{1,0:T(8,128)(2,1)}, bf16[512,2048]{1,0:T(8,128)(2,1)}, u32[]{:S(2)}, u32[]{:S(2)}) collective-permute-start(bf16[512,2048]{1,0:T(8,128)(2,1)} %collective-permute-done.34.refs_2_), channel_id=1, source_target_pairs={{0,1},{1,0},{2,3},{3,2},{4,5},{5,4},{6,7},{7,6}} | collective-permute-start | bytes 6291464 | tf_op jit(solution)/shard_map/ppermute | solution.py:554
  1837.4 145.4 %collective-permute-start.28 = (bf16[1024,1024]{1,0:T(8,128)(2,1)}, bf16[1024,1024]{1,0:T(8,128)(2,1)}, u32[]{:S(2)}, u32[]{:S(2)}) collective-permute-start(bf16[1024,1024]{1,0:T(8,128)(2,1)} %get-tuple-element.201.refs_0_), channel_id=1, source_target_pairs={{0,1},{1,0},{2,3},{3,2},{4,5},{5,4},{6,7},{7,6}} | collective-permute-start | bytes 6291464 | tf_op jit(solution)/shard_map/ppermute | solution.py:554
  1879.9 102.9 %collective-permute-start.29 = (bf16[1024,1024]{1,0:T(8,128)(2,1)}, bf16[1024,1024]{1,0:T(8,128)(2,1)}, u32[]{:S(2)}, u32[]{:S(2)}) collective-permute-start(bf16[1024,1024]{1,0:T(8,128)(2,1)} %get-tuple-element.203.refs_2_), channel_id=1, source_target_pairs={{0,1},{1,0},{2,3},{3,2},{4,5},{5,4},{6,7},{7,6}} | collective-permute-start | bytes 6291464 | tf_op jit(solution)/shard_map/ppermute | solution.py:554
  1881.9 100.9 %collective-permute-start.18 = (bf16[1024,1024]{1,0:T(8,128)(2,1)}, bf16[1024,1024]{1,0:T(8,128)(2,1)}, u32[]{:S(2)}, u32[]{:S(2)}) collective-permute-start(bf16[1024,1024]{1,0:T(8,128)(2,1)} %collective-permute-done.17.refs_0_), channel_id=1, source_target_pairs={{0,1},{1,0},{2,3},{3,2},{4,5},{5,4},{6,7},{7,6}} | collective-permute-start | bytes 6291464 | tf_op jit(solution)/shard_map/ppermute | solution.py:554
  1884.5 98.3 %collective-permute-start.21 = (bf16[1024,1024]{1,0:T(8,128)(2,1)}, bf16[1024,1024]{1,0:T(8,128)(2,1)}, u32[]{:S(2)}, u32[]{:S(2)}) collective-permute-start(bf16[1024,1024]{1,0:T(8,128)(2,1)} %collective-permute-done.20.refs_2_), channel_id=1, source_target_pairs={{0,1},{1,0},{2,3},{3,2},{4,5},{5,4},{6,7},{7,6}} | collective-permute-start | bytes 6291464 | tf_op jit(solution)/shard_map/ppermute | solution.py:554
  (64 other events, 3814.4 us)
Sparse Core Ops, SparseCore 0:
  14.8 19.2 all-gather.12
  36.1 18.2 all-gather.14
  186.6 14.8 reduce-scatter.4
  339.5 14.8 reduce-scatter.8
  356.1 156.3 all-gather.28
  514.4 17.0 all-gather.16
  533.6 18.2 all-gather.18
  685.1 14.8 reduce-scatter.6
  701.8 156.3 all-gather.30
  860.1 17.0 all-gather.20
  878.7 18.2 all-gather.22
  1030.8 14.8 reduce-scatter.10
  1130.9 85.3 all-gather.24
  1232.3 172.0 all-gather.26

commit v5 on v4

v5 whole, which is shorter than its diff:
```python
import functools

import jax
import jax.numpy as jnp
from jax import lax
from jax.experimental import pallas as pl
from jax.experimental.pallas import tpu as pltpu
from jax.sharding import PartitionSpec as P


EPS = 1e-6
BF16 = jnp.bfloat16
F32 = jnp.float32
VMEM_CAP = 64 * 1024 * 1024 - 65536
AXES = ("data", "model")


PARAMS = pltpu.CompilerParams(vmem_limit_bytes=VMEM_CAP)
ONCE = pl.Buffered(1)
ANY = pl.BlockSpec(memory_space=pl.ANY)
ROWS = (((1,), (0,)), ((), ()))
BOTH_ROWS = (((0,), (0,)), ((), ()))
BOTH_COLS = (((1,), (1,)), ((), ()))


def dot(a, b, dims=ROWS):
    return lax.dot_general(a, b, dims, preferred_element_type=F32)


def fixed(*shape, **options):
    return pl.BlockSpec(shape, lambda *_: (0,) * len(shape), **options)


def cost(flops, nbytes, exps=0):
    return pl.CostEstimate(flops=flops, bytes_accessed=nbytes, transcendentals=exps)


def array(dtype, *shape):
    return jax.ShapeDtypeStruct(shape, dtype)


def inverse_rms(state):
    return lax.rsqrt(jnp.mean(state * state, axis=-1, keepdims=True) + EPS)


def cut(size, count):
    return [slice(start, start + size // count) for start in range(0, size, size // count)]


def after(values, dep):
    return lax.optimization_barrier((values, dep))[0]


def mlp_kernel(layer, steps, wide, residual, where_ref, *refs):
    if residual:
        a_hbm, up_hbm, down_hbm, s_hbm, o_hbm, a_ref, up_ref, down_ref, first, second, act, acc, out, a_sem, up_sem, down_sem, o_sem, s_ref, s_sem = refs
    else:
        a_hbm, up_hbm, down_hbm, o_hbm, a_ref, up_ref, down_ref, first, second, act, acc, out, a_sem, up_sem, down_sem, o_sem = refs
    j = pl.program_id(0)
    rows, width = acc.shape
    tile = act.shape[2]
    half = tile // 2
    parts = 4
    size = rows // parts
    now = lax.rem(j, 2)

    def a_copy(r):
        source = pl.ds(pl.multiple_of(where_ref[0] * rows + r * size, size), size)
        return pltpu.make_async_copy(a_hbm.at[source], a_ref.at[pl.ds(r * size, size)], a_sem.at[r])

    def up_copy(k):
        return pltpu.make_async_copy(up_hbm.at[layer, :, pl.ds(pl.multiple_of(k * tile, tile), tile)], up_ref.at[lax.rem(k, 2)], up_sem.at[lax.rem(k, 2)])

    def down_copy(k):
        return pltpu.make_async_copy(down_hbm.at[layer, pl.ds(pl.multiple_of(k * tile, tile), tile)], down_ref.at[lax.rem(k, 2)], down_sem.at[lax.rem(k, 2)])

    def out_copy(k):
        cols = pl.ds(k * wide, wide)
        return pltpu.make_async_copy(out.at[:, cols], o_hbm.at[:, cols], o_sem.at[k])

    @pl.when(j == 0)
    def _():
        up_copy(0).start()
        for r in range(parts):
            a_copy(r).start()
        up_copy(1).start()
        down_copy(0).start()
        if residual:
            pltpu.make_async_copy(s_hbm, s_ref, s_sem.at[0]).start()
        up_copy(0).wait()
        for r, part in enumerate(cut(rows, parts)):
            a_copy(r).wait()
            first[part, :] = dot(a_ref[part, :], up_ref[0, :, :half])
            second[part, :] = dot(a_ref[part, :], up_ref[0, :, half:])
        act[0, :, :half] = jax.nn.gelu(first[...]).astype(BF16)

    @pl.when((j > 0) & (j < steps))
    def _():
        @pl.when(j + 1 < steps)
        def _():
            up_copy(j + 1).start()

        down_copy(j).start()
        up_copy(j).wait()
        act[1 - now, :, half:] = jax.nn.gelu(second[...]).astype(BF16)
        first[...] = dot(a_ref[...], up_ref[now, :, :half])
        for part in cut(rows, parts):
            act[now, part, :half] = jax.nn.gelu(first[part, :]).astype(BF16)
            second[part, :] = dot(a_ref[part, :], up_ref[now, :, half:])

    @pl.when(j == steps)
    def _():
        act[1 - now, :, half:] = jax.nn.gelu(second[...]).astype(BF16)

    def down(first_tile, last_tile):
        down_copy(j - 1).wait()
        if last_tile and residual:
            pltpu.make_async_copy(s_hbm, s_ref, s_sem.at[0]).wait()
        for k, cols in enumerate(cut(width, width // wide)):
            total = dot(act[1 - now], down_ref[1 - now, :, cols])
            if not first_tile:
                total = acc[:, cols] + total
            if not last_tile:
                acc[:, cols] = total
            else:
                if residual:
                    total = s_ref[:, cols].astype(F32) + total
                out[:, cols] = total.astype(BF16)
                out_copy(k).start()
        if last_tile:
            for k in range(width // wide):
                out_copy(k).wait()

    @pl.when(j == 1)
    def _():
        down(True, False)

    @pl.when((j > 1) & (j < steps))
    def _():
        down(False, False)

    @pl.when(j == steps)
    def _():
        down(False, True)


def mlp(a, up, down, layer, state=None, rows=None, where=None, tile=512, wide=512):
    depth = a.shape[1]
    rows = rows or a.shape[0]
    where = jnp.zeros((1,), jnp.int32) if where is None else where.astype(jnp.int32).reshape(1)
    hidden = up.shape[2]
    width = down.shape[2]
    steps = hidden // tile
    hbm = ANY
    scratch = [
        pltpu.VMEM((rows, depth), BF16),
        pltpu.VMEM((2, depth, tile), BF16),
        pltpu.VMEM((2, tile, width), BF16),
        pltpu.VMEM((rows, tile // 2), F32),
        pltpu.VMEM((rows, tile // 2), F32),
        pltpu.VMEM((2, rows, tile), BF16),
        pltpu.VMEM((rows, width), F32),
        pltpu.VMEM((rows, width), BF16),
        pltpu.SemaphoreType.DMA((4,)),
        pltpu.SemaphoreType.DMA((2,)),
        pltpu.SemaphoreType.DMA((2,)),
        pltpu.SemaphoreType.DMA((width // wide,)),
    ]
    args = [a, up, down]
    if state is not None:
        args.append(state)
        scratch += [pltpu.VMEM((rows, width), BF16), pltpu.SemaphoreType.DMA((1,))]
    return pl.pallas_call(
        functools.partial(mlp_kernel, layer, steps, wide, state is not None),
        grid_spec=pltpu.PrefetchScalarGridSpec(
            num_scalar_prefetch=1,
            grid=(steps + 1,),
            in_specs=[hbm] * len(args),
            out_specs=hbm,
            scratch_shapes=scratch,
        ),
        out_shape=array(BF16, rows, width),
        compiler_params=PARAMS,
        cost_estimate=pl.CostEstimate(
            flops=2 * rows * hidden * (depth + width),
            bytes_accessed=2 * (rows * (depth + width) + hidden * (depth + width)),
            transcendentals=rows * hidden,
        ),
        name="mlp",
    )(where, *args)


def norm_kernel(h_ref, g_ref, a_ref):
    state = h_ref[...].astype(F32)
    inv = inverse_rms(state)
    a_ref[...] = (state * inv * g_ref[...]).astype(BF16)


def step_kernel(h_ref, *refs):
    *parts, g_ref, o_ref, a_ref = refs
    delta = parts[0][...].astype(F32)
    if len(parts) > 1:
        delta = (delta + parts[1][...].astype(F32)).astype(BF16).astype(F32)
    state = (h_ref[...].astype(F32) + delta).astype(BF16)
    o_ref[...] = state
    state = state.astype(F32)
    inv = inverse_rms(state)
    a_ref[...] = (state * inv * g_ref[...]).astype(BF16)


def teacher_norm(hidden, delta, gains, layer, which=0, block=128):
    rows, width = hidden.shape[-2:]
    spec = pl.BlockSpec((block, width), lambda i: (i, 0))
    source = spec if hidden.ndim == 2 else pl.BlockSpec((None, block, width), lambda i: (which, i, 0))
    gain_spec = fixed(1, width)
    shape = array(BF16, rows, width)
    count = rows * width
    common = dict(
        grid=(rows // block,),
        compiler_params=PARAMS,
    )
    gain = gains[layer : layer + 1]
    if not delta:
        price = cost(8 * count, 4 * count)
        return hidden, pl.pallas_call(norm_kernel, in_specs=[source, gain_spec], out_specs=spec, out_shape=shape, cost_estimate=price, name="norm", **common)(hidden, gain)
    price = cost(10 * count, 8 * count)
    return pl.pallas_call(step_kernel, in_specs=[source] + [spec] * len(delta) + [gain_spec], out_specs=[spec, spec], out_shape=[shape, shape], cost_estimate=price, name="step", **common)(hidden, *delta, gain)


def pre_kernel(sub, me_ref, s_ref, g_ref, w_ref, a_ref, p_ref, u_ref):
    for part in cut(s_ref.shape[0], s_ref.shape[0] // sub):
        state = s_ref[part, :].astype(F32)
        inv = inverse_rms(state)
        a_ref[part, :] = (state * inv * g_ref[...]).astype(BF16)
    for part in cut(s_ref.shape[0], s_ref.shape[0] // sub):
        pre = dot(a_ref[part, :], w_ref[...])
        p_ref[part, :] = pre
        u_ref[part, :] = jax.nn.gelu(pre).astype(BF16)


def pre_of(me, states, gain, weights, parity, cols, block=512, sub=256):
    n_seq, seq_len, width = states.shape
    half = n_seq // 2
    rows = half * seq_len
    steps = seq_len // block
    out = lambda w: pl.BlockSpec((block, w), lambda i, j, me: (i * steps + j, 0))
    return pl.pallas_call(
        functools.partial(pre_kernel, sub),
        grid_spec=pltpu.PrefetchScalarGridSpec(
            num_scalar_prefetch=1,
            grid=(half, steps),
            in_specs=[
                pl.BlockSpec((None, block, width), lambda i, j, me: (2 * i + parity, j, 0)),
                fixed(1, width),
                pl.BlockSpec((None, width, cols), lambda i, j, me: (0, 0, me[0])),
            ],
            out_specs=[out(width), out(cols), out(cols)],
        ),
        out_shape=[
            array(BF16, rows, width),
            array(F32, rows, cols),
            array(BF16, rows, cols),
        ],
        compiler_params=PARAMS,
        cost_estimate=cost(2 * rows * width * cols, rows * (4 * width + 6 * cols), rows * cols),
        name="pre",
    )(me.reshape(1), states, gain, weights)


def errors_at(z_ref, s_ref, part):
    state = s_ref[part, :].astype(F32)
    inv = inverse_rms(state)
    unit = state * inv
    return z_ref[part, :].astype(F32) - unit, unit, inv


def finish_kernel(count, size, me_ref, h_ref, *refs):
    parts = refs[:count]
    q_ref = refs[count]
    feats = refs[-2 - size : -2]
    z_ref, acc = refs[-2:]
    k = pl.program_id(0)
    delta = parts[0][...].astype(F32)
    if count > 1:
        delta = (delta + parts[1][...].astype(F32)).astype(BF16).astype(F32)
    feat = (h_ref[...].astype(F32) + delta).astype(BF16)
    for bits in range(size):

        @pl.when(me_ref[0] ^ k == bits)
        def _():
            feats[bits][...] = feat

    term = dot(feat, q_ref[...])

    @pl.when(k == 0)
    def _():
        acc[...] = term

    @pl.when((k > 0) & (k < size - 1))
    def _():
        acc[...] += term

    @pl.when(k == size - 1)
    def _():
        z_ref[...] = (acc[...] + term).astype(BF16)


def finish_part(me, hidden, delta, proj, size):
    rows, width = hidden.shape
    cols = width // size
    out = proj.shape[2]
    spec = pl.BlockSpec((rows, cols), lambda k, me: (0, k))
    return pl.pallas_call(
        functools.partial(finish_kernel, len(delta), size),
        grid_spec=pltpu.PrefetchScalarGridSpec(
            num_scalar_prefetch=1,
            grid=(size,),
            in_specs=[spec] * (1 + len(delta)) + [pl.BlockSpec((None, cols, out), lambda k, me: (0, k, 0))],
            out_specs=[fixed(rows, cols)] * size + [fixed(rows, out)],
            scratch_shapes=[pltpu.VMEM((rows, out), F32)],
        ),
        out_shape=[array(BF16, rows, cols)] * size + [array(BF16, rows, out)],
        compiler_params=PARAMS,
        cost_estimate=cost(2 * rows * width * out, 2 * width * (4 * rows + out)),
        name="finish",
    )(me.reshape(1), hidden, *delta, proj)


def proj_kernel(scale, first, last, count, chunk, me_ref, *refs):
    pieces = refs[:count]
    z_ref, s_ref = refs[count : count + 2]
    outs = refs[count + (2 if first else 3) : -4]
    sq_ref, total, feat, error_buf = refs[-4:]
    k = pl.program_id(0)
    rows, width = z_ref.shape

    @pl.when(k == 0)
    def _():
        sq_ref[...] = jnp.zeros_like(sq_ref)
        if first:
            total[...] = jnp.zeros_like(total)
        else:
            total[...] = refs[count + 2][...]

    for i in range(count):

        @pl.when(k == i)
        def _():
            feat[...] = pieces[i][...]

    for part in cut(rows, rows // chunk):
        error = errors_at(z_ref, s_ref, part)[0]
        error_buf[part, :] = error.astype(BF16)
        sq_ref[...] += jnp.sum((error * error).reshape(chunk // 8, 8, width), axis=0)
    total[...] += dot(feat[...], error_buf[...], BOTH_ROWS)

    @pl.when(k == pl.num_programs(0) - 1)
    def _():
        if last:
            half = total.shape[0] // 2
            outs[0][...] = (scale * total[:half, :]).astype(BF16)
            outs[1][...] = (scale * total[half:, :]).astype(BF16)
        else:
            outs[0][...] = total[...]


def proj_part(me, pieces, targets, states, parity, scale, total, last, chunk=16):
    n_seq, _, width = states.shape
    size = n_seq
    rows, cols = pieces[0].shape
    whole = fixed(cols, width)
    in_specs = [fixed(rows, cols)] * size + [
        pl.BlockSpec((rows, width), lambda k, me: (me[0] ^ k, 0)),
        pl.BlockSpec((None, rows, width), lambda k, me: (2 * ((me[0] ^ k) // 2) + parity, (me[0] ^ k) % 2, 0)),
    ]
    args = [me.reshape(1), *pieces, targets, states]
    if total is not None:
        in_specs.append(whole)
        args.append(total)
    outs = [(cols // 2, BF16)] * 2 if last else [(cols, F32)]
    return pl.pallas_call(
        functools.partial(proj_kernel, scale, total is None, last, size, chunk),
        grid_spec=pltpu.PrefetchScalarGridSpec(
            num_scalar_prefetch=1,
            grid=(size,),
            in_specs=in_specs,
            out_specs=[fixed(h, width) for h, _ in outs] + [fixed(8, width)],
            scratch_shapes=[
                pltpu.VMEM((cols, width), F32),
                pltpu.VMEM((rows, cols), BF16),
                pltpu.VMEM((rows, width), BF16),
            ],
        ),
        out_shape=[array(t, h, width) for h, t in outs] + [array(F32, 8, width)],
        compiler_params=PARAMS,
        cost_estimate=cost(2 * size * rows * cols * width, size * rows * (4 * width + 2 * cols)),
        name="proj",
    )(*args)


def down_kernel(scale, first, last, chunk, z_ref, s_ref, u_ref, *refs):
    d_ref, *outs = refs[0 if first else 1 : -3]
    total, z_scale, s_scale = refs[-3:]
    k = pl.program_id(0) * pl.num_programs(1) + pl.program_id(1)

    @pl.when(k == 0)
    def _():
        total[...] = jnp.zeros_like(total) if first else refs[0][...]

    width = z_ref.shape[1]
    for part in cut(z_ref.shape[0], z_ref.shape[0] // chunk):
        state = s_ref[part, :].astype(F32)
        square = jnp.sum(state * state, axis=-1, keepdims=True) / width
        cross = jnp.sum(state * z_ref[part, :].astype(F32), axis=-1, keepdims=True) / width
        inv = lax.rsqrt(square + EPS)
        lean = inv * cross - inv * inv * square
        z_scale[part, :] = jnp.broadcast_to(-scale * inv, (chunk, 128))
        s_scale[part, :] = jnp.broadcast_to(scale * inv * inv * (1.0 + lean), (chunk, 128))
    for part in cut(z_ref.shape[0], z_ref.shape[0] // chunk):
        d_ref[part, :] = (s_ref[part, :].astype(F32) * s_scale[part, :1] + z_ref[part, :].astype(F32) * z_scale[part, :1]).astype(BF16)
    cols = total.shape[0]
    total[...] += dot(u_ref[...], d_ref[...], BOTH_ROWS)

    @pl.when(k == pl.num_programs(0) * pl.num_programs(1) - 1)
    def _():
        if last:
            outs[0][...] = total[: cols // 2, :].astype(BF16)
            outs[1][...] = total[cols // 2 :, :].astype(BF16)
        else:
            outs[0][...] = total[...]


def down_part_of(ups, targets, states, parity, scale, total, last, block=512, chunk=16):
    n_seq, seq_len, width = states.shape
    half = n_seq // 2
    cols = ups.shape[1]
    rows = half * seq_len
    steps = seq_len // block
    spec = lambda w: pl.BlockSpec((block, w), lambda i, j: (i * steps + j, 0))
    whole = fixed(cols, width, pipeline_mode=ONCE)
    in_specs = [spec(width), pl.BlockSpec((None, block, width), lambda i, j: (2 * i + parity, j, 0)), spec(cols)]
    args = [targets, states, ups]
    if total is not None:
        in_specs.append(whole)
        args.append(total)
    outs = [(cols // 2, BF16)] * 2 if last else [(cols, F32)]
    return pl.pallas_call(
        functools.partial(down_kernel, scale, total is None, last, chunk),
        grid=(half, steps),
        in_specs=in_specs,
        out_specs=[spec(width)] + [fixed(h, width, pipeline_mode=ONCE) for h, _ in outs],
        out_shape=[array(BF16, rows, width)] + [array(t, h, width) for h, t in outs],
        scratch_shapes=[pltpu.VMEM((cols, width), F32), pltpu.VMEM((block, 128), F32), pltpu.VMEM((block, 128), F32)],
        compiler_params=PARAMS,
        cost_estimate=cost(2 * rows * width * cols, rows * (6 * width + 2 * cols)),
        name="down",
    )(*args)


def place_kernel(count, ahead, owner_ref, half_ref, *refs):
    pieces = refs[:count]
    out_ref, buf, sem = refs[-3:]
    block = out_ref.shape[0]
    steps = pl.num_programs(1)
    now = pl.program_id(0) * steps + pl.program_id(1)
    slots = ahead + 1

    def copy(own, step):
        slot = lax.rem(step, slots)
        rows = pl.ds(pl.multiple_of(lax.rem(step, steps) * block, block), block)
        return pltpu.make_async_copy(pieces[own].at[rows], buf.at[slot], sem.at[slot])

    def fetch(step):
        for own in range(count):

            @pl.when((step >= own * steps) & (step < (own + 1) * steps))
            def _():
                copy(own, step).start()

    @pl.when(now == 0)
    def _():
        for step in range(ahead):
            fetch(step)

    fetch(now + ahead)
    copy(0, now).wait()
    out_ref[...] = buf[lax.rem(now, slots)].astype(F32)


def place(out, pieces, owners, halves, shape, by_cols, ahead=3):
    rows, cols = pieces[0].shape
    block = rows // 2
    count = len(pieces)
    if by_cols:
        where = lambda h, i, owner, half: (half[h] * 2 + i, owner[h])
    else:
        where = lambda h, i, owner, half: ((owner[h] * 2 + half[h]) * 2 + i, 0)
    args = [jnp.stack(owners).astype(jnp.int32), jnp.array(halves, jnp.int32), *pieces]
    alias = {}
    if out is not None:
        alias = {len(args): 0}
        args.append(out)
    return pl.pallas_call(
        functools.partial(place_kernel, count, ahead),
        grid_spec=pltpu.PrefetchScalarGridSpec(
            num_scalar_prefetch=2,
            grid=(count, 2),
            in_specs=[ANY] * (len(args) - 2),
            out_specs=pl.BlockSpec((block, cols), where),
            scratch_shapes=[pltpu.VMEM((ahead + 1, block, cols), BF16), pltpu.SemaphoreType.DMA((ahead + 1,))],
        ),
        out_shape=array(F32, *shape),
        input_output_aliases=alias,
        compiler_params=PARAMS,
        cost_estimate=cost(count * rows * cols, 6 * count * rows * cols),
        name="place",
    )(*args)


def gelu_slope(pre):
    scale = 0.7978845608028654
    square = pre * pre
    bend = jnp.tanh(scale * pre * (1.0 + 0.044715 * square))
    return 0.5 * (1.0 + bend) + (0.5 * scale) * pre * (1.0 - bend * bend) * (1.0 + 0.134145 * square)


def rest_kernel(first, last, sub, me_ref, d_ref, p_ref, a_ref, s_ref, up_ref, down_ref, *refs):
    outs, (gain_ref, total, dp) = refs[:-3], refs[-3:]
    outs = outs[0 if first else 1 :]
    k = pl.program_id(0) * pl.num_programs(1) + pl.program_id(1)
    rows, width = s_ref.shape

    @pl.when(k == 0)
    def _():
        gain_ref[...] = jnp.zeros_like(gain_ref)
        total[...] = jnp.zeros_like(total) if first else refs[0][...]

    for part in cut(rows, rows // sub):
        d_up = dot(d_ref[part, :], down_ref[...], BOTH_COLS)
        dp[part, :] = (gelu_slope(p_ref[part, :]) * d_up).astype(BF16)
    total[...] += dot(a_ref[...], dp[...], BOTH_ROWS)
    for part in cut(rows, rows // sub):
        state = s_ref[part, :].astype(F32)
        inv = inverse_rms(state)
        d_act = dot(dp[part, :], up_ref[...], BOTH_COLS)
        gain_ref[...] += jnp.sum((d_act * (s_ref[part, :].astype(F32) * inv)).reshape(sub // 8, 8, width), axis=0)

    @pl.when(k == pl.num_programs(0) * pl.num_programs(1) - 1)
    def _():
        if last:
            half = width // 2
            outs[0][...] = total[:half, :].astype(BF16)
            outs[1][...] = total[half:, :].astype(BF16)
        else:
            outs[0][...] = total[...]


def rest_part(me, d_out, pre, act, states, up, down, parity, total, last, block=512, sub=256):
    n_seq, seq_len, width = states.shape
    cols = pre.shape[1]
    half = n_seq // 2
    rows = half * seq_len
    steps = seq_len // block
    spec = lambda w: pl.BlockSpec((block, w), lambda i, j, me: (i * steps + j, 0))
    whole = lambda h: fixed(h, cols, pipeline_mode=ONCE)
    in_specs = [
        spec(width),
        spec(cols),
        spec(width),
        pl.BlockSpec((None, block, width), lambda i, j, me: (2 * i + parity, j, 0)),
        pl.BlockSpec((None, width, cols), lambda i, j, me: (0, 0, me[0]), pipeline_mode=ONCE),
        pl.BlockSpec((None, cols, width), lambda i, j, me: (0, me[0], 0), pipeline_mode=ONCE),
    ]
    args = [me.reshape(1), d_out, pre, act, states, up, down]
    if total is not None:
        in_specs.append(whole(width))
        args.append(total)
    outs = [(width // 2, BF16)] * 2 if last else [(width, F32)]
    return pl.pallas_call(
        functools.partial(rest_kernel, total is None, last, sub),
        grid_spec=pltpu.PrefetchScalarGridSpec(
            num_scalar_prefetch=1,
            grid=(half, steps),
            in_specs=in_specs,
            out_specs=[whole(h) for h, _ in outs] + [fixed(8, width)],
            scratch_shapes=[pltpu.VMEM((width, cols), F32), pltpu.VMEM((block, cols), BF16)],
        ),
        out_shape=[array(t, h, cols) for h, t in outs] + [array(F32, 8, width)],
        compiler_params=PARAMS,
        cost_estimate=cost(6 * rows * width * cols, rows * (6 * width + 4 * cols), rows * cols),
        name="rest",
    )(*args)


def flip(value, bits, size):
    return lax.ppermute(value, AXES, [(i, i ^ bits) for i in range(size)])


CORE, X, Y = 1, 2, 4


def send(halves, size):
    have = {(0, half): value for half, value in enumerate(halves)}

    def pass_on(*moves):
        for bits, half in moves:
            have[bits, half] = flip(halves[half], bits, size)

    pass_on((X, 0), (Y, 1))
    pass_on((X, 1), (Y, 0))
    pass_on((CORE, 0), (CORE, 1))
    return have


def relay(have, size, dep=()):
    firsts = after((have[X, 0], have[Y, 1]), dep)
    diag = {(X | Y, half): flip(value, (X | Y) ^ bits, size) for half, (bits, value) in enumerate(zip((X, Y), firsts))}
    near = {(bits | CORE, half): flip(have[bits, half], CORE, size) for bits in (X, Y) for half in range(2)}
    far = {(bits | CORE, half): flip(value, CORE, size) for (bits, half), value in diag.items()}
    return {**have, **diag, **near, **far}


def collect(out, have, me, chips, dep, shape, by_cols):
    keys = [(bits | core, half) for bits in chips for half in range(2) for core in range(2)]
    pieces = after([have[key] for key in keys], dep)
    return place(out, pieces, [me ^ key[0] for key in keys], [key[1] for key in keys], shape, by_cols)


def solution(mesh):
    size = mesh.shape["data"] * mesh.shape["model"]

    def step(teacher_in, student_in, teacher_gain, teacher_up_w, teacher_down, student_gain, student_up, student_down, student_proj):
        me = lax.axis_index("data") * 2 + lax.axis_index("model")
        n_layers = teacher_up_w.shape[0]
        t_width = teacher_in.shape[2]
        _, seq_len, s_width = student_in.shape
        s_hidden = student_up.shape[2]
        part = s_hidden // size
        total = size * seq_len * s_width
        grad_scale = 2.0 / total

        own = student_in[0]
        side = lax.axis_index("model")
        last = n_layers - 1
        hidden = [teacher_in, teacher_in]

        def finish(c, delta):
            *feats, target = finish_part(me, hidden[c], delta, student_proj, size)
            targets = lax.all_gather(target, AXES, axis=0, tiled=True)
            pieces = [flip(feats[bits], bits, size) if bits else feats[0] for bits in range(size)]
            return target, targets, pieces

        def normed(c, delta, layer):
            hidden[c], act = teacher_norm(hidden[c], delta, teacher_gain, layer, c)
            return act, lax.all_gather(act, "model", axis=0, tiled=True)

        def teach(act, layer, **window):
            return mlp(act, teacher_up_w, teacher_down, layer, **window)

        acts = [normed(c, (), 0)[1] for c in range(2)]
        for layer in range(n_layers):
            if layer == 0:
                all_in = lax.all_gather(after(own, acts[0]), AXES, axis=0, tiled=False)
            if layer == 1:
                all_out = lax.all_gather(after(own_out, acts[0]), AXES, axis=0, tiled=False)
            partial = teach(acts[0], layer)
            delta_0 = (lax.psum_scatter(partial, "model", scatter_dimension=0, tiled=True),)
            if layer == 0:
                partial = teach(acts[1], layer)
                delta_1 = (lax.psum_scatter(partial, "model", scatter_dimension=0, tiled=True),)
                act, acts[0] = normed(0, after(delta_0, partial), layer + 1)
                own_act = teacher_norm(after(own, act), (), student_gain, 0)[1]
                own_out = mlp(own_act, student_up, student_down, 0, own)
                delta_1 = after(delta_1, (own_out, all_in))
            else:
                rows = acts[1].shape[0] // 2
                partial = teach(acts[1], layer, rows=rows, where=1 - side)
                moved = flip(partial, 1, size)
                delta_0 = after(delta_0, partial)
                if layer < last:
                    ready, acts[0] = normed(0, delta_0, layer + 1)
                else:
                    ready, targets_0, feat_0 = finish(0, delta_0)
                partial = teach(after(acts[1], ready), layer, rows=rows, where=side)
                delta_1 = (partial, moved)
            if layer < last:
                if layer == 1:
                    delta_1 = after(delta_1, all_out)
                acts[1] = normed(1, delta_1, layer + 1)[1]
        target_1, targets_1, feat_1 = finish(1, delta_1)

        all_in, all_out = after((all_in, all_out), target_1)
        acts, pre, ups = zip(*[pre_of(me, all_in, student_gain, student_up, c, part) for c in range(2)])
        proj_sum, square_0 = proj_part(me, feat_0, after(targets_0, ups), all_out, 0, grad_scale, None, False)
        d_out_0, down_sum = down_part_of(ups[0], after(targets_0, (proj_sum, ups[1])), all_out, 0, grad_scale, None, False)
        targets_1 = after(targets_1, down_sum)
        *proj_halves, square_1 = proj_part(me, feat_1, targets_1, all_out, 1, grad_scale, proj_sum, True)
        proj_have = relay(send(proj_halves, size), size)
        loss = jnp.sum(square_0 + square_1) / total
        d_out_1, *down_halves = down_part_of(ups[1], after(targets_1, proj_halves), all_out, 1, grad_scale, down_sum, True)
        down_have = relay(send(down_halves, size), size)
        up_sum, gain_0 = rest_part(me, after(d_out_0, down_halves), pre[0], acts[0], all_in, student_up, student_down, 0, None, False)
        *up_halves, gain_1 = rest_part(me, d_out_1, pre[1], acts[1], all_in, student_up, student_down, 1, up_sum, True)
        up_have = send(up_halves, size)
        grad_gain = jnp.sum(gain_0 + gain_1, axis=0)
        for bits in (CORE, X, Y):
            grad_gain = grad_gain + flip(grad_gain, bits, size)

        grad_proj = collect(None, proj_have, me, (0, X, Y, X | Y), up_halves, (t_width, s_width), False)
        grad_down = collect(None, down_have, me, (0, X, Y), grad_proj, (s_hidden, s_width), False)
        up_have = relay(up_have, size, grad_down)
        grad_down = collect(grad_down, down_have, me, (X | Y,), (), (s_hidden, s_width), False)
        shape = (s_width, s_hidden)
        grad_up = collect(None, up_have, me, (0,), grad_down, shape, True)
        grad_up = collect(grad_up, up_have, me, (X, Y), (), shape, True)
        grad_up = collect(grad_up, up_have, me, (X | Y,), (), shape, True)
        return (loss, grad_up[None], grad_down[None], grad_gain[None], grad_proj[None])

    return jax.shard_map(
        step,
        mesh=mesh,
        in_specs=(
            P("data", "model", None),
            P(("data", "model"), None, None),
            P(),
            P(None, None, "model"),
            P(None, "model", None),
            P(),
            P(),
            P(),
            P(),
        ),
        out_specs=(P(), P(), P(), P(), P()),
        check_vma=False,
    )
```

time: 2060 us -> 2070 us (level)
  waiting for transfers between devices: 375 us -> 415 us
  starting transfers between devices: 50.1 us -> 78 us
  blocking collectives: 21.8 us -> 0 us
    ppermute x58 -> x61, waiting for transfers between devices: 247 us -> 286 us  [flip(): return lax.ppermute(value, AXES, [(i, i ^ bits) for i in range(size)])]
    ppermute x58 -> x61, starting transfers between devices: 49.5 us -> 77.4 us  [flip(): return lax.ppermute(value, AXES, [(i, i ^ bits) for i in range(size)])]
    psum x1 -> x0, blocking collectives: 21.8 us -> none  [step(): grad_gain = lax.psum(after(gain_sum, grad_down), AXES)]
    pallas_call x14 -> x8, Pallas kernels: 154 us -> 133 us  [the longest x6 89.1 us: place(): pl.pallas_call(functools.partial(place_kernel, count, ahead), grid_spec=p...]
  transfers between devices with their start and end apart: 72 -> 75, of which waited for: 20 -> 23; matrix products, arithmetic and copies ran while one was open for 1% -> 0% of each run, Pallas kernels for 72% -> 63%
where the time goes in v5:
time: 2070 us; the launch traced here: 2060 us
  Pallas kernels  1540 us (74%)
  waiting for transfers between devices  415 us (20%)
  starting transfers between devices  78 us (4%)
    pallas_call x9, Pallas kernels, mlp(): pl.pallas_call(functools.partial(mlp_kernel, layer, steps, wide, state is...  1020 us
    ppermute x61, waiting for transfers between devices, flip(): return lax.ppermute(value, AXES, [(i, i ^ bits) for i in range(size)])  286 us
    pallas_call x2, Pallas kernels, rest_part(): pl.pallas_call(functools.partial(rest_kernel, total is None, last, sub),...  148 us
    pallas_call x6, Pallas kernels, place(): pl.pallas_call(functools.partial(place_kernel, count, ahead), grid_spec=p...  89.1 us
    ppermute x61, starting transfers between devices, flip(): return lax.ppermute(value, AXES, [(i, i ^ bits) for i in range(size)])  77.4 us
    all_gather x1, waiting for transfers between devices, step(): all_in = lax.all_gather(after(own, acts[0]), AXES, axis=0, tiled=False)  74.3 us
    pallas_call x2, Pallas kernels, down_part_of(): pl.pallas_call(functools.partial(down_kernel, scale, total is None, last,...  72.8 us
    pallas_call x2, Pallas kernels, pre_of(): pl.pallas_call(functools.partial(pre_kernel, sub), grid_spec=pltpu.Prefet...  62 us
  transfers between devices with their start and end apart: 75, of which 23 were waited for; matrix products, arithmetic and copies ran while one was open for 0% of the time, Pallas kernels for 63%

profile of v5, /device:TPU:1, one launch (start us, length us, event | category | flops | bytes accessed | tf_op | source)
XLA Modules:
  0.0 2056.4 jit_solution(16870902333310604135)
XLA Ops:
  34.1 152.3 %mlp.9 = bf16[1024,4096]{1,0:T(8,128)(2,1)} custom-call(s32[1]{0:T(128)} %constant.10.clone.1.where_ref, bf16[1024,4096]{1,0:T(8,128)(2,1)} %all-gather.13.cloned.1.call-done.refs_0_, bf16[3,4096,8192]{2,1,0:T(8,128)(2,1)} %refs_1_.19, bf16[3,8192,4096]{2,1,0:T(8,128)(2,1)} %refs_2_.18), custom_call_target="tpu_custom_call" | custom-call | flops 137438953472 | bytes 150994944 | tf_op jit(solution)/shard_map/mlp/pallas_call | solution.py:173
  186.5 152.9 %mlp.10 = bf16[1024,4096]{1,0:T(8,128)(2,1)} custom-call(s32[1]{0:T(128)} %constant.10.clone.1.where_ref, bf16[1024,4096]{1,0:T(8,128)(2,1)} %all-gather.15.cloned.1.call-done.refs_0_, bf16[3,4096,8192]{2,1,0:T(8,128)(2,1)} %refs_1_.19, bf16[3,8192,4096]{2,1,0:T(8,128)(2,1)} %refs_2_.18), custom_call_target="tpu_custom_call" | custom-call | flops 137438953472 | bytes 150994944 | tf_op jit(solution)/shard_map/mlp/pallas_call | solution.py:173
  356.1 82.0 %mlp.12 = bf16[1024,2048]{1,0:T(8,128)(2,1)} custom-call(s32[1]{0:T(128)} %constant.10.clone.1.where_ref, bf16[1024,2048]{1,0:T(8,128)(2,1)} %norm.5.refs_0_, bf16[1,2048,8192]{2,1,0:T(8,128)(2,1)} %up_ref.3, bf16[1,8192,2048]{2,1,0:T(8,128)(2,1)} %down_ref.3, bf16[1024,2048]{1,0:T(8,128)(2,1)} %bitcast.28), custom_call_target="tpu_custom_call" | custom-call | flops 68719476736 | bytes 75497472 | tf_op jit(solution)/shard_map/mlp/pallas_call | solution.py:173
  438.2 74.3 %all-gather.29.cloned.1.call-done = bf16[8192,2048]{1,0:T(8,128)(2,1)} async-done(((bf16[1024,2048]{1,0:T(8,128)(2,1)}), bf16[8192,2048]{1,0:T(8,128)(2,1)}) %all-gather.29.cloned.1.call-update) | async-done | bytes 33554448 | tf_op jit(solution)/shard_map/all_gather | solution.py:663
  531.5 153.5 %mlp.11 = bf16[1024,4096]{1,0:T(8,128)(2,1)} custom-call(s32[1]{0:T(128)} %constant.10.clone.1.where_ref, bf16[1024,4096]{1,0:T(8,128)(2,1)} %all-gather.17.cloned.1.call-done.refs_0_, bf16[3,4096,8192]{2,1,0:T(8,128)(2,1)} %refs_1_.19, bf16[3,8192,4096]{2,1,0:T(8,128)(2,1)} %refs_2_.18), custom_call_target="tpu_custom_call" | custom-call | flops 137438953472 | bytes 150994944 | tf_op jit(solution)/shard_map/mlp/pallas_call | solution.py:173
  685.8 81.5 %mlp.13 = bf16[512,4096]{1,0:T(8,128)(2,1)} custom-call(s32[1]{0:T(128)} %bitcast.1.where_ref, bf16[1024,4096]{1,0:T(8,128)(2,1)} %all-gather.19.cloned.1.call-done.refs_0_, bf16[3,4096,8192]{2,1,0:T(8,128)(2,1)} %refs_1_.19, bf16[3,8192,4096]{2,1,0:T(8,128)(2,1)} %refs_2_.18), custom_call_target="tpu_custom_call" | custom-call | flops 68719476736 | bytes 142606336 | tf_op jit(solution)/shard_map/mlp/pallas_call | solution.py:173
  775.8 81.9 %mlp.15.refs_0_ = bf16[512,4096]{1,0:T(8,128)(2,1)} custom-call(s32[1]{0:T(128)} %bitcast.4.where_ref, bf16[1024,4096]{1,0:T(8,128)(2,1)} %all-gather.19.cloned.1.call-done.refs_0_, bf16[3,4096,8192]{2,1,0:T(8,128)(2,1)} %refs_1_.19, bf16[3,8192,4096]{2,1,0:T(8,128)(2,1)} %refs_2_.18), custom_call_target="tpu_custom_call" | custom-call | flops 68719476736 | bytes 142606336 | tf_op jit(solution)/shard_map/mlp/pallas_call | solution.py:173
  877.2 153.5 %mlp.14 = bf16[1024,4096]{1,0:T(8,128)(2,1)} custom-call(s32[1]{0:T(128)} %constant.10.clone.1.where_ref, bf16[1024,4096]{1,0:T(8,128)(2,1)} %all-gather.21.cloned.1.call-done.refs_0_, bf16[3,4096,8192]{2,1,0:T(8,128)(2,1)} %refs_1_.19, bf16[3,8192,4096]{2,1,0:T(8,128)(2,1)} %refs_2_.18), custom_call_target="tpu_custom_call" | custom-call | flops 137438953472 | bytes 150994944 | tf_op jit(solution)/shard_map/mlp/pallas_call | solution.py:173
  1030.8 81.5 %mlp.16 = bf16[512,4096]{1,0:T(8,128)(2,1)} custom-call(s32[1]{0:T(128)} %bitcast.1.where_ref, bf16[1024,4096]{1,0:T(8,128)(2,1)} %all-gather.23.cloned.1.call-done.refs_0_, bf16[3,4096,8192]{2,1,0:T(8,128)(2,1)} %refs_1_.19, bf16[3,8192,4096]{2,1,0:T(8,128)(2,1)} %refs_2_.18), custom_call_target="tpu_custom_call" | custom-call | flops 68719476736 | bytes 142606336 | tf_op jit(solution)/shard_map/mlp/pallas_call | solution.py:173
  1133.7 81.4 %mlp.17.refs_0_ = bf16[512,4096]{1,0:T(8,128)(2,1)} custom-call(s32[1]{0:T(128)} %bitcast.4.where_ref, bf16[1024,4096]{1,0:T(8,128)(2,1)} %all-gather.23.cloned.1.call-done.refs_0_, bf16[3,4096,8192]{2,1,0:T(8,128)(2,1)} %refs_1_.19, bf16[3,8192,4096]{2,1,0:T(8,128)(2,1)} %refs_2_.18), custom_call_target="tpu_custom_call" | custom-call | flops 68719476736 | bytes 142606336 | tf_op jit(solution)/shard_map/mlp/pallas_call | solution.py:173
  1215.1 23.2 %finish.3 = (bf16[512,512]{1,0:T(8,128)(2,1)}, bf16[512,512]{1,0:T(8,128)(2,1)}, bf16[512,512]{1,0:T(8,128)(2,1)}, bf16[512,512]{1,0:T(8,128)(2,1)}, bf16[512,51...) custom-call(s32[1]{0:T(128)} %bitcast.me_ref, ...), custom_call_target="tpu_custom_call" | custom-call | flops 8589934592 | bytes 33554432 | tf_op jit(solution)/shard_map/finish/pallas_call | solution.py:313
  1242.3 31.5 %pre.3 = (bf16[4096,2048]{1,0:T(8,128)(2,1)}, f32[4096,1024]{1,0:T(8,128)}, bf16[4096,1024]{1,0:T(8,128)(2,1)}) custom-call(s32[1]{0:T(128)} %bitcast.me_ref, bf16[8,1024,2048]{2,1,0:T(8,128)(2,1)} %bitcast.21, f32[1,2048]{1,0:T(1,128)} %g_ref.5, bf16[1,2048,8192]{2,1,0:T(8,128)(2,1)} %up_ref.3), custom_call_target="tpu_custom_call" | custom-call | flops 17179869184 | bytes 58720256 | tf_op jit(solution)/shard_map/pre/pallas_call | solution.py:247
  1276.5 30.5 %pre.2 = (bf16[4096,2048]{1,0:T(8,128)(2,1)}, f32[4096,1024]{1,0:T(8,128)}, bf16[4096,1024]{1,0:T(8,128)(2,1)}) custom-call(s32[1]{0:T(128)} %bitcast.me_ref, bf16[8,1024,2048]{2,1,0:T(8,128)(2,1)} %bitcast.22, f32[1,2048]{1,0:T(1,128)} %g_ref.5, bf16[1,2048,8192]{2,1,0:T(8,128)(2,1)} %up_ref.3), custom_call_target="tpu_custom_call" | custom-call | flops 17179869184 | bytes 58720256 | tf_op jit(solution)/shard_map/pre/pallas_call | solution.py:247
  1312.4 23.4 %proj.2 = (f32[512,2048]{1,0:T(8,128)}, f32[8,2048]{1,0:T(8,128)}) custom-call(s32[1]{0:T(128)} %bitcast.me_ref, bf16[512,512]{1,0:T(8,128)(2,1)} %get-tuple-element.141.refs_0_, bf16[512,512]{1,0:T(8,128)(2,1)} %collective-permute-done.1.refs_1_, bf16[512,512]{1,0:T(8,128)(2,1)} %collective-permute-done.2.refs_2_, ...), custom_call_target="tpu_custom_call" | custom-call | flops 8589934592 | bytes 37748736 | tf_op jit(solution)/shard_map/proj/pallas_call | solution.py:381
  1349.7 35.7 %down.2 = (bf16[4096,2048]{1,0:T(8,128)(2,1)}, f32[1024,2048]{1,0:T(8,128)}) custom-call(bf16[4096,2048]{1,0:T(8,128)(2,1)} %all-gather.25.cloned.1.call-done.refs_8_.z_ref, bf16[8,1024,2048]{2,1,0:T(8,128)(2,1)} %bitcast.18, bf16[4096,1024]{1,0:T(8,128)(2,1)} %get-tuple-element.154.u_ref), custom_call_target="tpu_custom_call" | custom-call | flops 17179869184 | bytes 58720256 | tf_op jit(solution)/shard_map/down/pallas_call | solution.py:447
  1427.1 37.1 %down.3 = (bf16[4096,2048]{1,0:T(8,128)(2,1)}, bf16[512,2048]{1,0:T(8,128)(2,1)}, bf16[512,2048]{1,0:T(8,128)(2,1)}) custom-call(bf16[4096,2048]{1,0:T(8,128)(2,1)} %all-gather.27.cloned.1.call-done.refs_8_.z_ref, bf16[8,1024,2048]{2,1,0:T(8,128)(2,1)} %bitcast.20, bf16[4096,1024]{1,0:T(8,128)(2,1)} %get-tuple-element.155.u_ref, ...), custom_call_target="tpu_custom_call" | custom-call | flops 17179869184 | bytes 58720256 | tf_op jit(solution)/shard_map/down/pallas_call | solution.py:447
  1464.1 73.5 %rest.2 = (f32[2048,1024]{1,0:T(8,128)}, f32[8,2048]{1,0:T(8,128)}) custom-call(s32[1]{0:T(128)} %bitcast.me_ref, bf16[4096,2048]{1,0:T(8,128)(2,1)} %get-tuple-element.181.d_ref, f32[4096,1024]{1,0:T(8,128)} %get-tuple-element.182.p_ref, bf16[4096,2048]{1,0:T(8,128)(2,1)} %get-tuple-element.183.a_ref, bf16[8,1024,2048]{2,1,0:T(8,128)(2,1)} %bitcast.23, ...), custom_call_target="tpu_custom_call" | custom-call | flops 51539607552 | bytes 67108864 | tf_op jit(solution)/shard_map/rest/pallas_call | solution.py:579
  1537.6 74.5 %rest.3 = (bf16[1024,1024]{1,0:T(8,128)(2,1)}, bf16[1024,1024]{1,0:T(8,128)(2,1)}, f32[8,2048]{1,0:T(8,128)}) custom-call(s32[1]{0:T(128)} %bitcast.me_ref, bf16[4096,2048]{1,0:T(8,128)(2,1)} %get-tuple-element.175.d_ref, f32[4096,1024]{1,0:T(8,128)} %get-tuple-element.176.p_ref, bf16[4096,2048]{1,0:T(8,128)(2,1)} %get-tuple-element.177.a_ref, ...), custom_call_target="tpu_custom_call" | custom-call | flops 51539607552 | bytes 67108864 | tf_op jit(solution)/shard_map/rest/pallas_call | solution.py:579
  1668.4 41.4 %collective-permute-done.34.refs_8_ = bf16[256,2048]{1,0:T(8,128)(2,1)S(1)} collective-permute-done((bf16[256,2048]{1,0:T(8,128)(2,1)}, bf16[256,2048]{1,0:T(8,128)(2,1)S(1)}, u32[]{:S(2)}, u32[]{:S(2)}) %collective-permute-start.34) | collective-permute-done | bytes 1048608 | tf_op jit(solution)/shard_map/ppermute | solution.py:596
  1746.3 30.4 %collective-permute-done.22.refs_6_ = bf16[512,2048]{1,0:T(8,128)(2,1)S(1)} collective-permute-done((bf16[512,2048]{1,0:T(8,128)(2,1)}, bf16[512,2048]{1,0:T(8,128)(2,1)S(1)}, u32[]{:S(2)}, u32[]{:S(2)}) %collective-permute-start.22) | collective-permute-done | bytes 2097184 | tf_op jit(solution)/shard_map/ppermute | solution.py:596
  1786.6 35.2 %collective-permute-done.16.refs_0_ = bf16[1024,1024]{1,0:T(8,128)(2,1)} collective-permute-done((bf16[1024,1024]{1,0:T(8,128)(2,1)}, bf16[1024,1024]{1,0:T(8,128)(2,1)}, u32[]{:S(2)}, u32[]{:S(2)}) %collective-permute-start.16) | collective-permute-done | bytes 2097184 | tf_op jit(solution)/shard_map/ppermute | solution.py:596
  1832.7 34.0 %collective-permute-done.47.refs_2_ = bf16[1024,1024]{1,0:T(8,128)(2,1)} collective-permute-done((bf16[1024,1024]{1,0:T(8,128)(2,1)}, bf16[1024,1024]{1,0:T(8,128)(2,1)}, u32[]{:S(2)}, u32[]{:S(2)}) %collective-permute-start.47) | collective-permute-done | bytes 2097184 | tf_op jit(solution)/shard_map/ppermute | solution.py:596
  1923.9 25.8 %place.7.refs_4_ = f32[8192,2048]{1,0:T(8,128)} custom-call(s32[12]{0:T(128)} %stack.32.owner_ref, s32[12]{0:T(128)} %constant.38.clone.half_ref, bf16[512,2048]{1,0:T(8,128)(2,1)} %get-tuple-element.205.refs_0_, bf16[512,2048]{1,0:T(8,128)(2,1)} %copy-done.2, bf16[512,2048]{1,0:T(8,128)(2,1)} %get-tuple-element.207.refs_2_, bf16[512,2048]{1,0:T(8,128)(2,1)} %copy-done.3, ...), custom_call_target="tpu_custom_call" | custom-call | flops 12582912 | bytes 75497472 | tf_op jit(solution)/shard_map/place/pallas_call | solution.py:503
  1951.7 45.6 %collective-permute-done.42.refs_0_ = bf16[1024,1024]{1,0:T(8,128)(2,1)} collective-permute-done((bf16[1024,1024]{1,0:T(8,128)(2,1)}, bf16[1024,1024]{1,0:T(8,128)(2,1)}, u32[]{:S(2)}, u32[]{:S(2)}) %collective-permute-start.42) | collective-permute-done | bytes 2097184 | tf_op jit(solution)/shard_map/ppermute | solution.py:596
  (229 shorter events, 403.3 us)
Async XLA Ops:
  14.6 171.9 %all-gather.15.cloned.1.call-start = ((), (), s32[]{:S(2)}) async-start(), calls=%async_computation.6 | async-start | bytes 12582912 | tf_op jit(solution)/shard_map/all_gather | solution.py:655
  20.5 319.5 %reduce-scatter.5.cloned.1.call-start = ((), (), s32[]{:S(2)}) async-start(), calls=%async_computation.5 | async-start | bytes 12582912 | tf_op jit(solution)/shard_map/reduce_scatter | solution.py:667
  186.4 251.7 %reduce-scatter.9.cloned.1.call-start = ((), (), s32[]{:S(2)}) async-start(), calls=%async_computation.9 | async-start | bytes 12582912 | tf_op jit(solution)/shard_map/reduce_scatter | solution.py:670
  339.4 173.1 %all-gather.29.cloned.1.call-start = ((), (), s32[]{:S(2)}) async-start(), calls=%async_computation.16 | async-start | bytes 37748736 | tf_op jit(solution)/shard_map/all_gather | solution.py:663
  340.0 191.5 %all-gather.17.cloned.1.call-start = ((), (), s32[]{:S(2)}) async-start(), calls=%async_computation.7 | async-start | bytes 12582912 | tf_op jit(solution)/shard_map/all_gather | solution.py:655
  348.3 337.5 %all-gather.19.cloned.1.call-start = ((), (), s32[]{:S(2)}) async-start(), calls=%async_computation.10 | async-start | bytes 12582912 | tf_op jit(solution)/shard_map/all_gather | solution.py:655
  520.2 247.2 %reduce-scatter.7.cloned.1.call-start = ((), (), s32[]{:S(2)}) async-start(), calls=%async_computation.8 | async-start | bytes 12582912 | tf_op jit(solution)/shard_map/reduce_scatter | solution.py:667
  685.0 173.2 %all-gather.31.cloned.1.call-start = ((), (), s32[]{:S(2)}) async-start(), calls=%async_computation.17 | async-start | bytes 37748736 | tf_op jit(solution)/shard_map/all_gather | solution.py:665
  685.7 191.5 %all-gather.21.cloned.1.call-start = ((), (), s32[]{:S(2)}) async-start(), calls=%async_computation.11 | async-start | bytes 12582912 | tf_op jit(solution)/shard_map/all_gather | solution.py:655
  775.5 255.2 %all-gather.23.cloned.1.call-start = ((), (), s32[]{:S(2)}) async-start(), calls=%async_computation.13 | async-start | bytes 12582912 | tf_op jit(solution)/shard_map/all_gather | solution.py:655
  775.6 82.1 %collective-permute-start = (bf16[512,4096]{1,0:T(8,128)(2,1)}, bf16[512,4096]{1,0:T(8,128)(2,1)}, u32[]{:S(2)}, u32[]{:S(2)}) collective-permute-start(bf16[512,4096]{1,0:T(8,128)(2,1)} %mlp.13), channel_id=1, source_target_pairs={{0,1},{1,0},{2,3},{3,2},{4,5},{5,4},{6,7},{7,6}} | collective-permute-start | bytes 12582920 | tf_op jit(solution)/shard_map/ppermute | solution.py:596
  868.1 244.2 %reduce-scatter.11.cloned.1.call-start = ((), (), s32[]{:S(2)}) async-start(), calls=%async_computation.12 | async-start | bytes 12582912 | tf_op jit(solution)/shard_map/reduce_scatter | solution.py:667
  1030.7 276.3 %all-gather.25.cloned.1.call-start = ((), (), s32[]{:S(2)}) async-start(), calls=%async_computation.14 | async-start | bytes 18874368 | tf_op jit(solution)/shard_map/all_gather | solution.py:649
  1133.3 270.9 %all-gather.27.cloned.1.call-start = ((), (), s32[]{:S(2)}) async-start(), calls=%async_computation.15 | async-start | bytes 18874368 | tf_op jit(solution)/shard_map/all_gather | solution.py:649
  1133.3 81.8 %collective-permute-start.8 = (bf16[512,4096]{1,0:T(8,128)(2,1)}, bf16[512,4096]{1,0:T(8,128)(2,1)}, u32[]{:S(2)}, u32[]{:S(2)}) collective-permute-start(bf16[512,4096]{1,0:T(8,128)(2,1)} %mlp.16), channel_id=1, source_target_pairs={{0,1},{1,0},{2,3},{3,2},{4,5},{5,4},{6,7},{7,6}} | collective-permute-start | bytes 12582920 | tf_op jit(solution)/shard_map/ppermute | solution.py:596
  1308.7 95.5 %collective-permute-start.12 = (bf16[512,512]{1,0:T(8,128)(2,1)}, bf16[512,512]{1,0:T(8,128)(2,1)}, u32[]{:S(2)}, u32[]{:S(2)}) collective-permute-start(bf16[512,512]{1,0:T(8,128)(2,1)} %get-tuple-element.163), channel_id=1, source_target_pairs={{0,4},{1,5},{2,6},{3,7},{4,0},{5,1},{6,2},{7,3}} | collective-permute-start | bytes 1572872 | tf_op jit(solution)/shard_map/ppermute | solution.py:596
  1309.9 94.3 %collective-permute-start.13 = (bf16[512,512]{1,0:T(8,128)(2,1)}, bf16[512,512]{1,0:T(8,128)(2,1)}, u32[]{:S(2)}, u32[]{:S(2)}) collective-permute-start(bf16[512,512]{1,0:T(8,128)(2,1)} %get-tuple-element.164), channel_id=1, source_target_pairs={{0,5},{1,4},{2,7},{3,6},{4,1},{5,0},{6,3},{7,2}} | collective-permute-start | bytes 1572872 | tf_op jit(solution)/shard_map/ppermute | solution.py:596
  1310.5 93.7 %collective-permute-start.14 = (bf16[512,512]{1,0:T(8,128)(2,1)}, bf16[512,512]{1,0:T(8,128)(2,1)}, u32[]{:S(2)}, u32[]{:S(2)}) collective-permute-start(bf16[512,512]{1,0:T(8,128)(2,1)} %get-tuple-element.165), channel_id=1, source_target_pairs={{0,6},{1,7},{2,4},{3,5},{4,2},{5,3},{6,0},{7,1}} | collective-permute-start | bytes 1572872 | tf_op jit(solution)/shard_map/ppermute | solution.py:596
  1619.7 93.9 %collective-permute-start.20 = (bf16[512,2048]{1,0:T(8,128)(2,1)}, bf16[512,2048]{1,0:T(8,128)(2,1)}, u32[]{:S(2)}, u32[]{:S(2)}) collective-permute-start(bf16[512,2048]{1,0:T(8,128)(2,1)} %get-tuple-element.205.refs_0_), channel_id=1, source_target_pairs={{0,2},{1,3},{2,0},{3,1},{4,6},{5,7},{6,4},{7,5}} | collective-permute-start | bytes 6291464 | tf_op jit(solution)/shard_map/ppermute | solution.py:596
  1620.8 92.8 %collective-permute-start.26 = (bf16[512,2048]{1,0:T(8,128)(2,1)}, bf16[512,2048]{1,0:T(8,128)(2,1)}, u32[]{:S(2)}, u32[]{:S(2)}) collective-permute-start(bf16[512,2048]{1,0:T(8,128)(2,1)} %get-tuple-element.207.refs_2_), channel_id=1, source_target_pairs={{0,4},{1,5},{2,6},{3,7},{4,0},{5,1},{6,2},{7,3}} | collective-permute-start | bytes 6291464 | tf_op jit(solution)/shard_map/ppermute | solution.py:596
  1746.0 75.8 %collective-permute-start.16 = (bf16[1024,1024]{1,0:T(8,128)(2,1)}, bf16[1024,1024]{1,0:T(8,128)(2,1)}, u32[]{:S(2)}, u32[]{:S(2)}) collective-permute-start(bf16[1024,1024]{1,0:T(8,128)(2,1)} %get-tuple-element.237.refs_0_), channel_id=1, source_target_pairs={{0,2},{1,3},{2,0},{3,1},{4,6},{5,7},{6,4},{7,5}} | collective-permute-start | bytes 6291464 | tf_op jit(solution)/shard_map/ppermute | solution.py:596
  1777.9 88.9 %collective-permute-start.47 = (bf16[1024,1024]{1,0:T(8,128)(2,1)}, bf16[1024,1024]{1,0:T(8,128)(2,1)}, u32[]{:S(2)}, u32[]{:S(2)}) collective-permute-start(bf16[1024,1024]{1,0:T(8,128)(2,1)} %get-tuple-element.239.refs_2_), channel_id=1, source_target_pairs={{0,2},{1,3},{2,0},{3,1},{4,6},{5,7},{6,4},{7,5}} | collective-permute-start | bytes 6291464 | tf_op jit(solution)/shard_map/ppermute | solution.py:596
  1778.3 92.2 %collective-permute-start.49 = (bf16[1024,1024]{1,0:T(8,128)(2,1)}, bf16[1024,1024]{1,0:T(8,128)(2,1)}, u32[]{:S(2)}, u32[]{:S(2)}) collective-permute-start(bf16[1024,1024]{1,0:T(8,128)(2,1)} %get-tuple-element.237.refs_0_), channel_id=1, source_target_pairs={{0,4},{1,5},{2,6},{3,7},{4,0},{5,1},{6,2},{7,3}} | collective-permute-start | bytes 6291464 | tf_op jit(solution)/shard_map/ppermute | solution.py:596
  1778.6 96.9 %collective-permute-start.21 = (bf16[512,2048]{1,0:T(8,128)(2,1)}, bf16[512,2048]{1,0:T(8,128)(2,1)S(1)}, u32[]{:S(2)}, u32[]{:S(2)}) collective-permute-start(bf16[512,2048]{1,0:T(8,128)(2,1)} %collective-permute-done.20.refs_4_), channel_id=1, source_target_pairs={{0,1},{1,0},{2,3},{3,2},{4,5},{5,4},{6,7},{7,6}} | collective-permute-start | bytes 6291464 | tf_op jit(solution)/shard_map/ppermute | solution.py:596
  (74 other events, 3356.6 us)
Sparse Core Ops, SparseCore 0:
  14.8 19.2 all-gather.12
  36.1 18.2 all-gather.14
  186.6 14.8 reduce-scatter.4
  339.5 14.8 reduce-scatter.8
  356.1 156.3 all-gather.28
  514.4 17.0 all-gather.16
  533.6 18.2 all-gather.18
  685.1 14.8 reduce-scatter.6
  701.8 156.3 all-gather.30
  860.1 17.0 all-gather.20
  878.7 18.2 all-gather.22
  1030.8 14.8 reduce-scatter.10
  1133.4 85.3 all-gather.24
  1238.5 165.6 all-gather.26

commit v6 on v5

--- a/solution.py
+++ b/solution.py
@@ -11,6 +11,8 @@
 EPS = 1e-6
 BF16 = jnp.bfloat16
 F32 = jnp.float32
+GELU_SCALE = 0.7978845608028654
+GELU_BEND = 0.044715
 VMEM_CAP = 64 * 1024 * 1024 - 65536
 AXES = ("data", "model")
 
@@ -92,7 +94,7 @@
             a_copy(r).wait()
             first[part, :] = dot(a_ref[part, :], up_ref[0, :, :half])
             second[part, :] = dot(a_ref[part, :], up_ref[0, :, half:])
-        act[0, :, :half] = jax.nn.gelu(first[...]).astype(BF16)
+        act[0, :, :half] = gelu(first[...]).astype(BF16)
 
     @pl.when((j > 0) & (j < steps))
     def _():
@@ -102,15 +104,15 @@
 
         down_copy(j).start()
         up_copy(j).wait()
-        act[1 - now, :, half:] = jax.nn.gelu(second[...]).astype(BF16)
+        act[1 - now, :, half:] = gelu(second[...]).astype(BF16)
         first[...] = dot(a_ref[...], up_ref[now, :, :half])
         for part in cut(rows, parts):
-            act[now, part, :half] = jax.nn.gelu(first[part, :]).astype(BF16)
+            act[now, part, :half] = gelu(first[part, :]).astype(BF16)
             second[part, :] = dot(a_ref[part, :], up_ref[now, :, half:])
 
     @pl.when(j == steps)
     def _():
-        act[1 - now, :, half:] = jax.nn.gelu(second[...]).astype(BF16)
+        act[1 - now, :, half:] = gelu(second[...]).astype(BF16)
 
     def down(first_tile, last_tile):
         down_copy(j - 1).wait()
@@ -208,8 +210,9 @@
     a_ref[...] = (state * inv * g_ref[...]).astype(BF16)
 
 
-def teacher_norm(hidden, delta, gains, layer, which=0, block=128):
+def teacher_norm(hidden, delta, gains, layer, which=0, size=2**18):
     rows, width = hidden.shape[-2:]
+    block = size // width
     spec = pl.BlockSpec((block, width), lambda i: (i, 0))
     source = spec if hidden.ndim == 2 else pl.BlockSpec((None, block, width), lambda i: (which, i, 0))
     gain_spec = fixed(1, width)
@@ -235,7 +238,7 @@
     for part in cut(s_ref.shape[0], s_ref.shape[0] // sub):
         pre = dot(a_ref[part, :], w_ref[...])
         p_ref[part, :] = pre
-        u_ref[part, :] = jax.nn.gelu(pre).astype(BF16)
+        u_ref[part, :] = gelu(pre).astype(BF16)
 
 
 def pre_of(me, states, gain, weights, parity, cols, block=512, sub=256):
@@ -274,7 +277,7 @@
     return z_ref[part, :].astype(F32) - unit, unit, inv
 
 
-def finish_kernel(count, size, me_ref, h_ref, *refs):
+def finish_kernel(count, size, wide, me_ref, h_ref, *refs):
     parts = refs[:count]
     q_ref = refs[count]
     feats = refs[-2 - size : -2]
@@ -284,38 +287,36 @@
     if count > 1:
         delta = (delta + parts[1][...].astype(F32)).astype(BF16).astype(F32)
     feat = (h_ref[...].astype(F32) + delta).astype(BF16)
-    for bits in range(size):
-
-        @pl.when(me_ref[0] ^ k == bits)
-        def _():
-            feats[bits][...] = feat
-
-    term = dot(feat, q_ref[...])
+    for own, cols in enumerate(cut(feat.shape[1], wide)):
+        for bits in range(size):
+
+            @pl.when(me_ref[0] ^ (k * wide + own) == bits)
+            def _():
+                feats[bits][...] = feat[:, cols]
 
     @pl.when(k == 0)
     def _():
-        acc[...] = term
-
-    @pl.when((k > 0) & (k < size - 1))
-    def _():
-        acc[...] += term
-
-    @pl.when(k == size - 1)
-    def _():
-        z_ref[...] = (acc[...] + term).astype(BF16)
-
-
-def finish_part(me, hidden, delta, proj, size):
+        acc[...] = jnp.zeros_like(acc)
+
+    acc[...] += dot(feat, q_ref[...])
+
+    @pl.when(k == pl.num_programs(0) - 1)
+    def _():
+        z_ref[...] = acc[...].astype(BF16)
+
+
+def finish_part(me, hidden, delta, proj, size, wide=2):
     rows, width = hidden.shape
     cols = width // size
     out = proj.shape[2]
-    spec = pl.BlockSpec((rows, cols), lambda k, me: (0, k))
+    deep = cols * wide
+    spec = pl.BlockSpec((rows, deep), lambda k, me: (0, k))
     return pl.pallas_call(
-        functools.partial(finish_kernel, len(delta), size),
+        functools.partial(finish_kernel, len(delta), size, wide),
         grid_spec=pltpu.PrefetchScalarGridSpec(
             num_scalar_prefetch=1,
-            grid=(size,),
-            in_specs=[spec] * (1 + len(delta)) + [pl.BlockSpec((None, cols, out), lambda k, me: (0, k, 0))],
+            grid=(size // wide,),
+            in_specs=[spec] * (1 + len(delta)) + [pl.BlockSpec((None, deep, out), lambda k, me: (0, k, 0))],
             out_specs=[fixed(rows, cols)] * size + [fixed(rows, out)],
             scratch_shapes=[pltpu.VMEM((rows, out), F32)],
         ),
@@ -517,11 +518,15 @@
     )(*args)
 
 
+def gelu(pre):
+    half = 0.5 * pre
+    return half + half * jnp.tanh(pre * (GELU_SCALE + GELU_SCALE * GELU_BEND * (pre * pre)))
+
+
 def gelu_slope(pre):
-    scale = 0.7978845608028654
     square = pre * pre
-    bend = jnp.tanh(scale * pre * (1.0 + 0.044715 * square))
-    return 0.5 * (1.0 + bend) + (0.5 * scale) * pre * (1.0 - bend * bend) * (1.0 + 0.134145 * square)
+    bend = jnp.tanh(GELU_SCALE * pre * (1.0 + GELU_BEND * square))
+    return 0.5 * (1.0 + bend) + (0.5 * GELU_SCALE) * pre * (1.0 - bend * bend) * (1.0 + 3.0 * GELU_BEND * square)
 
 
 def rest_kernel(first, last, sub, me_ref, d_ref, p_ref, a_ref, s_ref, up_ref, down_ref, *refs):
@@ -658,9 +663,10 @@
             return mlp(act, teacher_up_w, teacher_down, layer, **window)
 
         acts = [normed(c, (), 0)[1] for c in range(2)]
+        own_act = teacher_norm(own, (), student_gain, 0)[1]
         for layer in range(n_layers):
             if layer == 0:
-                all_in = lax.all_gather(after(own, acts[0]), AXES, axis=0, tiled=False)
+                all_in = lax.all_gather(after(own, (acts[0], own_act)), AXES, axis=0, tiled=False)
             if layer == 1:
                 all_out = lax.all_gather(after(own_out, acts[0]), AXES, axis=0, tiled=False)
             partial = teach(acts[0], layer)
@@ -669,8 +675,7 @@
                 partial = teach(acts[1], layer)
                 delta_1 = (lax.psum_scatter(partial, "model", scatter_dimension=0, tiled=True),)
                 act, acts[0] = normed(0, after(delta_0, partial), layer + 1)
-                own_act = teacher_norm(after(own, act), (), student_gain, 0)[1]
-                own_out = mlp(own_act, student_up, student_down, 0, own)
+                own_out = mlp(after(own_act, act), student_up, student_down, 0, own)
                 delta_1 = after(delta_1, (own_out, all_in))
             else:
                 rows = acts[1].shape[0] // 2

time: 2070 us -> 2060 us (level)
  no operation moved by 1% of the time
where the time goes in v6:
time: 2060 us; the launch traced here: 2050 us
  Pallas kernels  1540 us (75%)
  waiting for transfers between devices  407 us (20%)
  starting transfers between devices  78.5 us (4%)
    pallas_call x9, Pallas kernels, mlp(): pl.pallas_call(functools.partial(mlp_kernel, layer, steps, wide, state is...  1010 us
    ppermute x61, waiting for transfers between devices, flip(): return lax.ppermute(value, AXES, [(i, i ^ bits) for i in range(size)])  286 us
    pallas_call x2, Pallas kernels, rest_part(): pl.pallas_call(functools.partial(rest_kernel, total is None, last, sub),...  148 us
    pallas_call x6, Pallas kernels, place(): pl.pallas_call(functools.partial(place_kernel, count, ahead), grid_spec=p...  89.1 us
    ppermute x61, starting transfers between devices, flip(): return lax.ppermute(value, AXES, [(i, i ^ bits) for i in range(size)])  77.9 us
    all_gather x1, waiting for transfers between devices, step(): lax.all_gather(after(own, (acts[0], own_act)), AXES, axis=0, tiled=False)  73.6 us
    pallas_call x2, Pallas kernels, down_part_of(): pl.pallas_call(functools.partial(down_kernel, scale, total is None, last,...  72.6 us
    pallas_call x2, Pallas kernels, pre_of(): pl.pallas_call(functools.partial(pre_kernel, sub), grid_spec=pltpu.Prefet...  61.4 us
  transfers between devices with their start and end apart: 75, of which 23 were waited for; matrix products, arithmetic and copies ran while one was open for 0% of the time, Pallas kernels for 63%

profile of v6, /device:TPU:1, one launch (start us, length us, event | category | flops | bytes accessed | tf_op | source)
XLA Modules:
  0.0 2048.9 jit_solution(16683894859865578808)
XLA Ops:
  35.7 151.5 %mlp.9 = bf16[1024,4096]{1,0:T(8,128)(2,1)} custom-call(s32[1]{0:T(128)} %constant.10.clone.1.where_ref, bf16[1024,4096]{1,0:T(8,128)(2,1)} %all-gather.13.cloned.1.call-done.refs_0_, bf16[3,4096,8192]{2,1,0:T(8,128)(2,1)} %refs_1_.19, bf16[3,8192,4096]{2,1,0:T(8,128)(2,1)} %refs_2_.18), custom_call_target="tpu_custom_call" | custom-call | flops 137438953472 | bytes 150994944 | tf_op jit(solution)/shard_map/mlp/pallas_call | solution.py:175
  187.3 152.0 %mlp.10 = bf16[1024,4096]{1,0:T(8,128)(2,1)} custom-call(s32[1]{0:T(128)} %constant.10.clone.1.where_ref, bf16[1024,4096]{1,0:T(8,128)(2,1)} %all-gather.15.cloned.1.call-done.refs_0_, bf16[3,4096,8192]{2,1,0:T(8,128)(2,1)} %refs_1_.19, bf16[3,8192,4096]{2,1,0:T(8,128)(2,1)} %refs_2_.18), custom_call_target="tpu_custom_call" | custom-call | flops 137438953472 | bytes 150994944 | tf_op jit(solution)/shard_map/mlp/pallas_call | solution.py:175
  357.5 81.2 %mlp.12 = bf16[1024,2048]{1,0:T(8,128)(2,1)} custom-call(s32[1]{0:T(128)} %constant.10.clone.1.where_ref, bf16[1024,2048]{1,0:T(8,128)(2,1)} %norm.5.refs_0_, bf16[1,2048,8192]{2,1,0:T(8,128)(2,1)} %up_ref.3, bf16[1,8192,2048]{2,1,0:T(8,128)(2,1)} %down_ref.3, bf16[1024,2048]{1,0:T(8,128)(2,1)} %bitcast.28), custom_call_target="tpu_custom_call" | custom-call | flops 68719476736 | bytes 75497472 | tf_op jit(solution)/shard_map/mlp/pallas_call | solution.py:175
  438.8 73.6 %all-gather.29.cloned.1.call-done = bf16[8192,2048]{1,0:T(8,128)(2,1)} async-done(((bf16[1024,2048]{1,0:T(8,128)(2,1)}), bf16[8192,2048]{1,0:T(8,128)(2,1)}) %all-gather.29.cloned.1.call-update) | async-done | bytes 33554448 | tf_op jit(solution)/shard_map/all_gather | solution.py:669
  531.4 152.6 %mlp.11 = bf16[1024,4096]{1,0:T(8,128)(2,1)} custom-call(s32[1]{0:T(128)} %constant.10.clone.1.where_ref, bf16[1024,4096]{1,0:T(8,128)(2,1)} %all-gather.17.cloned.1.call-done.refs_0_, bf16[3,4096,8192]{2,1,0:T(8,128)(2,1)} %refs_1_.19, bf16[3,8192,4096]{2,1,0:T(8,128)(2,1)} %refs_2_.18), custom_call_target="tpu_custom_call" | custom-call | flops 137438953472 | bytes 150994944 | tf_op jit(solution)/shard_map/mlp/pallas_call | solution.py:175
  684.9 81.2 %mlp.13 = bf16[512,4096]{1,0:T(8,128)(2,1)} custom-call(s32[1]{0:T(128)} %bitcast.1.where_ref, bf16[1024,4096]{1,0:T(8,128)(2,1)} %all-gather.19.cloned.1.call-done.refs_0_, bf16[3,4096,8192]{2,1,0:T(8,128)(2,1)} %refs_1_.19, bf16[3,8192,4096]{2,1,0:T(8,128)(2,1)} %refs_2_.18), custom_call_target="tpu_custom_call" | custom-call | flops 68719476736 | bytes 142606336 | tf_op jit(solution)/shard_map/mlp/pallas_call | solution.py:175
  776.6 81.5 %mlp.15.refs_0_ = bf16[512,4096]{1,0:T(8,128)(2,1)} custom-call(s32[1]{0:T(128)} %bitcast.4.where_ref, bf16[1024,4096]{1,0:T(8,128)(2,1)} %all-gather.19.cloned.1.call-done.refs_0_, bf16[3,4096,8192]{2,1,0:T(8,128)(2,1)} %refs_1_.19, bf16[3,8192,4096]{2,1,0:T(8,128)(2,1)} %refs_2_.18), custom_call_target="tpu_custom_call" | custom-call | flops 68719476736 | bytes 142606336 | tf_op jit(solution)/shard_map/mlp/pallas_call | solution.py:175
  876.3 152.6 %mlp.14 = bf16[1024,4096]{1,0:T(8,128)(2,1)} custom-call(s32[1]{0:T(128)} %constant.10.clone.1.where_ref, bf16[1024,4096]{1,0:T(8,128)(2,1)} %all-gather.21.cloned.1.call-done.refs_0_, bf16[3,4096,8192]{2,1,0:T(8,128)(2,1)} %refs_1_.19, bf16[3,8192,4096]{2,1,0:T(8,128)(2,1)} %refs_2_.18), custom_call_target="tpu_custom_call" | custom-call | flops 137438953472 | bytes 150994944 | tf_op jit(solution)/shard_map/mlp/pallas_call | solution.py:175
  1029.0 81.1 %mlp.16 = bf16[512,4096]{1,0:T(8,128)(2,1)} custom-call(s32[1]{0:T(128)} %bitcast.1.where_ref, bf16[1024,4096]{1,0:T(8,128)(2,1)} %all-gather.23.cloned.1.call-done.refs_0_, bf16[3,4096,8192]{2,1,0:T(8,128)(2,1)} %refs_1_.19, bf16[3,8192,4096]{2,1,0:T(8,128)(2,1)} %refs_2_.18), custom_call_target="tpu_custom_call" | custom-call | flops 68719476736 | bytes 142606336 | tf_op jit(solution)/shard_map/mlp/pallas_call | solution.py:175
  1129.2 81.1 %mlp.17.refs_0_ = bf16[512,4096]{1,0:T(8,128)(2,1)} custom-call(s32[1]{0:T(128)} %bitcast.4.where_ref, bf16[1024,4096]{1,0:T(8,128)(2,1)} %all-gather.23.cloned.1.call-done.refs_0_, bf16[3,4096,8192]{2,1,0:T(8,128)(2,1)} %refs_1_.19, bf16[3,8192,4096]{2,1,0:T(8,128)(2,1)} %refs_2_.18), custom_call_target="tpu_custom_call" | custom-call | flops 68719476736 | bytes 142606336 | tf_op jit(solution)/shard_map/mlp/pallas_call | solution.py:175
  1235.2 31.2 %pre.3 = (bf16[4096,2048]{1,0:T(8,128)(2,1)}, f32[4096,1024]{1,0:T(8,128)}, bf16[4096,1024]{1,0:T(8,128)(2,1)}) custom-call(s32[1]{0:T(128)} %bitcast.me_ref, bf16[8,1024,2048]{2,1,0:T(8,128)(2,1)} %bitcast.21, f32[1,2048]{1,0:T(1,128)} %g_ref.5, bf16[1,2048,8192]{2,1,0:T(8,128)(2,1)} %up_ref.3), custom_call_target="tpu_custom_call" | custom-call | flops 17179869184 | bytes 58720256 | tf_op jit(solution)/shard_map/pre/pallas_call | solution.py:250
  1269.1 30.2 %pre.2 = (bf16[4096,2048]{1,0:T(8,128)(2,1)}, f32[4096,1024]{1,0:T(8,128)}, bf16[4096,1024]{1,0:T(8,128)(2,1)}) custom-call(s32[1]{0:T(128)} %bitcast.me_ref, bf16[8,1024,2048]{2,1,0:T(8,128)(2,1)} %bitcast.22, f32[1,2048]{1,0:T(1,128)} %g_ref.5, bf16[1,2048,8192]{2,1,0:T(8,128)(2,1)} %up_ref.3), custom_call_target="tpu_custom_call" | custom-call | flops 17179869184 | bytes 58720256 | tf_op jit(solution)/shard_map/pre/pallas_call | solution.py:250
  1304.9 23.7 %proj.2 = (f32[512,2048]{1,0:T(8,128)}, f32[8,2048]{1,0:T(8,128)}) custom-call(s32[1]{0:T(128)} %bitcast.me_ref, bf16[512,512]{1,0:T(8,128)(2,1)} %get-tuple-element.141.refs_0_, bf16[512,512]{1,0:T(8,128)(2,1)} %collective-permute-done.1.refs_1_, bf16[512,512]{1,0:T(8,128)(2,1)} %collective-permute-done.2.refs_2_, ...), custom_call_target="tpu_custom_call" | custom-call | flops 8589934592 | bytes 37748736 | tf_op jit(solution)/shard_map/proj/pallas_call | solution.py:382
  1341.7 35.3 %down.2 = (bf16[4096,2048]{1,0:T(8,128)(2,1)}, f32[1024,2048]{1,0:T(8,128)}) custom-call(bf16[4096,2048]{1,0:T(8,128)(2,1)} %all-gather.25.cloned.1.call-done.refs_8_.z_ref, bf16[8,1024,2048]{2,1,0:T(8,128)(2,1)} %bitcast.18, bf16[4096,1024]{1,0:T(8,128)(2,1)} %get-tuple-element.154.u_ref), custom_call_target="tpu_custom_call" | custom-call | flops 17179869184 | bytes 58720256 | tf_op jit(solution)/shard_map/down/pallas_call | solution.py:448
  1396.6 22.8 %proj.3 = (bf16[256,2048]{1,0:T(8,128)(2,1)}, bf16[256,2048]{1,0:T(8,128)(2,1)}, f32[8,2048]{1,0:T(8,128)}) custom-call(s32[1]{0:T(128)} %bitcast.me_ref, bf16[512,512]{1,0:T(8,128)(2,1)} %get-tuple-element.159.refs_0_, bf16[512,512]{1,0:T(8,128)(2,1)} %collective-permute-done.9.refs_1_, bf16[512,512]{1,0:T(8,128)(2,1)} %collective-permute-done.10.refs_2_, ...), custom_call_target="tpu_custom_call" | custom-call | flops 8589934592 | bytes 37748736 | tf_op jit(solution)/shard_map/proj/pallas_call | solution.py:382
  1419.4 37.3 %down.3 = (bf16[4096,2048]{1,0:T(8,128)(2,1)}, bf16[512,2048]{1,0:T(8,128)(2,1)}, bf16[512,2048]{1,0:T(8,128)(2,1)}) custom-call(bf16[4096,2048]{1,0:T(8,128)(2,1)} %all-gather.27.cloned.1.call-done.refs_8_.z_ref, bf16[8,1024,2048]{2,1,0:T(8,128)(2,1)} %bitcast.20, bf16[4096,1024]{1,0:T(8,128)(2,1)} %get-tuple-element.155.u_ref, ...), custom_call_target="tpu_custom_call" | custom-call | flops 17179869184 | bytes 58720256 | tf_op jit(solution)/shard_map/down/pallas_call | solution.py:448
  1456.6 73.3 %rest.2 = (f32[2048,1024]{1,0:T(8,128)}, f32[8,2048]{1,0:T(8,128)}) custom-call(s32[1]{0:T(128)} %bitcast.me_ref, bf16[4096,2048]{1,0:T(8,128)(2,1)} %get-tuple-element.181.d_ref, f32[4096,1024]{1,0:T(8,128)} %get-tuple-element.182.p_ref, bf16[4096,2048]{1,0:T(8,128)(2,1)} %get-tuple-element.183.a_ref, bf16[8,1024,2048]{2,1,0:T(8,128)(2,1)} %bitcast.23, ...), custom_call_target="tpu_custom_call" | custom-call | flops 51539607552 | bytes 67108864 | tf_op jit(solution)/shard_map/rest/pallas_call | solution.py:584
  1530.0 74.5 %rest.3 = (bf16[1024,1024]{1,0:T(8,128)(2,1)}, bf16[1024,1024]{1,0:T(8,128)(2,1)}, f32[8,2048]{1,0:T(8,128)}) custom-call(s32[1]{0:T(128)} %bitcast.me_ref, bf16[4096,2048]{1,0:T(8,128)(2,1)} %get-tuple-element.175.d_ref, f32[4096,1024]{1,0:T(8,128)} %get-tuple-element.176.p_ref, bf16[4096,2048]{1,0:T(8,128)(2,1)} %get-tuple-element.177.a_ref, ...), custom_call_target="tpu_custom_call" | custom-call | flops 51539607552 | bytes 67108864 | tf_op jit(solution)/shard_map/rest/pallas_call | solution.py:584
  1660.8 41.3 %collective-permute-done.34.refs_8_ = bf16[256,2048]{1,0:T(8,128)(2,1)S(1)} collective-permute-done((bf16[256,2048]{1,0:T(8,128)(2,1)}, bf16[256,2048]{1,0:T(8,128)(2,1)S(1)}, u32[]{:S(2)}, u32[]{:S(2)}) %collective-permute-start.34) | collective-permute-done | bytes 1048608 | tf_op jit(solution)/shard_map/ppermute | solution.py:601
  1738.7 30.7 %collective-permute-done.22.refs_6_ = bf16[512,2048]{1,0:T(8,128)(2,1)S(1)} collective-permute-done((bf16[512,2048]{1,0:T(8,128)(2,1)}, bf16[512,2048]{1,0:T(8,128)(2,1)S(1)}, u32[]{:S(2)}, u32[]{:S(2)}) %collective-permute-start.22) | collective-permute-done | bytes 2097184 | tf_op jit(solution)/shard_map/ppermute | solution.py:601
  1779.0 35.4 %collective-permute-done.16.refs_0_ = bf16[1024,1024]{1,0:T(8,128)(2,1)} collective-permute-done((bf16[1024,1024]{1,0:T(8,128)(2,1)}, bf16[1024,1024]{1,0:T(8,128)(2,1)}, u32[]{:S(2)}, u32[]{:S(2)}) %collective-permute-start.16) | collective-permute-done | bytes 2097184 | tf_op jit(solution)/shard_map/ppermute | solution.py:601
  1825.3 34.0 %collective-permute-done.47.refs_2_ = bf16[1024,1024]{1,0:T(8,128)(2,1)} collective-permute-done((bf16[1024,1024]{1,0:T(8,128)(2,1)}, bf16[1024,1024]{1,0:T(8,128)(2,1)}, u32[]{:S(2)}, u32[]{:S(2)}) %collective-permute-start.47) | collective-permute-done | bytes 2097184 | tf_op jit(solution)/shard_map/ppermute | solution.py:601
  1916.2 25.8 %place.7.refs_4_ = f32[8192,2048]{1,0:T(8,128)} custom-call(s32[12]{0:T(128)} %stack.32.owner_ref, s32[12]{0:T(128)} %constant.38.clone.half_ref, bf16[512,2048]{1,0:T(8,128)(2,1)} %get-tuple-element.205.refs_0_, bf16[512,2048]{1,0:T(8,128)(2,1)} %copy-done.2, bf16[512,2048]{1,0:T(8,128)(2,1)} %get-tuple-element.207.refs_2_, bf16[512,2048]{1,0:T(8,128)(2,1)} %copy-done.3, ...), custom_call_target="tpu_custom_call" | custom-call | flops 12582912 | bytes 75497472 | tf_op jit(solution)/shard_map/place/pallas_call | solution.py:504
  1944.1 45.5 %collective-permute-done.42.refs_0_ = bf16[1024,1024]{1,0:T(8,128)(2,1)} collective-permute-done((bf16[1024,1024]{1,0:T(8,128)(2,1)}, bf16[1024,1024]{1,0:T(8,128)(2,1)}, u32[]{:S(2)}, u32[]{:S(2)}) %collective-permute-start.42) | collective-permute-done | bytes 2097184 | tf_op jit(solution)/shard_map/ppermute | solution.py:601
  (229 shorter events, 402.9 us)
Async XLA Ops:
  16.3 171.0 %all-gather.15.cloned.1.call-start = ((), (), s32[]{:S(2)}) async-start(), calls=%async_computation.6 | async-start | bytes 12582912 | tf_op jit(solution)/shard_map/all_gather | solution.py:660
  24.0 323.1 %reduce-scatter.5.cloned.1.call-start = ((), (), s32[]{:S(2)}) async-start(), calls=%async_computation.5 | async-start | bytes 12582912 | tf_op jit(solution)/shard_map/reduce_scatter | solution.py:673
  187.2 251.6 %reduce-scatter.9.cloned.1.call-start = ((), (), s32[]{:S(2)}) async-start(), calls=%async_computation.9 | async-start | bytes 12582912 | tf_op jit(solution)/shard_map/reduce_scatter | solution.py:676
  339.3 173.0 %all-gather.29.cloned.1.call-start = ((), (), s32[]{:S(2)}) async-start(), calls=%async_computation.16 | async-start | bytes 37748736 | tf_op jit(solution)/shard_map/all_gather | solution.py:669
  346.9 184.5 %all-gather.17.cloned.1.call-start = ((), (), s32[]{:S(2)}) async-start(), calls=%async_computation.7 | async-start | bytes 12582912 | tf_op jit(solution)/shard_map/all_gather | solution.py:660
  357.5 327.4 %all-gather.19.cloned.1.call-start = ((), (), s32[]{:S(2)}) async-start(), calls=%async_computation.10 | async-start | bytes 12582912 | tf_op jit(solution)/shard_map/all_gather | solution.py:660
  522.3 243.8 %reduce-scatter.7.cloned.1.call-start = ((), (), s32[]{:S(2)}) async-start(), calls=%async_computation.8 | async-start | bytes 12582912 | tf_op jit(solution)/shard_map/reduce_scatter | solution.py:673
  684.0 174.1 %all-gather.31.cloned.1.call-start = ((), (), s32[]{:S(2)}) async-start(), calls=%async_computation.17 | async-start | bytes 37748736 | tf_op jit(solution)/shard_map/all_gather | solution.py:671
  684.8 191.5 %all-gather.21.cloned.1.call-start = ((), (), s32[]{:S(2)}) async-start(), calls=%async_computation.11 | async-start | bytes 12582912 | tf_op jit(solution)/shard_map/all_gather | solution.py:660
  776.3 252.7 %all-gather.23.cloned.1.call-start = ((), (), s32[]{:S(2)}) async-start(), calls=%async_computation.13 | async-start | bytes 12582912 | tf_op jit(solution)/shard_map/all_gather | solution.py:660
  776.4 81.8 %collective-permute-start = (bf16[512,4096]{1,0:T(8,128)(2,1)}, bf16[512,4096]{1,0:T(8,128)(2,1)}, u32[]{:S(2)}, u32[]{:S(2)}) collective-permute-start(bf16[512,4096]{1,0:T(8,128)(2,1)} %mlp.13), channel_id=1, source_target_pairs={{0,1},{1,0},{2,3},{3,2},{4,5},{5,4},{6,7},{7,6}} | collective-permute-start | bytes 12582920 | tf_op jit(solution)/shard_map/ppermute | solution.py:601
  869.9 240.3 %reduce-scatter.11.cloned.1.call-start = ((), (), s32[]{:S(2)}) async-start(), calls=%async_computation.12 | async-start | bytes 12582912 | tf_op jit(solution)/shard_map/reduce_scatter | solution.py:673
  1028.9 270.4 %all-gather.25.cloned.1.call-start = ((), (), s32[]{:S(2)}) async-start(), calls=%async_computation.14 | async-start | bytes 18874368 | tf_op jit(solution)/shard_map/all_gather | solution.py:654
  1128.8 267.7 %all-gather.27.cloned.1.call-start = ((), (), s32[]{:S(2)}) async-start(), calls=%async_computation.15 | async-start | bytes 18874368 | tf_op jit(solution)/shard_map/all_gather | solution.py:654
  1128.9 81.4 %collective-permute-start.8 = (bf16[512,4096]{1,0:T(8,128)(2,1)}, bf16[512,4096]{1,0:T(8,128)(2,1)}, u32[]{:S(2)}, u32[]{:S(2)}) collective-permute-start(bf16[512,4096]{1,0:T(8,128)(2,1)} %mlp.16), channel_id=1, source_target_pairs={{0,1},{1,0},{2,3},{3,2},{4,5},{5,4},{6,7},{7,6}} | collective-permute-start | bytes 12582920 | tf_op jit(solution)/shard_map/ppermute | solution.py:601
  1301.0 95.5 %collective-permute-start.12 = (bf16[512,512]{1,0:T(8,128)(2,1)}, bf16[512,512]{1,0:T(8,128)(2,1)}, u32[]{:S(2)}, u32[]{:S(2)}) collective-permute-start(bf16[512,512]{1,0:T(8,128)(2,1)} %get-tuple-element.163), channel_id=1, source_target_pairs={{0,4},{1,5},{2,6},{3,7},{4,0},{5,1},{6,2},{7,3}} | collective-permute-start | bytes 1572872 | tf_op jit(solution)/shard_map/ppermute | solution.py:601
  1302.4 94.2 %collective-permute-start.13 = (bf16[512,512]{1,0:T(8,128)(2,1)}, bf16[512,512]{1,0:T(8,128)(2,1)}, u32[]{:S(2)}, u32[]{:S(2)}) collective-permute-start(bf16[512,512]{1,0:T(8,128)(2,1)} %get-tuple-element.164), channel_id=1, source_target_pairs={{0,5},{1,4},{2,7},{3,6},{4,1},{5,0},{6,3},{7,2}} | collective-permute-start | bytes 1572872 | tf_op jit(solution)/shard_map/ppermute | solution.py:601
  1303.0 93.5 %collective-permute-start.14 = (bf16[512,512]{1,0:T(8,128)(2,1)}, bf16[512,512]{1,0:T(8,128)(2,1)}, u32[]{:S(2)}, u32[]{:S(2)}) collective-permute-start(bf16[512,512]{1,0:T(8,128)(2,1)} %get-tuple-element.165), channel_id=1, source_target_pairs={{0,6},{1,7},{2,4},{3,5},{4,2},{5,3},{6,0},{7,1}} | collective-permute-start | bytes 1572872 | tf_op jit(solution)/shard_map/ppermute | solution.py:601
  1612.0 93.9 %collective-permute-start.20 = (bf16[512,2048]{1,0:T(8,128)(2,1)}, bf16[512,2048]{1,0:T(8,128)(2,1)}, u32[]{:S(2)}, u32[]{:S(2)}) collective-permute-start(bf16[512,2048]{1,0:T(8,128)(2,1)} %get-tuple-element.205.refs_0_), channel_id=1, source_target_pairs={{0,2},{1,3},{2,0},{3,1},{4,6},{5,7},{6,4},{7,5}} | collective-permute-start | bytes 6291464 | tf_op jit(solution)/shard_map/ppermute | solution.py:601
  1613.4 92.6 %collective-permute-start.26 = (bf16[512,2048]{1,0:T(8,128)(2,1)}, bf16[512,2048]{1,0:T(8,128)(2,1)}, u32[]{:S(2)}, u32[]{:S(2)}) collective-permute-start(bf16[512,2048]{1,0:T(8,128)(2,1)} %get-tuple-element.207.refs_2_), channel_id=1, source_target_pairs={{0,4},{1,5},{2,6},{3,7},{4,0},{5,1},{6,2},{7,3}} | collective-permute-start | bytes 6291464 | tf_op jit(solution)/shard_map/ppermute | solution.py:601
  1738.5 75.9 %collective-permute-start.16 = (bf16[1024,1024]{1,0:T(8,128)(2,1)}, bf16[1024,1024]{1,0:T(8,128)(2,1)}, u32[]{:S(2)}, u32[]{:S(2)}) collective-permute-start(bf16[1024,1024]{1,0:T(8,128)(2,1)} %get-tuple-element.237.refs_0_), channel_id=1, source_target_pairs={{0,2},{1,3},{2,0},{3,1},{4,6},{5,7},{6,4},{7,5}} | collective-permute-start | bytes 6291464 | tf_op jit(solution)/shard_map/ppermute | solution.py:601
  1770.3 89.1 %collective-permute-start.47 = (bf16[1024,1024]{1,0:T(8,128)(2,1)}, bf16[1024,1024]{1,0:T(8,128)(2,1)}, u32[]{:S(2)}, u32[]{:S(2)}) collective-permute-start(bf16[1024,1024]{1,0:T(8,128)(2,1)} %get-tuple-element.239.refs_2_), channel_id=1, source_target_pairs={{0,2},{1,3},{2,0},{3,1},{4,6},{5,7},{6,4},{7,5}} | collective-permute-start | bytes 6291464 | tf_op jit(solution)/shard_map/ppermute | solution.py:601
  1770.8 92.3 %collective-permute-start.49 = (bf16[1024,1024]{1,0:T(8,128)(2,1)}, bf16[1024,1024]{1,0:T(8,128)(2,1)}, u32[]{:S(2)}, u32[]{:S(2)}) collective-permute-start(bf16[1024,1024]{1,0:T(8,128)(2,1)} %get-tuple-element.237.refs_0_), channel_id=1, source_target_pairs={{0,4},{1,5},{2,6},{3,7},{4,0},{5,1},{6,2},{7,3}} | collective-permute-start | bytes 6291464 | tf_op jit(solution)/shard_map/ppermute | solution.py:601
  1771.0 96.9 %collective-permute-start.21 = (bf16[512,2048]{1,0:T(8,128)(2,1)}, bf16[512,2048]{1,0:T(8,128)(2,1)S(1)}, u32[]{:S(2)}, u32[]{:S(2)}) collective-permute-start(bf16[512,2048]{1,0:T(8,128)(2,1)} %collective-permute-done.20.refs_4_), channel_id=1, source_target_pairs={{0,1},{1,0},{2,3},{3,2},{4,5},{5,4},{6,7},{7,6}} | collective-permute-start | bytes 6291464 | tf_op jit(solution)/shard_map/ppermute | solution.py:601
  (74 other events, 3354.9 us)
Sparse Core Ops, SparseCore 0:
  16.4 19.2 all-gather.12
  37.8 18.2 all-gather.14
  187.3 14.8 reduce-scatter.4
  339.5 14.8 reduce-scatter.8
  356.0 156.2 all-gather.28
  514.3 17.0 all-gather.16
  533.5 18.2 all-gather.18
  684.2 14.8 reduce-scatter.6
  700.9 156.2 all-gather.30
  859.2 17.0 all-gather.20
  877.8 18.2 all-gather.22
  1029.0 14.8 reduce-scatter.10
  1128.9 85.3 all-gather.24
  1231.5 165.0 all-gather.26

commit v7 on v6

--- a/solution.py
+++ b/solution.py
@@ -210,7 +210,7 @@
     a_ref[...] = (state * inv * g_ref[...]).astype(BF16)
 
 
-def teacher_norm(hidden, delta, gains, layer, which=0, size=2**18):
+def teacher_norm(hidden, delta, gains, layer, which=0, size=2**19):
     rows, width = hidden.shape[-2:]
     block = size // width
     spec = pl.BlockSpec((block, width), lambda i: (i, 0))
@@ -241,19 +241,18 @@
         u_ref[part, :] = gelu(pre).astype(BF16)
 
 
-def pre_of(me, states, gain, weights, parity, cols, block=512, sub=256):
+def pre_of(me, states, gain, weights, cols, block=512, sub=256):
     n_seq, seq_len, width = states.shape
-    half = n_seq // 2
-    rows = half * seq_len
+    rows = n_seq * seq_len
     steps = seq_len // block
     out = lambda w: pl.BlockSpec((block, w), lambda i, j, me: (i * steps + j, 0))
     return pl.pallas_call(
         functools.partial(pre_kernel, sub),
         grid_spec=pltpu.PrefetchScalarGridSpec(
             num_scalar_prefetch=1,
-            grid=(half, steps),
+            grid=(n_seq, steps),
             in_specs=[
-                pl.BlockSpec((None, block, width), lambda i, j, me: (2 * i + parity, j, 0)),
+                pl.BlockSpec((None, block, width), lambda i, j, me: (i, j, 0)),
                 fixed(1, width),
                 pl.BlockSpec((None, width, cols), lambda i, j, me: (0, 0, me[0])),
             ],
@@ -439,7 +438,8 @@
     steps = seq_len // block
     spec = lambda w: pl.BlockSpec((block, w), lambda i, j: (i * steps + j, 0))
     whole = fixed(cols, width, pipeline_mode=ONCE)
-    in_specs = [spec(width), pl.BlockSpec((None, block, width), lambda i, j: (2 * i + parity, j, 0)), spec(cols)]
+    natural = pl.BlockSpec((block, cols), lambda i, j: ((2 * i + parity) * steps + j, 0))
+    in_specs = [spec(width), pl.BlockSpec((None, block, width), lambda i, j: (2 * i + parity, j, 0)), natural]
     args = [targets, states, ups]
     if total is not None:
         in_specs.append(whole)
@@ -567,11 +567,12 @@
     rows = half * seq_len
     steps = seq_len // block
     spec = lambda w: pl.BlockSpec((block, w), lambda i, j, me: (i * steps + j, 0))
+    natural = lambda w: pl.BlockSpec((block, w), lambda i, j, me: ((2 * i + parity) * steps + j, 0))
     whole = lambda h: fixed(h, cols, pipeline_mode=ONCE)
     in_specs = [
         spec(width),
-        spec(cols),
-        spec(width),
+        natural(cols),
+        natural(width),
         pl.BlockSpec((None, block, width), lambda i, j, me: (2 * i + parity, j, 0)),
         pl.BlockSpec((None, width, cols), lambda i, j, me: (0, 0, me[0]), pipeline_mode=ONCE),
         pl.BlockSpec((None, cols, width), lambda i, j, me: (0, me[0], 0), pipeline_mode=ONCE),
@@ -625,8 +626,8 @@
     return {**have, **diag, **near, **far}
 
 
-def collect(out, have, me, chips, dep, shape, by_cols):
-    keys = [(bits | core, half) for bits in chips for half in range(2) for core in range(2)]
+def collect(out, have, me, chips, dep, shape, by_cols, cores=(0, 1)):
+    keys = [(bits | core, half) for bits in chips for half in range(2) for core in cores]
     pieces = after([have[key] for key in keys], dep)
     return place(out, pieces, [me ^ key[0] for key in keys], [key[1] for key in keys], shape, by_cols)
 
@@ -641,6 +642,7 @@
         _, seq_len, s_width = student_in.shape
         s_hidden = student_up.shape[2]
         part = s_hidden // size
+        t_part = t_width // size
         total = size * seq_len * s_width
         grad_scale = 2.0 / total
 
@@ -685,7 +687,11 @@
                 if layer < last:
                     ready, acts[0] = normed(0, delta_0, layer + 1)
                 else:
-                    ready, targets_0, feat_0 = finish(0, delta_0)
+                    feats = (hidden[0].astype(F32) + delta_0[0].astype(F32)).astype(BF16)
+                    pieces = [lax.dynamic_slice(feats, (0, (me ^ bits) * t_part), (rows, t_part)) for bits in range(size)]
+                    feat_0 = [flip(piece, bits, size) if bits else piece for bits, piece in enumerate(pieces)]
+                    ready = dot(feats, student_proj[0]).astype(BF16)
+                    targets_0 = lax.all_gather(ready, AXES, axis=0, tiled=True)
                 partial = teach(after(acts[1], ready), layer, rows=rows, where=side)
                 delta_1 = (partial, moved)
             if layer < last:
@@ -695,17 +701,17 @@
         target_1, targets_1, feat_1 = finish(1, delta_1)
 
         all_in, all_out = after((all_in, all_out), target_1)
-        acts, pre, ups = zip(*[pre_of(me, all_in, student_gain, student_up, c, part) for c in range(2)])
+        acts, pre, ups = pre_of(me, all_in, student_gain, student_up, part)
         proj_sum, square_0 = proj_part(me, feat_0, after(targets_0, ups), all_out, 0, grad_scale, None, False)
-        d_out_0, down_sum = down_part_of(ups[0], after(targets_0, (proj_sum, ups[1])), all_out, 0, grad_scale, None, False)
+        d_out_0, down_sum = down_part_of(ups, after(targets_0, (proj_sum, ups)), all_out, 0, grad_scale, None, False)
         targets_1 = after(targets_1, down_sum)
         *proj_halves, square_1 = proj_part(me, feat_1, targets_1, all_out, 1, grad_scale, proj_sum, True)
         proj_have = relay(send(proj_halves, size), size)
         loss = jnp.sum(square_0 + square_1) / total
-        d_out_1, *down_halves = down_part_of(ups[1], after(targets_1, proj_halves), all_out, 1, grad_scale, down_sum, True)
+        d_out_1, *down_halves = down_part_of(ups, after(targets_1, proj_halves), all_out, 1, grad_scale, down_sum, True)
         down_have = relay(send(down_halves, size), size)
-        up_sum, gain_0 = rest_part(me, after(d_out_0, down_halves), pre[0], acts[0], all_in, student_up, student_down, 0, None, False)
-        *up_halves, gain_1 = rest_part(me, d_out_1, pre[1], acts[1], all_in, student_up, student_down, 1, up_sum, True)
+        up_sum, gain_0 = rest_part(me, after(d_out_0, down_halves), pre, acts, all_in, student_up, student_down, 0, None, False)
+        *up_halves, gain_1 = rest_part(me, d_out_1, pre, acts, all_in, student_up, student_down, 1, up_sum, True)
         up_have = send(up_halves, size)
         grad_gain = jnp.sum(gain_0 + gain_1, axis=0)
         for bits in (CORE, X, Y):
@@ -718,7 +724,8 @@
         shape = (s_width, s_hidden)
         grad_up = collect(None, up_have, me, (0,), grad_down, shape, True)
         grad_up = collect(grad_up, up_have, me, (X, Y), (), shape, True)
-        grad_up = collect(grad_up, up_have, me, (X | Y,), (), shape, True)
+        for core in range(2):
+            grad_up = collect(grad_up, up_have, me, (X | Y,), (), shape, True, (core,))
         return (loss, grad_up[None], grad_down[None], grad_gain[None], grad_proj[None])
 
     return jax.shard_map(

time: 2060 us -> 2090 us (1.015)
  Pallas kernels: 1540 us -> 1500 us
  waiting for transfers between devices: 407 us -> 436 us
    ppermute x61, waiting for transfers between devices: 286 us -> 323 us  [flip(): return lax.ppermute(value, AXES, [(i, i ^ bits) for i in range(size)])]
    pallas_call x2 -> x1, Pallas kernels: 61.4 us -> 55.2 us  [pre_of(): pl.pallas_call(functools.partial(pre_kernel, sub), grid_spec=pltpu.Prefet...]
    pallas_call x6 -> x7, Pallas kernels: 89.1 us -> 91.1 us  [place(): pl.pallas_call(functools.partial(place_kernel, count, ahead), grid_spec=p...]
  transfers between devices with their start and end apart: 75 -> 75, of which waited for: 23 -> 24; matrix products, arithmetic and copies ran while one was open for 0% -> 1% of each run, Pallas kernels for 63% -> 62%
where the time goes in v7:
time: 2090 us; the launch traced here: 2080 us
  Pallas kernels  1500 us (72%)
  waiting for transfers between devices  436 us (21%)
  starting transfers between devices  87.5 us (4%)
    pallas_call x9, Pallas kernels, mlp(): pl.pallas_call(functools.partial(mlp_kernel, layer, steps, wide, state is...  1020 us
    ppermute x61, waiting for transfers between devices, flip(): return lax.ppermute(value, AXES, [(i, i ^ bits) for i in range(size)])  323 us
    pallas_call x2, Pallas kernels, rest_part(): pl.pallas_call(functools.partial(rest_kernel, total is None, last, sub),...  148 us
    pallas_call x7, Pallas kernels, place(): pl.pallas_call(functools.partial(place_kernel, count, ahead), grid_spec=p...  91.1 us
    ppermute x61, starting transfers between devices, flip(): return lax.ppermute(value, AXES, [(i, i ^ bits) for i in range(size)])  86.9 us
    all_gather x1, waiting for transfers between devices, step(): lax.all_gather(after(own, (acts[0], own_act)), AXES, axis=0, tiled=False)  77.3 us
    pallas_call x2, Pallas kernels, down_part_of(): pl.pallas_call(functools.partial(down_kernel, scale, total is None, last,...  72.9 us
    pallas_call x1, Pallas kernels, pre_of(): pl.pallas_call(functools.partial(pre_kernel, sub), grid_spec=pltpu.Prefet...  55.2 us
  transfers between devices with their start and end apart: 75, of which 24 were waited for; matrix products, arithmetic and copies ran while one was open for 1% of the time, Pallas kernels for 62%

profile of v7, /device:TPU:1, one launch (start us, length us, event | category | flops | bytes accessed | tf_op | source)
XLA Modules:
  0.0 2076.9 jit_solution(3652782388512666304)
XLA Ops:
  34.1 151.5 %mlp.9 = bf16[1024,4096]{1,0:T(8,128)(2,1)} custom-call(s32[1]{0:T(128)} %constant.10.clone.1.where_ref, bf16[1024,4096]{1,0:T(8,128)(2,1)} %all-gather.13.cloned.1.call-done.refs_0_, bf16[3,4096,8192]{2,1,0:T(8,128)(2,1)} %refs_1_.17, bf16[3,8192,4096]{2,1,0:T(8,128)(2,1)} %refs_2_.18), custom_call_target="tpu_custom_call" | custom-call | flops 137438953472 | bytes 150994944 | tf_op jit(solution)/shard_map/mlp/pallas_call | solution.py:175
  185.7 152.0 %mlp.10 = bf16[1024,4096]{1,0:T(8,128)(2,1)} custom-call(s32[1]{0:T(128)} %constant.10.clone.1.where_ref, bf16[1024,4096]{1,0:T(8,128)(2,1)} %all-gather.15.cloned.1.call-done.refs_0_, bf16[3,4096,8192]{2,1,0:T(8,128)(2,1)} %refs_1_.17, bf16[3,8192,4096]{2,1,0:T(8,128)(2,1)} %refs_2_.18), custom_call_target="tpu_custom_call" | custom-call | flops 137438953472 | bytes 150994944 | tf_op jit(solution)/shard_map/mlp/pallas_call | solution.py:175
  352.0 81.3 %mlp.12 = bf16[1024,2048]{1,0:T(8,128)(2,1)} custom-call(s32[1]{0:T(128)} %constant.10.clone.1.where_ref, bf16[1024,2048]{1,0:T(8,128)(2,1)} %norm.5.refs_0_, bf16[1,2048,8192]{2,1,0:T(8,128)(2,1)} %up_ref.3, bf16[1,8192,2048]{2,1,0:T(8,128)(2,1)} %down_ref.3, bf16[1024,2048]{1,0:T(8,128)(2,1)} %bitcast.33), custom_call_target="tpu_custom_call" | custom-call | flops 68719476736 | bytes 75497472 | tf_op jit(solution)/shard_map/mlp/pallas_call | solution.py:175
  433.4 77.3 %all-gather.29.cloned.1.call-done = bf16[8192,2048]{1,0:T(8,128)(2,1)} async-done(((bf16[1024,2048]{1,0:T(8,128)(2,1)}), bf16[8192,2048]{1,0:T(8,128)(2,1)}) %all-gather.29.cloned.1.call-update) | async-done | bytes 33554448 | tf_op jit(solution)/shard_map/all_gather | solution.py:671
  529.7 152.6 %mlp.11 = bf16[1024,4096]{1,0:T(8,128)(2,1)} custom-call(s32[1]{0:T(128)} %constant.10.clone.1.where_ref, bf16[1024,4096]{1,0:T(8,128)(2,1)} %all-gather.17.cloned.1.call-done.refs_0_, bf16[3,4096,8192]{2,1,0:T(8,128)(2,1)} %refs_1_.17, bf16[3,8192,4096]{2,1,0:T(8,128)(2,1)} %refs_2_.18), custom_call_target="tpu_custom_call" | custom-call | flops 137438953472 | bytes 150994944 | tf_op jit(solution)/shard_map/mlp/pallas_call | solution.py:175
  683.2 81.2 %mlp.13 = bf16[512,4096]{1,0:T(8,128)(2,1)} custom-call(s32[1]{0:T(128)} %bitcast.1.where_ref, bf16[1024,4096]{1,0:T(8,128)(2,1)} %all-gather.19.cloned.1.call-done.refs_0_, bf16[3,4096,8192]{2,1,0:T(8,128)(2,1)} %refs_1_.17, bf16[3,8192,4096]{2,1,0:T(8,128)(2,1)} %refs_2_.18), custom_call_target="tpu_custom_call" | custom-call | flops 68719476736 | bytes 142606336 | tf_op jit(solution)/shard_map/mlp/pallas_call | solution.py:175
  773.0 81.6 %mlp.15.refs_0_ = bf16[512,4096]{1,0:T(8,128)(2,1)} custom-call(s32[1]{0:T(128)} %bitcast.4.where_ref, bf16[1024,4096]{1,0:T(8,128)(2,1)} %all-gather.19.cloned.1.call-done.refs_0_, bf16[3,4096,8192]{2,1,0:T(8,128)(2,1)} %refs_1_.17, bf16[3,8192,4096]{2,1,0:T(8,128)(2,1)} %refs_2_.18), custom_call_target="tpu_custom_call" | custom-call | flops 68719476736 | bytes 142606336 | tf_op jit(solution)/shard_map/mlp/pallas_call | solution.py:175
  874.6 152.6 %mlp.14 = bf16[1024,4096]{1,0:T(8,128)(2,1)} custom-call(s32[1]{0:T(128)} %constant.10.clone.1.where_ref, bf16[1024,4096]{1,0:T(8,128)(2,1)} %all-gather.21.cloned.1.call-done.refs_0_, bf16[3,4096,8192]{2,1,0:T(8,128)(2,1)} %refs_1_.17, bf16[3,8192,4096]{2,1,0:T(8,128)(2,1)} %refs_2_.18), custom_call_target="tpu_custom_call" | custom-call | flops 137438953472 | bytes 150994944 | tf_op jit(solution)/shard_map/mlp/pallas_call | solution.py:175
  1027.3 81.1 %mlp.16 = bf16[512,4096]{1,0:T(8,128)(2,1)} custom-call(s32[1]{0:T(128)} %bitcast.1.where_ref, bf16[1024,4096]{1,0:T(8,128)(2,1)} %all-gather.23.cloned.1.call-done.refs_0_, bf16[3,4096,8192]{2,1,0:T(8,128)(2,1)} %refs_1_.17, bf16[3,8192,4096]{2,1,0:T(8,128)(2,1)} %refs_2_.18), custom_call_target="tpu_custom_call" | custom-call | flops 68719476736 | bytes 142606336 | tf_op jit(solution)/shard_map/mlp/pallas_call | solution.py:175
  1129.6 81.1 %mlp.17.refs_0_ = bf16[512,4096]{1,0:T(8,128)(2,1)} custom-call(s32[1]{0:T(128)} %bitcast.4.where_ref, bf16[1024,4096]{1,0:T(8,128)(2,1)} %all-gather.23.cloned.1.call-done.refs_0_, bf16[3,4096,8192]{2,1,0:T(8,128)(2,1)} %refs_1_.17, bf16[3,8192,4096]{2,1,0:T(8,128)(2,1)} %refs_2_.18), custom_call_target="tpu_custom_call" | custom-call | flops 68719476736 | bytes 142606336 | tf_op jit(solution)/shard_map/mlp/pallas_call | solution.py:175
  1263.1 55.2 %pre.1 = (bf16[8192,2048]{1,0:T(8,128)(2,1)}, f32[8192,1024]{1,0:T(8,128)}, bf16[8192,1024]{1,0:T(8,128)(2,1)}) custom-call(s32[1]{0:T(128)} %bitcast.me_ref, bf16[8,1024,2048]{2,1,0:T(8,128)(2,1)} %bitcast.28, f32[1,2048]{1,0:T(1,128)} %g_ref.3, bf16[1,2048,8192]{2,1,0:T(8,128)(2,1)} %up_ref.3), custom_call_target="tpu_custom_call" | custom-call | flops 34359738368 | bytes 117440512 | tf_op jit(solution)/shard_map/pre/pallas_call | solution.py:249
  1322.2 22.5 %proj.2 = (f32[512,2048]{1,0:T(8,128)}, f32[8,2048]{1,0:T(8,128)}) custom-call(s32[1]{0:T(128)} %bitcast.me_ref, bf16[512,512]{1,0:T(8,128)(2,1)} %get-tuple-element.226.refs_0_, bf16[512,512]{1,0:T(8,128)(2,1)} %collective-permute-done.1.refs_1_, bf16[512,512]{1,0:T(8,128)(2,1)} %collective-permute-done.2.refs_2_, ...), custom_call_target="tpu_custom_call" | custom-call | flops 8589934592 | bytes 37748736 | tf_op jit(solution)/shard_map/proj/pallas_call | solution.py:381
  1366.6 35.8 %down.2 = (bf16[4096,2048]{1,0:T(8,128)(2,1)}, f32[1024,2048]{1,0:T(8,128)}) custom-call(bf16[4096,2048]{1,0:T(8,128)(2,1)} %all-gather.25.cloned.1.call-done.refs_8_.z_ref, bf16[8,1024,2048]{2,1,0:T(8,128)(2,1)} %bitcast.24, bf16[8192,1024]{1,0:T(8,128)(2,1)} %get-tuple-element.133.u_ref), custom_call_target="tpu_custom_call" | custom-call | flops 17179869184 | bytes 58720256 | tf_op jit(solution)/shard_map/down/pallas_call | solution.py:448
  1404.7 22.8 %proj.3 = (bf16[256,2048]{1,0:T(8,128)(2,1)}, bf16[256,2048]{1,0:T(8,128)(2,1)}, f32[8,2048]{1,0:T(8,128)}) custom-call(s32[1]{0:T(128)} %bitcast.me_ref, bf16[512,512]{1,0:T(8,128)(2,1)} %get-tuple-element.137.refs_0_, bf16[512,512]{1,0:T(8,128)(2,1)} %collective-permute-done.9.refs_1_, bf16[512,512]{1,0:T(8,128)(2,1)} %collective-permute-done.10.refs_2_, ...), custom_call_target="tpu_custom_call" | custom-call | flops 8589934592 | bytes 37748736 | tf_op jit(solution)/shard_map/proj/pallas_call | solution.py:381
  1427.5 37.1 %down.3 = (bf16[4096,2048]{1,0:T(8,128)(2,1)}, bf16[512,2048]{1,0:T(8,128)(2,1)}, bf16[512,2048]{1,0:T(8,128)(2,1)}) custom-call(bf16[4096,2048]{1,0:T(8,128)(2,1)} %all-gather.27.cloned.1.call-done.refs_8_.z_ref, bf16[8,1024,2048]{2,1,0:T(8,128)(2,1)} %bitcast.26, bf16[8192,1024]{1,0:T(8,128)(2,1)} %get-tuple-element.133.u_ref, ...), custom_call_target="tpu_custom_call" | custom-call | flops 17179869184 | bytes 58720256 | tf_op jit(solution)/shard_map/down/pallas_call | solution.py:448
  1464.6 73.7 %rest.2 = (f32[2048,1024]{1,0:T(8,128)}, f32[8,2048]{1,0:T(8,128)}) custom-call(s32[1]{0:T(128)} %bitcast.me_ref, bf16[4096,2048]{1,0:T(8,128)(2,1)} %get-tuple-element.159.d_ref, f32[8192,1024]{1,0:T(8,128)} %get-tuple-element.154.p_ref, bf16[8192,2048]{1,0:T(8,128)(2,1)} %get-tuple-element.155.a_ref, bf16[8,1024,2048]{2,1,0:T(8,128)(2,1)} %bitcast.29, ...), custom_call_target="tpu_custom_call" | custom-call | flops 51539607552 | bytes 67108864 | tf_op jit(solution)/shard_map/rest/pallas_call | solution.py:585
  1538.3 74.7 %rest.3 = (bf16[1024,1024]{1,0:T(8,128)(2,1)}, bf16[1024,1024]{1,0:T(8,128)(2,1)}, f32[8,2048]{1,0:T(8,128)}) custom-call(s32[1]{0:T(128)} %bitcast.me_ref, bf16[4096,2048]{1,0:T(8,128)(2,1)} %get-tuple-element.153.d_ref, f32[8192,1024]{1,0:T(8,128)} %get-tuple-element.154.p_ref, bf16[8192,2048]{1,0:T(8,128)(2,1)} %get-tuple-element.155.a_ref, ...), custom_call_target="tpu_custom_call" | custom-call | flops 51539607552 | bytes 67108864 | tf_op jit(solution)/shard_map/rest/pallas_call | solution.py:585
  1669.7 41.7 %collective-permute-done.34.refs_8_ = bf16[256,2048]{1,0:T(8,128)(2,1)S(1)} collective-permute-done((bf16[256,2048]{1,0:T(8,128)(2,1)}, bf16[256,2048]{1,0:T(8,128)(2,1)S(1)}, u32[]{:S(2)}, u32[]{:S(2)}) %collective-permute-start.34) | collective-permute-done | bytes 1048608 | tf_op jit(solution)/shard_map/ppermute | solution.py:602
  1747.7 31.0 %collective-permute-done.22.refs_6_ = bf16[512,2048]{1,0:T(8,128)(2,1)} collective-permute-done((bf16[512,2048]{1,0:T(8,128)(2,1)}, bf16[512,2048]{1,0:T(8,128)(2,1)}, u32[]{:S(2)}, u32[]{:S(2)}) %collective-permute-start.22) | collective-permute-done | bytes 2097184 | tf_op jit(solution)/shard_map/ppermute | solution.py:602
  1781.6 42.0 %collective-permute-done.16.refs_0_ = bf16[1024,1024]{1,0:T(8,128)(2,1)} collective-permute-done((bf16[1024,1024]{1,0:T(8,128)(2,1)}, bf16[1024,1024]{1,0:T(8,128)(2,1)}, u32[]{:S(2)}, u32[]{:S(2)}) %collective-permute-start.16) | collective-permute-done | bytes 2097184 | tf_op jit(solution)/shard_map/ppermute | solution.py:602
  1834.4 34.1 %collective-permute-done.47.refs_2_ = bf16[1024,1024]{1,0:T(8,128)(2,1)} collective-permute-done((bf16[1024,1024]{1,0:T(8,128)(2,1)}, bf16[1024,1024]{1,0:T(8,128)(2,1)}, u32[]{:S(2)}, u32[]{:S(2)}) %collective-permute-start.47) | collective-permute-done | bytes 2097184 | tf_op jit(solution)/shard_map/ppermute | solution.py:602
  1882.0 27.1 %collective-permute-done.54.refs_0_ = bf16[512,2048]{1,0:T(8,128)(2,1)} collective-permute-done((bf16[512,2048]{1,0:T(8,128)(2,1)S(1)}, bf16[512,2048]{1,0:T(8,128)(2,1)}, u32[]{:S(2)}, u32[]{:S(2)}) %collective-permute-start.54) | collective-permute-done | bytes 2097184 | tf_op jit(solution)/shard_map/ppermute | solution.py:602
  1939.9 25.8 %place.8.refs_4_ = f32[8192,2048]{1,0:T(8,128)} custom-call(s32[12]{0:T(128)} %stack.35.owner_ref, s32[12]{0:T(128)} %constant.46.clone.half_ref, bf16[512,2048]{1,0:T(8,128)(2,1)} %get-tuple-element.181.refs_0_, bf16[512,2048]{1,0:T(8,128)(2,1)} %copy-done.3, bf16[512,2048]{1,0:T(8,128)(2,1)} %get-tuple-element.183.refs_2_, bf16[512,2048]{1,0:T(8,128)(2,1)} %copy-done.4, ...), custom_call_target="tpu_custom_call" | custom-call | flops 12582912 | bytes 75497472 | tf_op jit(solution)/shard_map/place/pallas_call | solution.py:504
  1968.4 44.7 %collective-permute-done.42.refs_0_ = bf16[1024,1024]{1,0:T(8,128)(2,1)} collective-permute-done((bf16[1024,1024]{1,0:T(8,128)(2,1)}, bf16[1024,1024]{1,0:T(8,128)(2,1)}, u32[]{:S(2)}, u32[]{:S(2)}) %collective-permute-start.42) | collective-permute-done | bytes 2097184 | tf_op jit(solution)/shard_map/ppermute | solution.py:602
  (232 shorter events, 399.7 us)
Async XLA Ops:
  14.6 171.0 %all-gather.15.cloned.1.call-start = ((), (), s32[]{:S(2)}) async-start(), calls=%async_computation.6 | async-start | bytes 12582912 | tf_op jit(solution)/shard_map/all_gather | solution.py:662
  20.5 322.8 %reduce-scatter.5.cloned.1.call-start = ((), (), s32[]{:S(2)}) async-start(), calls=%async_computation.5 | async-start | bytes 12582912 | tf_op jit(solution)/shard_map/reduce_scatter | solution.py:675
  185.6 247.8 %reduce-scatter.9.cloned.1.call-start = ((), (), s32[]{:S(2)}) async-start(), calls=%async_computation.9 | async-start | bytes 12582912 | tf_op jit(solution)/shard_map/reduce_scatter | solution.py:678
  337.7 173.0 %all-gather.29.cloned.1.call-start = ((), (), s32[]{:S(2)}) async-start(), calls=%async_computation.16 | async-start | bytes 37748736 | tf_op jit(solution)/shard_map/all_gather | solution.py:671
  343.2 186.5 %all-gather.17.cloned.1.call-start = ((), (), s32[]{:S(2)}) async-start(), calls=%async_computation.7 | async-start | bytes 12582912 | tf_op jit(solution)/shard_map/all_gather | solution.py:662
  352.0 331.2 %all-gather.19.cloned.1.call-start = ((), (), s32[]{:S(2)}) async-start(), calls=%async_computation.10 | async-start | bytes 12582912 | tf_op jit(solution)/shard_map/all_gather | solution.py:662
  518.4 246.0 %reduce-scatter.7.cloned.1.call-start = ((), (), s32[]{:S(2)}) async-start(), calls=%async_computation.8 | async-start | bytes 12582912 | tf_op jit(solution)/shard_map/reduce_scatter | solution.py:675
  682.4 173.2 %all-gather.31.cloned.1.call-start = ((), (), s32[]{:S(2)}) async-start(), calls=%async_computation.17 | async-start | bytes 37748736 | tf_op jit(solution)/shard_map/all_gather | solution.py:673
  683.1 191.5 %all-gather.21.cloned.1.call-start = ((), (), s32[]{:S(2)}) async-start(), calls=%async_computation.11 | async-start | bytes 12582912 | tf_op jit(solution)/shard_map/all_gather | solution.py:662
  772.7 254.6 %all-gather.23.cloned.1.call-start = ((), (), s32[]{:S(2)}) async-start(), calls=%async_computation.13 | async-start | bytes 12582912 | tf_op jit(solution)/shard_map/all_gather | solution.py:662
  772.7 81.9 %collective-permute-start = (bf16[512,4096]{1,0:T(8,128)(2,1)}, bf16[512,4096]{1,0:T(8,128)(2,1)}, u32[]{:S(2)}, u32[]{:S(2)}) collective-permute-start(bf16[512,4096]{1,0:T(8,128)(2,1)} %mlp.13), channel_id=1, source_target_pairs={{0,1},{1,0},{2,3},{3,2},{4,5},{5,4},{6,7},{7,6}} | collective-permute-start | bytes 12582920 | tf_op jit(solution)/shard_map/ppermute | solution.py:602
  865.5 243.0 %reduce-scatter.11.cloned.1.call-start = ((), (), s32[]{:S(2)}) async-start(), calls=%async_computation.12 | async-start | bytes 12582912 | tf_op jit(solution)/shard_map/reduce_scatter | solution.py:675
  1027.2 291.0 %all-gather.25.cloned.1.call-start = ((), (), s32[]{:S(2)}) async-start(), calls=%async_computation.14 | async-start | bytes 18874368 | tf_op jit(solution)/shard_map/all_gather | solution.py:694
  1129.3 273.1 %all-gather.27.cloned.1.call-start = ((), (), s32[]{:S(2)}) async-start(), calls=%async_computation.15 | async-start | bytes 18874368 | tf_op jit(solution)/shard_map/all_gather | solution.py:656
  1129.3 81.4 %collective-permute-start.8 = (bf16[512,4096]{1,0:T(8,128)(2,1)}, bf16[512,4096]{1,0:T(8,128)(2,1)}, u32[]{:S(2)}, u32[]{:S(2)}) collective-permute-start(bf16[512,4096]{1,0:T(8,128)(2,1)} %mlp.16), channel_id=1, source_target_pairs={{0,1},{1,0},{2,3},{3,2},{4,5},{5,4},{6,7},{7,6}} | collective-permute-start | bytes 12582920 | tf_op jit(solution)/shard_map/ppermute | solution.py:602
  1318.7 83.7 %collective-permute-start.12 = (bf16[512,512]{1,0:T(8,128)(2,1)}, bf16[512,512]{1,0:T(8,128)(2,1)}, u32[]{:S(2)}, u32[]{:S(2)}) collective-permute-start(bf16[512,512]{1,0:T(8,128)(2,1)} %get-tuple-element.141), channel_id=1, source_target_pairs={{0,4},{1,5},{2,6},{3,7},{4,0},{5,1},{6,2},{7,3}} | collective-permute-start | bytes 1572872 | tf_op jit(solution)/shard_map/ppermute | solution.py:602
  1319.4 83.0 %collective-permute-start.13 = (bf16[512,512]{1,0:T(8,128)(2,1)}, bf16[512,512]{1,0:T(8,128)(2,1)}, u32[]{:S(2)}, u32[]{:S(2)}) collective-permute-start(bf16[512,512]{1,0:T(8,128)(2,1)} %get-tuple-element.142), channel_id=1, source_target_pairs={{0,5},{1,4},{2,7},{3,6},{4,1},{5,0},{6,3},{7,2}} | collective-permute-start | bytes 1572872 | tf_op jit(solution)/shard_map/ppermute | solution.py:602
  1621.1 93.9 %collective-permute-start.20 = (bf16[512,2048]{1,0:T(8,128)(2,1)}, bf16[512,2048]{1,0:T(8,128)(2,1)S(1)}, u32[]{:S(2)}, u32[]{:S(2)}) collective-permute-start(bf16[512,2048]{1,0:T(8,128)(2,1)} %get-tuple-element.181.refs_0_), channel_id=1, source_target_pairs={{0,2},{1,3},{2,0},{3,1},{4,6},{5,7},{6,4},{7,5}} | collective-permute-start | bytes 6291464 | tf_op jit(solution)/shard_map/ppermute | solution.py:602
  1622.5 92.5 %collective-permute-start.26 = (bf16[512,2048]{1,0:T(8,128)(2,1)}, bf16[512,2048]{1,0:T(8,128)(2,1)S(1)}, u32[]{:S(2)}, u32[]{:S(2)}) collective-permute-start(bf16[512,2048]{1,0:T(8,128)(2,1)} %get-tuple-element.183.refs_2_), channel_id=1, source_target_pairs={{0,4},{1,5},{2,6},{3,7},{4,0},{5,1},{6,2},{7,3}} | collective-permute-start | bytes 6291464 | tf_op jit(solution)/shard_map/ppermute | solution.py:602
  1779.5 89.0 %collective-permute-start.47 = (bf16[1024,1024]{1,0:T(8,128)(2,1)}, bf16[1024,1024]{1,0:T(8,128)(2,1)}, u32[]{:S(2)}, u32[]{:S(2)}) collective-permute-start(bf16[1024,1024]{1,0:T(8,128)(2,1)} %get-tuple-element.215.refs_2_), channel_id=1, source_target_pairs={{0,2},{1,3},{2,0},{3,1},{4,6},{5,7},{6,4},{7,5}} | collective-permute-start | bytes 6291464 | tf_op jit(solution)/shard_map/ppermute | solution.py:602
  1780.1 95.4 %collective-permute-start.49 = (bf16[1024,1024]{1,0:T(8,128)(2,1)}, bf16[1024,1024]{1,0:T(8,128)(2,1)}, u32[]{:S(2)}, u32[]{:S(2)}) collective-permute-start(bf16[1024,1024]{1,0:T(8,128)(2,1)} %get-tuple-element.213.refs_0_), channel_id=1, source_target_pairs={{0,4},{1,5},{2,6},{3,7},{4,0},{5,1},{6,2},{7,3}} | collective-permute-start | bytes 6291464 | tf_op jit(solution)/shard_map/ppermute | solution.py:602
  1780.1 128.9 %collective-permute-start.54 = (bf16[512,2048]{1,0:T(8,128)(2,1)S(1)}, bf16[512,2048]{1,0:T(8,128)(2,1)}, u32[]{:S(2)}, u32[]{:S(2)}) collective-permute-start(bf16[512,2048]{1,0:T(8,128)(2,1)S(1)} %collective-permute-done.20.refs_4_), channel_id=1, source_target_pairs={{0,4},{1,5},{2,6},{3,7},{4,0},{5,1},{6,2},{7,3}} | collective-permute-start | bytes 6291464 | tf_op jit(solution)/shard_map/ppermute | solution.py:602
  1823.6 93.3 %collective-permute-start.56 = (bf16[512,2048]{1,0:T(8,128)(2,1)S(1)}, bf16[512,2048]{1,0:T(8,128)(2,1)}, u32[]{:S(2)}, u32[]{:S(2)}) collective-permute-start(bf16[512,2048]{1,0:T(8,128)(2,1)S(1)} %collective-permute-done.26.refs_10_), channel_id=1, source_target_pairs={{0,2},{1,3},{2,0},{3,1},{4,6},{5,7},{6,4},{7,5}} | collective-permute-start | bytes 6291464 | tf_op jit(solution)/shard_map/ppermute | solution.py:602
  1823.6 93.5 %collective-permute-start.21 = (bf16[512,2048]{1,0:T(8,128)(2,1)S(1)}, bf16[512,2048]{1,0:T(8,128)(2,1)S(1)}, u32[]{:S(2)}, u32[]{:S(2)}) collective-permute-start(bf16[512,2048]{1,0:T(8,128)(2,1)S(1)} %collective-permute-done.20.refs_4_), channel_id=1, source_target_pairs={{0,1},{1,0},{2,3},{3,2},{4,5},{5,4},{6,7},{7,6}} | collective-permute-start | bytes 6291464 | tf_op jit(solution)/shard_map/ppermute | solution.py:602
  (73 other events, 4413.6 us)
Sparse Core Ops, SparseCore 0:
  14.8 19.2 all-gather.12
  36.1 18.2 all-gather.14
  185.7 14.8 reduce-scatter.4
  337.8 14.8 reduce-scatter.8
  354.4 156.3 all-gather.28
  512.7 17.0 all-gather.16
  531.8 18.2 all-gather.18
  682.5 14.8 reduce-scatter.6
  699.2 156.2 all-gather.30
  857.5 17.0 all-gather.20
  876.1 18.2 all-gather.22
  1027.4 14.8 reduce-scatter.10
  1129.4 85.3 all-gather.24
  1231.8 167.6 all-gather.26
